TPU v7x, 256 devices: a whole 4x4x8 slice. The times are simulated.
256 devices in a mesh: row: 16 (over x, y), col: 16 (over z, core).
Axes of the slice: x: 4, y: 4, z: 8, core: 2. Of those that a mesh axis runs over, the one named last changes fastest.
Arguments:
- head_start: float32 [6144, 16384], P('row', 'col'), may hold values from -6 to 6
- recharge: float32 [6144, 16384], P('row', 'col'), may hold values from -4 to 4
- storage: float32 [6144, 16384], P('row', 'col'), may hold values from 0.02 to 0.5
- seg_block: int32 [262144], P(('row', 'col')), may hold values from 0 to 3071
- seg_mask: int32 [262144, 128], P(('row', 'col')), may hold values 0 or 1
- seg_cond: float32 [262144, 128], P(('row', 'col')), may hold values from 0.02 to 0.2
- seg_reach: int32 [262144], P(('row', 'col')), may hold values from 0 to 65535, as said below
- reach_bed: float32 [65536], P(('row', 'col')), may hold values from -1 to 1
- section_start: float32 [65536], P(('row', 'col')), may hold values from 0 to 2
- reach_net: int32 [65536], P(('row', 'col')), may hold values from 0 to 63
- net_inflow: float32 [64], replicated, may hold values from 2 to 16
Outputs:
- head: float32 [6144, 16384], P('row', 'col')
- section: float32 [65536], P(('row', 'col'))
Inputs may be any that keep to these rules, and one draw needn't show every extreme that they name: `seg_reach`: A segment on device (i, j) names a reach owned by device (i, j - 1), (i, j) or (i, j + 1), columns taken modulo 16, where reach r is owned by device r // 256 in the numbering i * 16 + j.
All inputs are finite; a program needn't handle non-finite values. No bound on the sum of `seg_mask` on one device may be relied on, other than what follows from the above.
Results may differ from a plain program's by a relative error of at most 0.00029.
Values sent between devices are 32-bit elements; how exact they have to be, the bound alone decides.
No kernel may reach another device: no remote copies, remote signals or barrier semaphores. Data moves between devices by JAX's collectives and lax.ppermute only.
A program may use at most 64 MiB of HBM per device.

v0:
```python
import jax
import jax.numpy as jnp
from jax import lax
from jax.sharding import PartitionSpec as P

NETS = 64
PICARD = 2
SWEEPS = 4


def with_halo(cells, sides, width):
    for axis, dim in sides:
        count = lax.axis_size(axis)
        head = lax.slice_in_dim(cells, 0, width, axis=dim)
        tail = lax.slice_in_dim(cells, cells.shape[dim] - width, cells.shape[dim], axis=dim)
        cells = jnp.concatenate(
            [
                lax.ppermute(tail, axis, [(i, (i + 1) % count) for i in range(count)]),
                cells,
                lax.ppermute(head, axis, [((i + 1) % count, i) for i in range(count)]),
            ],
            axis=dim,
        )
    return cells


def passed_along(array, axis, by):
    length = lax.axis_size(axis)
    return lax.ppermute(array, axis, [(i, (i + by) % length) for i in range(length)])


def padded_2(array, sides, width):
    edges = {}
    for axis, dim in sides:
        size, length = (lax.axis_size(axis), array.shape[dim])
        up = [(i, (i + 1) % size) for i in range(size - 1)]
        last = lax.slice_in_dim(array, length - width, length, axis=dim)
        initial = lax.slice_in_dim(array, 0, width, axis=dim)
        edges[dim] = (
            lax.ppermute(last, axis, up),
            lax.ppermute(initial, axis, [(b, a) for a, b in up]),
        )
    done = []
    for _, dim in sides:
        low, high = edges[dim]
        around = [(width, width) if d in done else (0, 0) for d in range(array.ndim)]
        array = jnp.concatenate([jnp.pad(low, around), array, jnp.pad(high, around)], axis=dim)
        done.append(dim)
    return array


def relax(padded, storage, supply, cond, source):
    beside = padded[:-2, 1:-1] + padded[2:, 1:-1] + padded[1:-1, :-2] + padded[1:-1, 2:]
    return (beside + supply + source) / (4.0 + storage + cond)


def new_section(bed, inflow, total):
    return bed + jnp.sqrt(1.0 + jax.nn.softplus(inflow - total)) - 1.0


def body(
    head_start,
    recharge,
    storage,
    seg_block,
    seg_mask,
    seg_cond,
    seg_reach,
    reach_bed,
    section_start,
    reach_net,
    net_inflow,
):
    rows, cols = head_start.shape
    blocks = rows * cols // 128
    reaches = reach_bed.shape[0]
    n_col = lax.axis_size("col")
    col_index = lax.axis_index("col")
    weight = seg_mask.astype(jnp.float32) * seg_cond
    cond = jax.ops.segment_sum(weight, seg_block, blocks).reshape(rows, cols)
    picks = (reach_net[:, None] == jnp.arange(NETS, dtype=jnp.int32)[None, :]).astype(jnp.float32)
    inflow = jnp.dot(picks, net_inflow, precision=lax.Precision.HIGHEST)
    supply = storage * head_start + recharge
    owner_col = seg_reach // reaches % n_col
    window_slot = (owner_col - col_index + 1 + n_col) % n_col * reaches + seg_reach % reaches
    consts = with_halo(jnp.stack([reach_bed, inflow, section_start]), (("col", 1),), reaches)
    bed_window = consts[0]
    inflow_window = consts[1]
    first_seg = jnp.take(consts[2], window_slot)
    head = head_start
    section_seg = first_seg
    section = section_start
    for step in range(PICARD):
        head_seg = jnp.take(head.reshape(blocks, 128), seg_block, axis=0)
        leak = jnp.sum(weight * (section_seg[:, None] - head_seg), axis=1)
        partial_value = jax.ops.segment_sum(leak, window_slot, 3 * reaches).reshape(3, reaches)
        left_one = passed_along(partial_value, "col", 1)
        right_one = passed_along(partial_value, "col", -1)
        left_two = passed_along(partial_value[2], "col", 2)
        right_two = passed_along(partial_value[0], "col", -2)
        total = jnp.concatenate(
            [
                partial_value[0] + left_one[1] + left_two,
                partial_value[1] + left_one[2] + right_one[0],
                partial_value[2] + right_one[1] + right_two,
            ]
        )
        section_window = new_section(bed_window, inflow_window, total)
        section = section_window[reaches : 2 * reaches]
        section_seg = jnp.take(section_window, window_slot)
        source = jax.ops.segment_sum(weight * section_seg[:, None], seg_block, blocks).reshape(
            rows, cols
        )
        for sweep in range(SWEEPS):
            padded = padded_2(head, (("row", 0), ("col", 1)), 1)
            head = relax(padded, storage, supply, cond, source)
    return (head, section)


def solution(mesh):
    placed = (
        P("row", "col"),
        P("row", "col"),
        P("row", "col"),
        P(("row", "col")),
        P(("row", "col"), None),
        P(("row", "col"), None),
        P(("row", "col")),
        P(("row", "col")),
        P(("row", "col")),
        P(("row", "col")),
        P(),
    )
    return jax.shard_map(
        body,
        mesh=mesh,
        in_specs=placed,
        out_specs=(P("row", "col"), P(("row", "col"))),
        check_vma=False,
    )
```

profile of v0, /device:TPU:99, one launch (start us, length us, event | category | flops | bytes accessed | tf_op | source)
XLA Modules:
  0.0 264.6 jit_solution(13116102944946420644)
XLA Ops:
  30.5 7.6 %scatter_custom_fusion = f32[768]{0:T(1024)S(1)} fusion(s32[1024]{0:T(1024)S(1)} %get-tuple-element.15, f32[1024]{0:T(1024)S(1)} %get-tuple-element.10, f32[]{:T(128)} %constant.75.clone.1), kind=kCustom, calls=%fused_computation.212 | custom fusion | flops 1024 | bytes 3076 | tf_op jit(solution)/shard_map/scatter-add | solution.py:96
  41.1 6.5 %scatter_custom_fusion.2 = f32[3072,128]{1,0:T(8,128)S(1)} fusion(s32[1024]{0:T(1024)} %param.18, f32[1024,128]{1,0:T(8,128)S(1)} %get-tuple-element.11, f32[]{:T(128)} %constant.75.clone.1), kind=kCustom, calls=%fused_computation.144 | custom fusion | flops 131072 | bytes 1573376 | tf_op jit(solution)/shard_map/scatter-add | solution.py:80
  53.4 4.5 %gather_fusion.2 = f32[1024]{0:T(1024)S(1)} fusion(f32[768]{0:T(1024)S(1)} %fusion.89, s32[1024]{0:T(1024)S(1)} %get-tuple-element.14), kind=kCustom, calls=%fused_computation.2.clone | custom fusion | bytes 12288 | tf_op jit(solution)/shard_map/jit(_take)/gather | solution.py:110
  58.0 7.1 %scatter_custom_fusion.1 = f32[3072,128]{1,0:T(8,128)S(1)} fusion(s32[1024]{0:T(1024)} %param.18, f32[]{:T(128)} %constant.75.clone.1, f32[1024,128]{1,0:T(8,128)S(1)} %get-tuple-element.11, f32[1024]{0:T(1024)S(1)} %broadcast_select_fusion.1), kind=kCustom, calls=%fused_computation.146 | custom fusion | flops 262144 | bytes 2101760 | tf_op jit(solution)/shard_map/scatter-add | solution.py:111
  67.0 7.4 %fusion.60 = (f32[384,1024]{1,0:T(8,128)S(1)}, f32[384,1024]{1,0:T(8,128)S(1)}, f32[384,1024]{1,0:T(8,128)S(1)}) fusion(f32[384,1024]{1,0:T(8,128)} %reshape.53, f32[384,1]{1,0:T(8,128)S(1)} %collective-permute-done.3, f32[1,1024]{1,0:T(1,128)} %collective-permute-done.1, f32[384,1024]{1,0:T(8,128)} %param.15, f32[1,1024]{1,0:T(1,128)} %copy-done.14, ...), kind=kLoop, calls=%fused_computation.127 | loop fusion | flops 9437184 | bytes 12594176 | tf_op jit(solution)/shard_map/div | solution.py:54
  76.4 5.5 %collective-permute-start.11 = (f32[1,1024]{1,0:T(1,128)S(1)}, f32[1,1024]{1,0:T(1,128)S(1)}, u32[]{:S(2)}, u32[]{:S(2)}) collective-permute-start(f32[1,1024]{1,0:T(1,128)S(1)} %get-tuple-element.43), channel_id=1, source_target_pairs={{16,0},{32,16},{48,32},{64,48},{80,64},{96,80},{112,96},{128,112},... | collective-permute-start | bytes 12296 | tf_op jit(solution)/shard_map/ppermute | solution.py:41
  82.0 5.4 %collective-permute-start.12 = (f32[384,1]{1,0:T(8,128)S(1)}, f32[384,1]{1,0:T(8,128)S(1)}, u32[]{:S(2)}, u32[]{:S(2)}) collective-permute-start(f32[384,1]{1,0:T(8,128)S(1)} %get-tuple-element.40), channel_id=1, source_target_pairs={{0,1},{1,2},{2,3},{3,4},{4,5},{5,6},{6,7},{7,8},{8,9},{9,10},{10,1... | collective-permute-start | bytes 4616 | tf_op jit(solution)/shard_map/ppermute | solution.py:40
  90.0 5.6 %collective-permute-done.13 = f32[384,1]{1,0:T(8,128)S(1)} collective-permute-done((f32[384,1]{1,0:T(8,128)S(1)}, f32[384,1]{1,0:T(8,128)S(1)}, u32[]{:S(2)}, u32[]{:S(2)}) %collective-permute-start.13) | collective-permute-done | bytes 1568 | tf_op jit(solution)/shard_map/ppermute | solution.py:41
  100.1 5.5 %collective-permute-start.15 = (f32[1,1024]{1,0:T(1,128)S(1)}, f32[1,1024]{1,0:T(1,128)S(1)}, u32[]{:S(2)}, u32[]{:S(2)}) collective-permute-start(f32[1,1024]{1,0:T(1,128)S(1)} %get-tuple-element.39), channel_id=1, source_target_pairs={{16,0},{32,16},{48,32},{64,48},{80,64},{96,80},{112,96},{128,112},... | collective-permute-start | bytes 12296 | tf_op jit(solution)/shard_map/ppermute | solution.py:41
  110.6 5.6 %collective-permute-done.17 = f32[384,1]{1,0:T(8,128)S(1)} collective-permute-done((f32[384,1]{1,0:T(8,128)S(1)}, f32[384,1]{1,0:T(8,128)S(1)}, u32[]{:S(2)}, u32[]{:S(2)}) %collective-permute-start.17) | collective-permute-done | bytes 1568 | tf_op jit(solution)/shard_map/ppermute | solution.py:41
  120.6 5.5 %collective-permute-start.19 = (f32[1,1024]{1,0:T(1,128)S(1)}, f32[1,1024]{1,0:T(1,128)S(1)}, u32[]{:S(2)}, u32[]{:S(2)}) collective-permute-start(f32[1,1024]{1,0:T(1,128)S(1)} %get-tuple-element.35), channel_id=1, source_target_pairs={{16,0},{32,16},{48,32},{64,48},{80,64},{96,80},{112,96},{128,112},... | collective-permute-start | bytes 12296 | tf_op jit(solution)/shard_map/ppermute | solution.py:41
  131.1 5.6 %collective-permute-done.21 = f32[384,1]{1,0:T(8,128)S(1)} collective-permute-done((f32[384,1]{1,0:T(8,128)S(1)}, f32[384,1]{1,0:T(8,128)S(1)}, u32[]{:S(2)}, u32[]{:S(2)}) %collective-permute-start.21) | collective-permute-done | bytes 1568 | tf_op jit(solution)/shard_map/ppermute | solution.py:41
  143.0 5.4 %gather_fusion.3 = f32[1024,128]{1,0:T(8,128)} fusion(f32[3072,128]{1,0:T(8,128)} %reshape.55, s32[1024]{0:T(1024)S(1)} %copy-done.10), kind=kCustom, calls=%fused_computation.4.clone | custom fusion | bytes 1052672 | tf_op jit(solution)/shard_map/jit(_take)/gather | solution.py:94
  150.8 7.8 %scatter_custom_fusion.3 = f32[768]{0:T(1024)S(1)} fusion(s32[1024]{0:T(1024)} %copy-done.11, f32[1024]{0:T(1024)} %fusion.71, f32[]{:T(128)} %constant.75.clone.1), kind=kCustom, calls=%fused_computation.210 | custom fusion | flops 1024 | bytes 3584 | tf_op jit(solution)/shard_map/scatter-add | solution.py:96
  163.5 5.5 %collective-permute-start.23 = (f32[1,1024]{1,0:T(1,128)}, f32[1,1024]{1,0:T(1,128)}, u32[]{:S(2)}, u32[]{:S(2)}) collective-permute-start(f32[1,1024]{1,0:T(1,128)} %get-tuple-element.31), channel_id=1, source_target_pairs={{16,0},{32,16},{48,32},{64,48},{80,64},{96,80},{112,96},{128,112},... | collective-permute-start | bytes 12296 | tf_op jit(solution)/shard_map/ppermute | solution.py:41
  177.7 4.5 %gather_fusion.4 = f32[1024]{0:T(1024)S(1)} fusion(f32[768]{0:T(1024)S(1)} %fusion.93, s32[1024]{0:T(1024)S(1)} %get-tuple-element.14), kind=kCustom, calls=%fused_computation.3.clone | custom fusion | bytes 12288 | tf_op jit(solution)/shard_map/jit(_take)/gather | solution.py:110
  182.9 8.1 %scatter_custom_fusion.4 = f32[3072,128]{1,0:T(8,128)} fusion(s32[1024]{0:T(1024)} %param.18, f32[]{:T(128)} %constant.75.clone.1, f32[1024,128]{1,0:T(8,128)} %copy-done.4, f32[1024]{0:T(1024)S(1)} %broadcast_select_fusion), kind=kCustom, calls=%fused_computation.142 | custom fusion | flops 262144 | bytes 2101760 | tf_op jit(solution)/shard_map/scatter-add | solution.py:111
  193.7 6.3 %fusion.28 = f32[384,1024]{1,0:T(8,128)S(1)} fusion(f32[384,1024]{1,0:T(8,128)S(1)} %get-tuple-element.9, f32[384,1024]{1,0:T(8,128)} %reshape.57, f32[384,1024]{1,0:T(8,128)S(1)} %get-tuple-element.8, f32[384,1]{1,0:T(8,128)} %collective-permute-done.25, f32[1,1024]{1,0:T(1,128)} %collective-permute-done.23, f32[384,1024]{1,0:T(8,128)} %copy-done.3, ...), kind=kLoop, calls=%fused_computation.63 | loop fusion | flops 7864320 | bytes 7875584 | tf_op jit(solution)/shard_map/div | solution.py:54
  201.9 5.5 %collective-permute-start.31 = (f32[1,1024]{1,0:T(1,128)S(1)}, f32[1,1024]{1,0:T(1,128)S(1)}, u32[]{:S(2)}, u32[]{:S(2)}) collective-permute-start(f32[1,1024]{1,0:T(1,128)S(1)} %get-tuple-element.27), channel_id=1, source_target_pairs={{16,0},{32,16},{48,32},{64,48},{80,64},{96,80},{112,96},{128,112},... | collective-permute-start | bytes 12296 | tf_op jit(solution)/shard_map/ppermute | solution.py:41
  214.5 5.6 %collective-permute-done.33 = f32[384,1]{1,0:T(8,128)S(1)} collective-permute-done((f32[384,1]{1,0:T(8,128)S(1)}, f32[384,1]{1,0:T(8,128)S(1)}, u32[]{:S(2)}, u32[]{:S(2)}) %collective-permute-start.33) | collective-permute-done | bytes 1568 | tf_op jit(solution)/shard_map/ppermute | solution.py:41
  224.6 5.5 %collective-permute-start.35 = (f32[1,1024]{1,0:T(1,128)S(1)}, f32[1,1024]{1,0:T(1,128)S(1)}, u32[]{:S(2)}, u32[]{:S(2)}) collective-permute-start(f32[1,1024]{1,0:T(1,128)S(1)} %get-tuple-element.23), channel_id=1, source_target_pairs={{16,0},{32,16},{48,32},{64,48},{80,64},{96,80},{112,96},{128,112},... | collective-permute-start | bytes 12296 | tf_op jit(solution)/shard_map/ppermute | solution.py:41
  235.1 5.6 %collective-permute-done.37 = f32[384,1]{1,0:T(8,128)S(1)} collective-permute-done((f32[384,1]{1,0:T(8,128)S(1)}, f32[384,1]{1,0:T(8,128)S(1)}, u32[]{:S(2)}, u32[]{:S(2)}) %collective-permute-start.37) | collective-permute-done | bytes 1568 | tf_op jit(solution)/shard_map/ppermute | solution.py:41
  245.1 5.5 %collective-permute-start.39 = (f32[1,1024]{1,0:T(1,128)S(1)}, f32[1,1024]{1,0:T(1,128)S(1)}, u32[]{:S(2)}, u32[]{:S(2)}) collective-permute-start(f32[1,1024]{1,0:T(1,128)S(1)} %get-tuple-element.19), channel_id=1, source_target_pairs={{16,0},{32,16},{48,32},{64,48},{80,64},{96,80},{112,96},{128,112},... | collective-permute-start | bytes 12296 | tf_op jit(solution)/shard_map/ppermute | solution.py:41
  255.7 5.6 %collective-permute-done.41 = f32[384,1]{1,0:T(8,128)S(1)} collective-permute-done((f32[384,1]{1,0:T(8,128)S(1)}, f32[384,1]{1,0:T(8,128)S(1)}, u32[]{:S(2)}, u32[]{:S(2)}) %collective-permute-start.41) | collective-permute-done | bytes 1568 | tf_op jit(solution)/shard_map/ppermute | solution.py:41
  (157 shorter events, 120.5 us)
Async XLA Ops:
  2.9 22.2 %collective-permute-start.5 = (f32[3,256]{1,0:T(4,128)S(1)}, f32[3,256]{1,0:T(4,128)S(1)}, u32[]{:S(2)}, u32[]{:S(2)}) collective-permute-start(f32[3,256]{1,0:T(4,128)S(1)} %pad_maximum_fusion.48), channel_id=1, source_target_pairs={{1,0},{2,1},{3,2},{4,3},{5,4},{6,5},{7,6},{8,7},{9,8},{10,9},{11,1... | collective-permute-start | bytes 9224 | tf_op jit(solution)/shard_map/ppermute | solution.py:20
  3.6 21.6 %collective-permute-start.4 = (f32[3,256]{1,0:T(4,128)S(1)}, f32[3,256]{1,0:T(4,128)S(1)}, u32[]{:S(2)}, u32[]{:S(2)}) collective-permute-start(f32[3,256]{1,0:T(4,128)S(1)} %pad_maximum_fusion.48), channel_id=1, source_target_pairs={{0,1},{1,2},{2,3},{3,4},{4,5},{5,6},{6,7},{7,8},{8,9},{9,10},{10,1... | collective-permute-start | bytes 9224 | tf_op jit(solution)/shard_map/ppermute | solution.py:18
  7.1 59.3 %collective-permute-start = (f32[1,1024]{1,0:T(1,128)S(1)}, f32[1,1024]{1,0:T(1,128)S(1)}, u32[]{:S(2)}, u32[]{:S(2)}) collective-permute-start(f32[1,1024]{1,0:T(1,128)S(1)} %get-tuple-element.46), channel_id=1, source_target_pairs={{0,16},{16,32},{32,48},{48,64},{64,80},{80,96},{96,112},{112,128},... | collective-permute-start | bytes 12296 | tf_op jit(solution)/shard_map/ppermute | solution.py:40
  10.3 56.7 %collective-permute-start.1 = (f32[1,1024]{1,0:T(1,128)S(1)}, f32[1,1024]{1,0:T(1,128)}, u32[]{:S(2)}, u32[]{:S(2)}) collective-permute-start(f32[1,1024]{1,0:T(1,128)S(1)} %get-tuple-element.47), channel_id=1, source_target_pairs={{16,0},{32,16},{48,32},{64,48},{80,64},{96,80},{112,96},{128,112},... | collective-permute-start | bytes 12296 | tf_op jit(solution)/shard_map/ppermute | solution.py:41
  15.7 50.8 %collective-permute-start.2 = (f32[384,1]{1,0:T(8,128)S(1)}, f32[384,1]{1,0:T(8,128)S(1)}, u32[]{:S(2)}, u32[]{:S(2)}) collective-permute-start(f32[384,1]{1,0:T(8,128)S(1)} %get-tuple-element.44), channel_id=1, source_target_pairs={{0,1},{1,2},{2,3},{3,4},{4,5},{5,6},{6,7},{7,8},{8,9},{9,10},{10,1... | collective-permute-start | bytes 4616 | tf_op jit(solution)/shard_map/ppermute | solution.py:40
  51.4 15.0 %collective-permute-start.3 = (f32[384,1]{1,0:T(8,128)S(1)}, f32[384,1]{1,0:T(8,128)S(1)}, u32[]{:S(2)}, u32[]{:S(2)}) collective-permute-start(f32[384,1]{1,0:T(8,128)S(1)} %get-tuple-element.45), channel_id=1, source_target_pairs={{1,0},{2,1},{3,2},{4,3},{5,4},{6,5},{7,6},{8,7},{9,8},{10,9},{11,1... | collective-permute-start | bytes 4616 | tf_op jit(solution)/shard_map/ppermute | solution.py:41
  74.4 21.2 %collective-permute-start.10 = (f32[1,1024]{1,0:T(1,128)S(1)}, f32[1,1024]{1,0:T(1,128)S(1)}, u32[]{:S(2)}, u32[]{:S(2)}) collective-permute-start(f32[1,1024]{1,0:T(1,128)S(1)} %get-tuple-element.42), channel_id=1, source_target_pairs={{0,16},{16,32},{32,48},{48,64},{64,80},{80,96},{96,112},{112,128},... | collective-permute-start | bytes 12296 | tf_op jit(solution)/shard_map/ppermute | solution.py:40
  76.4 19.2 %collective-permute-start.11 = (f32[1,1024]{1,0:T(1,128)S(1)}, f32[1,1024]{1,0:T(1,128)S(1)}, u32[]{:S(2)}, u32[]{:S(2)}) collective-permute-start(f32[1,1024]{1,0:T(1,128)S(1)} %get-tuple-element.43), channel_id=1, source_target_pairs={{16,0},{32,16},{48,32},{64,48},{80,64},{96,80},{112,96},{128,112},... | collective-permute-start | bytes 12296 | tf_op jit(solution)/shard_map/ppermute | solution.py:41
  98.1 18.0 %collective-permute-start.14 = (f32[1,1024]{1,0:T(1,128)S(1)}, f32[1,1024]{1,0:T(1,128)S(1)}, u32[]{:S(2)}, u32[]{:S(2)}) collective-permute-start(f32[1,1024]{1,0:T(1,128)S(1)} %get-tuple-element.38), channel_id=1, source_target_pairs={{0,16},{16,32},{32,48},{48,64},{64,80},{80,96},{96,112},{112,128},... | collective-permute-start | bytes 12296 | tf_op jit(solution)/shard_map/ppermute | solution.py:40
  100.1 16.1 %collective-permute-start.15 = (f32[1,1024]{1,0:T(1,128)S(1)}, f32[1,1024]{1,0:T(1,128)S(1)}, u32[]{:S(2)}, u32[]{:S(2)}) collective-permute-start(f32[1,1024]{1,0:T(1,128)S(1)} %get-tuple-element.39), channel_id=1, source_target_pairs={{16,0},{32,16},{48,32},{64,48},{80,64},{96,80},{112,96},{128,112},... | collective-permute-start | bytes 12296 | tf_op jit(solution)/shard_map/ppermute | solution.py:41
  118.7 18.0 %collective-permute-start.18 = (f32[1,1024]{1,0:T(1,128)S(1)}, f32[1,1024]{1,0:T(1,128)S(1)}, u32[]{:S(2)}, u32[]{:S(2)}) collective-permute-start(f32[1,1024]{1,0:T(1,128)S(1)} %get-tuple-element.34), channel_id=1, source_target_pairs={{0,16},{16,32},{32,48},{48,64},{64,80},{80,96},{96,112},{112,128},... | collective-permute-start | bytes 12296 | tf_op jit(solution)/shard_map/ppermute | solution.py:40
  120.6 16.1 %collective-permute-start.19 = (f32[1,1024]{1,0:T(1,128)S(1)}, f32[1,1024]{1,0:T(1,128)S(1)}, u32[]{:S(2)}, u32[]{:S(2)}) collective-permute-start(f32[1,1024]{1,0:T(1,128)S(1)} %get-tuple-element.35), channel_id=1, source_target_pairs={{16,0},{32,16},{48,32},{64,48},{80,64},{96,80},{112,96},{128,112},... | collective-permute-start | bytes 12296 | tf_op jit(solution)/shard_map/ppermute | solution.py:41
  158.6 12.9 %collective-permute-start.28 = (f32[3,256]{1,0:T(4,128)S(1)}, f32[3,256]{1,0:T(4,128)S(1)}, u32[]{:S(2)}, u32[]{:S(2)}) collective-permute-start(f32[3,256]{1,0:T(4,128)S(1)} %reshape.56), channel_id=1, source_target_pairs={{0,15},{1,0},{2,1},{3,2},{4,3},{5,4},{6,5},{7,6},{8,7},{9,8},{10,9... | collective-permute-start | bytes 9224 | tf_op jit(solution)/shard_map/ppermute | solution.py:29
  158.6 12.9 %collective-permute-start.26 = (f32[3,256]{1,0:T(4,128)S(1)}, f32[3,256]{1,0:T(4,128)S(1)}, u32[]{:S(2)}, u32[]{:S(2)}) collective-permute-start(f32[3,256]{1,0:T(4,128)S(1)} %reshape.56), channel_id=1, source_target_pairs={{0,1},{1,2},{2,3},{3,4},{4,5},{5,6},{6,7},{7,8},{8,9},{9,10},{10,1... | collective-permute-start | bytes 9224 | tf_op jit(solution)/shard_map/ppermute | solution.py:29
  161.6 32.1 %collective-permute-start.22 = (f32[1,1024]{1,0:T(1,128)}, f32[1,1024]{1,0:T(1,128)}, u32[]{:S(2)}, u32[]{:S(2)}) collective-permute-start(f32[1,1024]{1,0:T(1,128)} %get-tuple-element.30), channel_id=1, source_target_pairs={{0,16},{16,32},{32,48},{48,64},{64,80},{80,96},{96,112},{112,128},... | collective-permute-start | bytes 12296 | tf_op jit(solution)/shard_map/ppermute | solution.py:40
  163.5 30.1 %collective-permute-start.23 = (f32[1,1024]{1,0:T(1,128)}, f32[1,1024]{1,0:T(1,128)}, u32[]{:S(2)}, u32[]{:S(2)}) collective-permute-start(f32[1,1024]{1,0:T(1,128)} %get-tuple-element.31), channel_id=1, source_target_pairs={{16,0},{32,16},{48,32},{64,48},{80,64},{96,80},{112,96},{128,112},... | collective-permute-start | bytes 12296 | tf_op jit(solution)/shard_map/ppermute | solution.py:41
  169.0 24.7 %collective-permute-start.24 = (f32[384,1]{1,0:T(8,128)S(1)}, f32[384,1]{1,0:T(8,128)}, u32[]{:S(2)}, u32[]{:S(2)}) collective-permute-start(f32[384,1]{1,0:T(8,128)S(1)} %get-tuple-element.28), channel_id=1, source_target_pairs={{0,1},{1,2},{2,3},{3,4},{4,5},{5,6},{6,7},{7,8},{8,9},{9,10},{10,1... | collective-permute-start | bytes 4616 | tf_op jit(solution)/shard_map/ppermute | solution.py:40
  174.1 19.5 %collective-permute-start.25 = (f32[384,1]{1,0:T(8,128)S(1)}, f32[384,1]{1,0:T(8,128)}, u32[]{:S(2)}, u32[]{:S(2)}) collective-permute-start(f32[384,1]{1,0:T(8,128)S(1)} %get-tuple-element.29), channel_id=1, source_target_pairs={{1,0},{2,1},{3,2},{4,3},{5,4},{6,5},{7,6},{8,7},{9,8},{10,9},{11,1... | collective-permute-start | bytes 4616 | tf_op jit(solution)/shard_map/ppermute | solution.py:41
  199.9 20.2 %collective-permute-start.30 = (f32[1,1024]{1,0:T(1,128)S(1)}, f32[1,1024]{1,0:T(1,128)S(1)}, u32[]{:S(2)}, u32[]{:S(2)}) collective-permute-start(f32[1,1024]{1,0:T(1,128)S(1)} %get-tuple-element.26), channel_id=1, source_target_pairs={{0,16},{16,32},{32,48},{48,64},{64,80},{80,96},{96,112},{112,128},... | collective-permute-start | bytes 12296 | tf_op jit(solution)/shard_map/ppermute | solution.py:40
  201.9 18.3 %collective-permute-start.31 = (f32[1,1024]{1,0:T(1,128)S(1)}, f32[1,1024]{1,0:T(1,128)S(1)}, u32[]{:S(2)}, u32[]{:S(2)}) collective-permute-start(f32[1,1024]{1,0:T(1,128)S(1)} %get-tuple-element.27), channel_id=1, source_target_pairs={{16,0},{32,16},{48,32},{64,48},{80,64},{96,80},{112,96},{128,112},... | collective-permute-start | bytes 12296 | tf_op jit(solution)/shard_map/ppermute | solution.py:41
  222.7 18.0 %collective-permute-start.34 = (f32[1,1024]{1,0:T(1,128)S(1)}, f32[1,1024]{1,0:T(1,128)S(1)}, u32[]{:S(2)}, u32[]{:S(2)}) collective-permute-start(f32[1,1024]{1,0:T(1,128)S(1)} %get-tuple-element.22), channel_id=1, source_target_pairs={{0,16},{16,32},{32,48},{48,64},{64,80},{80,96},{96,112},{112,128},... | collective-permute-start | bytes 12296 | tf_op jit(solution)/shard_map/ppermute | solution.py:40
  224.6 16.1 %collective-permute-start.35 = (f32[1,1024]{1,0:T(1,128)S(1)}, f32[1,1024]{1,0:T(1,128)S(1)}, u32[]{:S(2)}, u32[]{:S(2)}) collective-permute-start(f32[1,1024]{1,0:T(1,128)S(1)} %get-tuple-element.23), channel_id=1, source_target_pairs={{16,0},{32,16},{48,32},{64,48},{80,64},{96,80},{112,96},{128,112},... | collective-permute-start | bytes 12296 | tf_op jit(solution)/shard_map/ppermute | solution.py:41
  243.2 18.0 %collective-permute-start.38 = (f32[1,1024]{1,0:T(1,128)S(1)}, f32[1,1024]{1,0:T(1,128)S(1)}, u32[]{:S(2)}, u32[]{:S(2)}) collective-permute-start(f32[1,1024]{1,0:T(1,128)S(1)} %get-tuple-element.18), channel_id=1, source_target_pairs={{0,16},{16,32},{32,48},{48,64},{64,80},{80,96},{96,112},{112,128},... | collective-permute-start | bytes 12296 | tf_op jit(solution)/shard_map/ppermute | solution.py:40
  245.1 16.1 %collective-permute-start.39 = (f32[1,1024]{1,0:T(1,128)S(1)}, f32[1,1024]{1,0:T(1,128)S(1)}, u32[]{:S(2)}, u32[]{:S(2)}) collective-permute-start(f32[1,1024]{1,0:T(1,128)S(1)} %get-tuple-element.19), channel_id=1, source_target_pairs={{16,0},{32,16},{48,32},{64,48},{80,64},{96,80},{112,96},{128,112},... | collective-permute-start | bytes 12296 | tf_op jit(solution)/shard_map/ppermute | solution.py:41
  (35 other events, 329.8 us)
where the time goes:
time: 266 us; the launch traced here: 265 us
  starting transfers between devices  113 us (42%)
  other arithmetic  73.7 us (28%)
  waiting for transfers between devices  38.6 us (15%)
  local copies, waits for them, and re-layouts  37.1 us (14%)
    ppermute x16, starting transfers between devices, padded_2(): lax.ppermute(initial, axis, [(b, a) for a, b in up])  59.4 us
    ppermute x16, starting transfers between devices, padded_2(): lax.ppermute(last, axis, up)  41.1 us
    ppermute x16, waiting for transfers between devices, padded_2(): lax.ppermute(initial, axis, [(b, a) for a, b in up])  33.7 us
    div x8, other arithmetic, relax(): return (beside + supply + source) / (4.0 + storage + cond)  29.4 us
    scatter-add x2, other arithmetic, body(): jax.ops.segment_sum(leak, window_slot, 3 * reaches).reshape(3, reaches)  15.4 us
    scatter-add x2, other arithmetic, body(): jax.ops.segment_sum(weight * section_seg[:, None], seg_block, blocks)  15.2 us
    gather x2, local copies, waits for them, and re-layouts, body(): section_seg = jnp.take(section_window, window_slot)  9.06 us
    ppermute x8, starting transfers between devices, passed_along(): lax.ppermute(array, axis, [(i, (i + by) % length) for i in range(length)])  8.89 us
  transfers between devices with their start and end apart: 42, of which 13 were waited for; matrix products, arithmetic and copies ran while one was open for 23% of the time, Pallas kernels for 0%

commit v1 on v0

v1 whole, which is shorter than its diff:
```python
import functools

import jax
import jax.numpy as jnp
from jax import lax
from jax.experimental import pallas as pl
from jax.experimental.pallas import tpu as pltpu
from jax.sharding import PartitionSpec as P

NETS = 64
SWEEPS = 4
ROWS, COLS = 384, 1024
TILES = COLS // 128
SEG = 1024
REACH = 256
FRAME = 4 * REACH
OFF = 16
EXT = ROWS + 2 * OFF
H = 4
CHUNKS = ROWS // 8 + 2
F32 = jnp.float32
BF16 = jnp.bfloat16


def spec(space=pltpu.VMEM):
    return pl.BlockSpec(memory_space=space)


def split2(x):
    hi = x.astype(BF16)
    lo = (x - hi.astype(F32)).astype(BF16)
    return hi, lo


def column_of(row):
    return jnp.broadcast_to(row, (128, 128)).T


def gather_rows(read, blk, out):
    def group(g, carry):
        for u in range(16):
            s = g * 16 + u
            b = blk[s]
            out[pl.ds(s, 1), :] = read(b >> 3, b & 7)
        return carry

    lax.fori_loop(0, SEG // 16, group, 0)


def row_sums(get, lhs, first):
    for k in range(SEG // 128):
        at = slice(k * 128, (k + 1) * 128)
        row = jnp.sum(get(at).T, axis=0, keepdims=True)
        hi = row.astype(BF16).astype(F32)
        mid = (row - hi).astype(BF16).astype(F32)
        lhs[first : first + 1, at] = hi
        lhs[first + 1 : first + 2, at] = mid
        lhs[first + 2 : first + 3, at] = row - hi - mid


def clear_rim(ref):
    zero = jnp.zeros((OFF, 128), F32)
    for c in range(TILES):
        ref[c, 0:OFF, :] = zero
        ref[c, OFF + ROWS : EXT, :] = zero
    ref[TILES, :, :] = jnp.zeros((EXT, 128), F32)


def prep(head, blk, reach, mask, condu, bed, sec0, net, infl, part, oh, weight, headx, hs, lhs):
    j = lax.axis_index("col")
    base = (j // 2) * 2 - 1
    reach8 = reach[...]
    slot8 = (((reach8 // REACH) % 16 - base + 16) % 16) * REACH + reach8 % REACH

    def read(r, c):
        return headx[c, pl.ds(r + OFF, 1), :]

    clear_rim(headx)
    for c in range(TILES):
        headx[c, OFF : OFF + ROWS, :] = head[:, c * 128 : (c + 1) * 128]
    weight[...] = mask[...].astype(F32) * condu[...]
    gather_rows(read, blk, hs)
    lhs[...] = jnp.zeros_like(lhs)
    row_sums(lambda at: weight[at, :] * hs[at, :], lhs, 0)
    row_sums(lambda at: weight[at, :], lhs, 3)
    lane = lax.broadcasted_iota(jnp.int32, (128, 128), 1)
    for k in range(SEG // 128):
        slots = column_of(slot8[k : k + 1, :])
        for q in range(FRAME // 128):
            oh[k * 128 : (k + 1) * 128, q * 128 : (q + 1) * 128] = jnp.where(
                slots == lane + q * 128, 1.0, 0.0
            ).astype(BF16)
    sums = jnp.dot(lhs[...].astype(BF16), oh[...], preferred_element_type=F32)
    part[...] = jnp.zeros_like(part)
    part[0:1, :] = sums[0:1] + sums[1:2] + sums[2:3]
    part[1:2, :] = sums[3:4] + sums[4:5] + sums[5:6]
    nets = net[...]
    inflow = jnp.zeros(nets.shape, F32)
    for n in range(NETS):
        inflow = jnp.where(nets == n, infl[n], inflow)
    values = (bed[...], inflow, sec0[...])
    odd = j % 2
    for w in range(2):
        keep = odd == w
        for t in range(2):
            at = (1 + w) * REACH + t * 128
            for q, v in enumerate(values):
                part[2 + q : 3 + q, at : at + 128] = jnp.where(keep, v[t : t + 1, :], 0.0)


def fields(headx, recharge, storage, blk8, weight, onehot, inv, supply):
    blk = blk8[...]
    target = (blk & 7) * ROWS + (blk >> 3)
    iota = lax.broadcasted_iota(jnp.int32, (ROWS, 128), 0)
    for k in range(SEG // 128):
        row = jnp.broadcast_to(target[k : k + 1, :], (ROWS, 128))
        for c in range(TILES):
            onehot[c * ROWS : (c + 1) * ROWS, k * 128 : (k + 1) * 128] = jnp.where(
                row == iota + c * ROWS, 1.0, 0.0
            ).astype(BF16)
    hi, lo = split2(weight[...])
    both = jnp.concatenate([hi, lo], axis=1)
    clear_rim(inv)
    for c in range(TILES):
        at = slice(c * 128, (c + 1) * 128)
        got = jnp.dot(onehot[c * ROWS : (c + 1) * ROWS, :], both, preferred_element_type=F32)
        cond = got[:, :128] + got[:, 128:]
        start = headx[c, OFF : OFF + ROWS, :]
        store = storage[:, at]
        inv[c, OFF : OFF + ROWS, :] = 1.0 / (4.0 + store + cond)
        supply[c] = store * start + recharge[:, at]


def source_kernel(first, *refs):
    if first:
        own, up, down, oh, onehot, weight, supply, inv, headx, frame, section, rhs, sa, sb = refs
        fields_sent = (headx, rhs, inv)
    else:
        own, up, down, old, oh, onehot, weight, supply, headx, section, rhs, sa, sb = refs
        fields_sent = (headx, rhs)
    i = lax.axis_index("row")
    j = lax.axis_index("col")
    full = own[...] + jnp.concatenate([up[...], down[...]], axis=1)
    leak = full[0:1]
    if first:
        wsum, bed, inflow, sec = full[1:2], full[2:3], full[3:4], full[4:5]
    else:
        wsum, bed, inflow, sec = (old[q : q + 1, :] for q in (1, 2, 3, 4))
    x = inflow - (sec * wsum - leak)
    soft = jnp.maximum(x, 0.0) + jnp.log1p(jnp.exp(-jnp.abs(x)))
    sec = bed + jnp.sqrt(1.0 + soft) - 1.0
    if first:
        frame[...] = full
        frame[4:5, :] = sec
    odd = j % 2 == 1
    for t in range(2):
        a = REACH + t * 128
        b = 2 * REACH + t * 128
        section[t : t + 1, :] = jnp.where(odd, sec[:, b : b + 128], sec[:, a : a + 128])
    hi, lo = split2(sec)
    wide = jnp.concatenate(
        [jnp.broadcast_to(hi.astype(F32), (128, FRAME)), jnp.broadcast_to(lo.astype(F32), (128, FRAME))], axis=0
    ).astype(BF16)
    got = lax.dot_general(oh[...], wide, (((1,), (1,)), ((), ())), preferred_element_type=F32)
    hi, lo = split2(weight[...] * (got[:, :128] + got[:, 128:]))
    both = jnp.concatenate([hi, lo], axis=1)
    clear_rim(rhs)
    for c in range(TILES):
        got = jnp.dot(onehot[c * ROWS : (c + 1) * ROWS, :], both, preferred_element_type=F32)
        rhs[c, OFF : OFF + ROWS, :] = supply[c] + got[:, :128] + got[:, 128:]
    row_odd = i % 2 == 1
    if sa.shape[1] > len(fields_sent) * H:
        sa[...] = jnp.zeros_like(sa)
        sb[...] = jnp.zeros_like(sb)
    for q, ref in enumerate(fields_sent):
        top = ref[0:TILES, OFF : OFF + H, :]
        bottom = ref[0:TILES, OFF + ROWS - H : OFF + ROWS, :]
        sa[:, q * H : (q + 1) * H, :] = jnp.where(row_odd, top, bottom)
        sb[:, q * H : (q + 1) * H, :] = jnp.where(row_odd, bottom, top)


def columns(*refs):
    count = (len(refs) - 2)
    ma, mb = refs[count:]
    odd = lax.axis_index("col") % 2 == 1
    ma[...] = jnp.zeros_like(ma)
    mb[...] = jnp.zeros_like(mb)
    for q in range(count):
        for k in range(ROWS // 128):
            at = slice(OFF + k * 128, OFF + (k + 1) * 128)
            left = refs[q][0, at, :].T[0:H, :]
            right = refs[q][TILES - 1, at, :].T[128 - H : 128, :]
            ma[q * H : (q + 1) * H, k * 128 : (k + 1) * 128] = jnp.where(odd, left, right)
            mb[q * H : (q + 1) * H, k * 128 : (k + 1) * 128] = jnp.where(odd, right, left)


def top_bottom(ra, rb):
    i = lax.axis_index("row")
    odd = i % 2 == 1
    top = jnp.where(i == 0, 0.0, jnp.where(odd, ra, rb))
    bottom = jnp.where(i == 15, 0.0, jnp.where(odd, rb, ra))
    return top, bottom


def corners(ra, rb, ma, mb, na, nb, tall):
    odd = lax.axis_index("col") % 2 == 1
    depth = ra.shape[1]
    parts = []
    for c in (0, TILES - 1):
        top, bottom = top_bottom(ra[c], rb[c])
        tall[...] = jnp.zeros_like(tall)
        tall[0:depth, :] = top
        tall[depth : 2 * depth, :] = bottom
        turned = tall[...].T
        parts.append(turned[0:H, :] if c == 0 else turned[128 - H : 128, :])
    left, right = parts
    na[...] = ma[...]
    nb[...] = mb[...]
    na[0:H, ROWS : ROWS + 128] = jnp.where(odd, left, right)
    nb[0:H, ROWS : ROWS + 128] = jnp.where(odd, right, left)


def sweep(src, dst, rhs, inv):
    lane = lax.broadcasted_iota(jnp.int32, (8, 128), 1)
    first = lane == 0
    last = lane == 127

    def chunk(k):
        r = 8 + k * 8
        mid = [src[c, pl.ds(r, 8), :] for c in range(TILES + 1)]
        fwd = [pltpu.roll(m, 1, 1) for m in mid]
        bwd = [pltpu.roll(m, 127, 1) for m in mid]
        for c in range(TILES + 1):
            left = jnp.where(first, fwd[c - 1], fwd[c])
            right = jnp.where(last, bwd[(c + 1) % (TILES + 1)], bwd[c])
            beside = src[c, pl.ds(r - 1, 8), :] + src[c, pl.ds(r + 1, 8), :]
            total = beside + (left + right) + rhs[c, pl.ds(r, 8), :]
            dst[c, pl.ds(r, 8), :] = total * inv[c, pl.ds(r, 8), :]

    def group(g, carry):
        for u in range(5):
            chunk(g * 5 + u)
        return carry

    lax.fori_loop(0, CHUNKS // 5, group, 0)


def place_halo(refs, ra, rb, ca, cb, wide):
    depth = ra.shape[1]
    j = lax.axis_index("col")
    odd = j % 2 == 1
    top, bottom = top_bottom(ra[...], rb[...])
    right = jnp.where(j == 15, 0.0, jnp.where(odd, cb[...], ca[...]))
    left = jnp.where(j == 0, 0.0, jnp.where(odd, ca[...], cb[...]))
    wide[...] = jnp.zeros_like(wide)
    wide[0:H, 0:128] = right[0:H, ROWS : ROWS + 128]
    wide[128 - H : 128, 0:128] = left[0:H, ROWS : ROWS + 128]
    turned = wide[:, 0:128].T
    for q, ref in enumerate(refs):
        own = slice(q * H, (q + 1) * H)
        ref[0:TILES, OFF - H : OFF, :] = top[:, own, :]
        ref[0:TILES, OFF + ROWS : OFF + ROWS + H, :] = bottom[:, own, :]
        ref[TILES, OFF - H : OFF, :] = turned[own, :]
        ref[TILES, OFF + ROWS : OFF + ROWS + H, :] = turned[depth + q * H : depth + (q + 1) * H, :]
        wide[0:H, :] = right[own, 0:ROWS]
        wide[128 - H : 128, :] = left[own, 0:ROWS]
        for k in range(ROWS // 128):
            ref[TILES, OFF + k * 128 : OFF + (k + 1) * 128, :] = wide[:, k * 128 : (k + 1) * 128].T


def relax_first(ra, rb, ca, cb, head_in, rhs_in, inv_in, blk, weight, oh, head, rhs, inv, part, other, wide, hs, lhs):
    place_halo((head, rhs, inv), ra, rb, ca, cb, wide)
    for c in range(TILES + 1):
        other[c, 0:8, :] = jnp.zeros((8, 128), F32)
        other[c, EXT - 8 : EXT, :] = jnp.zeros((8, 128), F32)
    for _ in range(SWEEPS // 2):
        sweep(head, other, rhs, inv)
        sweep(other, head, rhs, inv)

    def read(r, c):
        return head[c, pl.ds(r + OFF, 1), :]

    gather_rows(read, blk, hs)
    lhs[...] = jnp.zeros_like(lhs)
    row_sums(lambda at: weight[at, :] * hs[at, :], lhs, 0)
    sums = jnp.dot(lhs[...].astype(BF16), oh[...], preferred_element_type=F32)
    part[...] = jnp.zeros_like(part)
    part[0:1, :] = sums[0:1] + sums[1:2] + sums[2:3]


def relax_last(ra, rb, ca, cb, head_in, rhs_in, inv, out, head, rhs, other, wide):
    place_halo((head, rhs), ra, rb, ca, cb, wide)
    for c in range(TILES + 1):
        other[c, 0:8, :] = jnp.zeros((8, 128), F32)
        other[c, EXT - 8 : EXT, :] = jnp.zeros((8, 128), F32)
    for _ in range(SWEEPS // 2):
        sweep(head, other, rhs, inv)
        sweep(other, head, rhs, inv)
    for c in range(TILES):
        out[:, c * 128 : (c + 1) * 128] = head[c, OFF : OFF + ROWS, :]


def shape(*dims, dtype=F32):
    return jax.ShapeDtypeStruct(dims, dtype)


def call(kernel, outs, ins, name, scratch=(), smem=(), aliases=None, limit=20, flops=10_000_000):
    return pl.pallas_call(
        kernel,
        out_shape=outs,
        in_specs=[spec(pltpu.SMEM) if k in smem else spec() for k in range(len(ins))],
        out_specs=jax.tree.map(lambda _: spec(), outs),
        scratch_shapes=list(scratch),
        input_output_aliases=aliases or {},
        compiler_params=pltpu.CompilerParams(vmem_limit_bytes=limit * 2**20),
        cost_estimate=pl.CostEstimate(flops=flops, bytes_accessed=4_000_000, transcendentals=0),
        name=name,
    )(*ins)


def swap(x, axis, which):
    n = lax.axis_size(axis)
    if which == 0:
        pairs = [(k, k ^ 1) for k in range(n)]
    else:
        pairs = [(k, (k + 1) % n if k % 2 else (k - 1) % n) for k in range(n)]
    return lax.ppermute(x, axis, pairs)


def shift(x, axis, by):
    n = lax.axis_size(axis)
    return lax.ppermute(x, axis, [(k, (k + by) % n) for k in range(n)])


def exchange_sums(part):
    both = part + swap(part, "col", 0)
    up = shift(both[:, 2 * REACH :], "col", 2)
    down = shift(both[:, : 2 * REACH], "col", -2)
    return both, up, down


ext = shape(TILES + 1, EXT, 128)


def halo_exchange(sent, sa, sb, count):
    depth = 16 if count == 3 else 8
    ma, mb = call(columns, (shape(depth, 512), shape(depth, 512)), sent, "cols")
    ra = swap(sa, "row", 0)
    rb = swap(sb, "row", 1)
    na, nb = call(
        corners,
        (shape(depth, 512), shape(depth, 512)),
        (ra, rb, ma, mb),
        "corners",
        scratch=[pltpu.VMEM((128, 128), F32)],
    )
    ca = swap(na, "col", 0)
    cb = swap(nb, "col", 1)
    return ra, rb, ca, cb


def body(head0, recharge, storage, seg_block, seg_mask, seg_cond, seg_reach, bed, sec0, net, infl):
    blk8 = seg_block.reshape(8, 128)
    part, oh, weight, headx = call(
        prep,
        (shape(8, FRAME), shape(SEG, FRAME, dtype=BF16), shape(SEG, 128), ext),
        (
            head0,
            seg_block,
            seg_reach.reshape(8, 128),
            seg_mask,
            seg_cond,
            bed.reshape(2, 128),
            sec0.reshape(2, 128),
            net.reshape(2, 128),
            infl,
        ),
        "prep",
        scratch=[pltpu.VMEM((SEG, 128), F32), pltpu.VMEM((16, SEG), F32)],
        smem=(1, 8),
    )
    both, up, down = exchange_sums(part)
    onehot, inv, supply = call(
        fields,
        (shape(TILES * ROWS, SEG, dtype=BF16), ext, shape(TILES, ROWS, 128)),
        (headx, recharge, storage, blk8, weight),
        "fields",
        limit=24,
    )
    strip = shape(TILES, 16, 128)
    frame, section, rhs, sa, sb = call(
        functools.partial(source_kernel, True),
        (shape(8, FRAME), shape(2, 128), ext, strip, strip),
        (both, up, down, oh, onehot, weight, supply, inv, headx),
        "source1",
        limit=24,
    )
    ra, rb, ca, cb = halo_exchange((headx, rhs, inv), sa, sb, 3)
    head, rhs, inv, part = call(
        relax_first,
        (ext, ext, ext, shape(8, FRAME)),
        (ra, rb, ca, cb, headx, rhs, inv, seg_block, weight, oh),
        "relax1",
        scratch=[
            pltpu.VMEM((TILES + 1, EXT, 128), F32),
            pltpu.VMEM((128, ROWS), F32),
            pltpu.VMEM((SEG, 128), F32),
            pltpu.VMEM((16, SEG), F32),
        ],
        smem=(7,),
        aliases={4: 0, 5: 1, 6: 2},
    )
    both, up, down = exchange_sums(part)
    strip = shape(TILES, 8, 128)
    section, rhs, sa, sb = call(
        functools.partial(source_kernel, False),
        (shape(2, 128), ext, strip, strip),
        (both, up, down, frame, oh, onehot, weight, supply, head),
        "source2",
        limit=24,
    )
    ra, rb, ca, cb = halo_exchange((head, rhs), sa, sb, 2)
    out, head, rhs = call(
        relax_last,
        (shape(ROWS, COLS), ext, ext),
        (ra, rb, ca, cb, head, rhs, inv),
        "relax2",
        scratch=[pltpu.VMEM((TILES + 1, EXT, 128), F32), pltpu.VMEM((128, ROWS), F32)],
        aliases={4: 1, 5: 2},
    )
    return out, section.reshape(REACH)


def solution(mesh):
    placed = (
        P("row", "col"),
        P("row", "col"),
        P("row", "col"),
        P(("row", "col")),
        P(("row", "col"), None),
        P(("row", "col"), None),
        P(("row", "col")),
        P(("row", "col")),
        P(("row", "col")),
        P(("row", "col")),
        P(),
    )
    return jax.shard_map(
        body,
        mesh=mesh,
        in_specs=placed,
        out_specs=(P("row", "col"), P(("row", "col"))),
        check_vma=False,
    )
```

time: 266 us -> 85.7 us (0.32)
  the two profiles are of different devices: /device:TPU:99 before, /device:TPU:1 now
where the time goes in v1:
time: 85.7 us; the launch traced here: 85.4 us
  Pallas kernels  33.4 us (39%)
  starting transfers between devices  26.5 us (31%)
  waiting for transfers between devices  15.7 us (18%)
  local copies, waits for them, and re-layouts  8.97 us (10%)
    pallas_call x10, Pallas kernels, call(): pl.pallas_call(kernel, out_shape=outs, in_specs=[spec(pltpu.SMEM) if k in...  33.4 us
    ppermute x10, starting transfers between devices, swap(): return lax.ppermute(x, axis, pairs)  20.1 us
    ppermute x10, waiting for transfers between devices, swap(): return lax.ppermute(x, axis, pairs)  11.9 us
    unnamed x24, local copies, waits for them, and re-layouts  8.96 us
    ppermute x4, starting transfers between devices, shift(): return lax.ppermute(x, axis, [(k, (k + by) % n) for k in range(n)])  6.46 us
    ppermute x4, waiting for transfers between devices, shift(): return lax.ppermute(x, axis, [(k, (k + by) % n) for k in range(n)])  3.8 us
  transfers between devices with their start and end apart: 14, of which 10 were waited for; matrix products, arithmetic and copies ran while one was open for 0% of the time, Pallas kernels for 4%

profile of v1, /device:TPU:1, one launch (start us, length us, event | category | flops | bytes accessed | tf_op | source)
XLA Modules:
  0.0 85.4 jit_solution(656831308585588747)
XLA Ops:
  0.7 1.4 %copy-done = f32[384,1024]{1,0:T(8,128)S(1)} copy-done((f32[384,1024]{1,0:T(8,128)S(1)}, f32[384,1024]{1,0:T(8,128)}, u32[]{:S(2)}) %copy-start) | copy-done | bytes 1572888
  2.1 1.0 %copy-done.3 = s32[1024,128]{1,0:T(8,128)S(1)} copy-done((s32[1024,128]{1,0:T(8,128)S(1)}, s32[1024,128]{1,0:T(8,128)}, u32[]{:S(2)}) %copy-start.3) | copy-done | bytes 524312
  3.1 1.0 %copy-done.4 = f32[1024,128]{1,0:T(8,128)S(1)} copy-done((f32[1024,128]{1,0:T(8,128)S(1)}, f32[1024,128]{1,0:T(8,128)}, u32[]{:S(2)}) %copy-start.4) | copy-done | bytes 524312
  8.2 3.9 %prep.1 = (f32[8,1024]{1,0:T(8,128)S(1)}, bf16[1024,1024]{1,0:T(8,128)(2,1)S(1)}, f32[1024,128]{1,0:T(8,128)S(1)}, f32[9,416,128]{2,1,0:T(8,128)S(1)}) custom-call(f32[384,1024]{1,0:T(8,128)S(1)} %copy-done, s32[1024]{0:T(1024)S(1)} %copy-done.5, s32[8,128]{1,0:T(8,128)S(1)} %bitcast.7, s32[1024,128]{1,0:T(8,128)S(1)} %copy-done.3, ...), custom_call_target="tpu_custom_call" | custom-call | flops 10000000 | bytes 4000000 | tf_op jit(solution)/shard_map/prep/pallas_call | solution.py:308
  12.1 3.3 %collective-permute-start = (f32[8,1024]{1,0:T(8,128)S(1)}, f32[8,1024]{1,0:T(8,128)S(1)}, u32[]{:S(2)}, u32[]{:S(2)}) collective-permute-start(f32[8,1024]{1,0:T(8,128)S(1)} %get-tuple-element.29), channel_id=1, source_target_pairs={{0,1},{1,0},{2,3},{3,2},{4,5},{5,4},{6,7},{7,6},{8,9},{9,8},{10,11... | collective-permute-start | bytes 98312 | tf_op jit(solution)/shard_map/ppermute | solution.py:327
  16.3 3.9 %collective-permute-start.2 = (f32[8,512]{1,0:T(8,128)S(1)}, f32[8,512]{1,0:T(8,128)S(1)}, u32[]{:S(2)}, u32[]{:S(2)}) collective-permute-start(f32[8,512]{1,0:T(8,128)S(1)} %get-tuple-element.58), channel_id=1, source_target_pairs={{0,14},{1,15},{2,0},{3,1},{4,2},{5,3},{6,4},{7,5},{8,6},{9,7},{10,... | collective-permute-start | bytes 49160 | tf_op jit(solution)/shard_map/ppermute | solution.py:332
  20.3 1.4 %copy-done.2 = f32[384,1024]{1,0:T(8,128)S(1)} copy-done((f32[384,1024]{1,0:T(8,128)S(1)}, f32[384,1024]{1,0:T(8,128)}, u32[]{:S(2)}) %copy-start.2) | copy-done | bytes 1572888
  21.7 2.7 %fields.1 = (bf16[3072,1024]{1,0:T(8,128)(2,1)S(1)}, f32[9,416,128]{2,1,0:T(8,128)S(1)}, f32[8,384,128]{2,1,0:T(8,128)S(1)}) custom-call(f32[9,416,128]{2,1,0:T(8,128)S(1)} %get-tuple-element.31.headx.refs_8_.refs_0_.head_in, f32[384,1024]{1,0:T(8,128)S(1)} %copy-done.1, f32[384,1024]{1,0:T(8,128)S(1)} %copy-done.2, s32[8,128]{1,0:T(8,128)S(1)} %bitcast.6, ...), custom_call_target="tpu_custom_call" | custom-call | flops 10000000 | bytes 4000000 | tf_op jit(solution)/shard_map/fields/pallas_call | solution.py:308
  24.4 3.7 %source1.1 = (f32[8,1024]{1,0:T(8,128)S(1)}, f32[2,128]{1,0:T(2,128)}, f32[9,416,128]{2,1,0:T(8,128)S(1)}, f32[8,16,128]{2,1,0:T(8,128)S(1)}, f32[8,16,128]{2,1,0:T(8,128)S(1)}) custom-call(f32[8,1024]{1,0:T(8,128)S(1)} %add.6.refs_0_, f32[8,512]{1,0:T(8,128)S(1)} %collective-permute-done.1.refs_1_, f32[8,512]{1,0:T(8,128)S(1)} %collective-permute-done.2.refs_2_, ...), custom_call_target="tpu_custom_call" | custom-call | flops 10000000 | bytes 4000000 | tf_op jit(solution)/shard_map/source1/pallas_call | solution.py:308
  28.1 1.3 %collective-permute-start.3 = (f32[8,16,128]{2,1,0:T(8,128)S(1)}, f32[8,16,128]{2,1,0:T(8,128)S(1)}, u32[]{:S(2)}, u32[]{:S(2)}) collective-permute-start(f32[8,16,128]{2,1,0:T(8,128)S(1)} %get-tuple-element.36), channel_id=1, source_target_pairs={{0,16},{16,0},{32,48},{48,32},{64,80},{80,64},{96,112},{112,96},{1... | collective-permute-start | bytes 196616 | tf_op jit(solution)/shard_map/ppermute | solution.py:327
  29.4 4.1 %collective-permute-start.4 = (f32[8,16,128]{2,1,0:T(8,128)S(1)}, f32[8,16,128]{2,1,0:T(8,128)S(1)}, u32[]{:S(2)}, u32[]{:S(2)}) collective-permute-start(f32[8,16,128]{2,1,0:T(8,128)S(1)} %get-tuple-element.37), channel_id=1, source_target_pairs={{0,240},{16,32},{32,16},{48,64},{64,48},{80,96},{96,80},{112,128},... | collective-permute-start | bytes 196616 | tf_op jit(solution)/shard_map/ppermute | solution.py:327
  33.9 2.0 %collective-permute-done.4.rb = f32[8,16,128]{2,1,0:T(8,128)S(1)} collective-permute-done((f32[8,16,128]{2,1,0:T(8,128)S(1)}, f32[8,16,128]{2,1,0:T(8,128)S(1)}, u32[]{:S(2)}, u32[]{:S(2)}) %collective-permute-start.4) | collective-permute-done | bytes 65568 | tf_op jit(solution)/shard_map/ppermute | solution.py:327
  36.0 2.9 %collective-permute-start.5 = (f32[16,512]{1,0:T(8,128)S(1)}, f32[16,512]{1,0:T(8,128)S(1)}, u32[]{:S(2)}, u32[]{:S(2)}) collective-permute-start(f32[16,512]{1,0:T(8,128)S(1)} %get-tuple-element.41), channel_id=1, source_target_pairs={{0,1},{1,0},{2,3},{3,2},{4,5},{5,4},{6,7},{7,6},{8,9},{9,8},{10,11... | collective-permute-start | bytes 98312 | tf_op jit(solution)/shard_map/ppermute | solution.py:327
  39.7 2.5 %collective-permute-done.6.cb = f32[16,512]{1,0:T(8,128)S(1)} collective-permute-done((f32[16,512]{1,0:T(8,128)S(1)}, f32[16,512]{1,0:T(8,128)S(1)}, u32[]{:S(2)}, u32[]{:S(2)}) %collective-permute-start.6) | collective-permute-done | bytes 32800 | tf_op jit(solution)/shard_map/ppermute | solution.py:327
  42.2 10.2 %relax1.1 = (f32[9,416,128]{2,1,0:T(8,128)S(1)}, f32[9,416,128]{2,1,0:T(8,128)S(1)}, f32[9,416,128]{2,1,0:T(8,128)S(1)}, f32[8,1024]{1,0:T(8,128)S(1)}) custom-call(f32[8,16,128]{2,1,0:T(8,128)S(1)} %collective-permute-done.3.ra, f32[8,16,128]{2,1,0:T(8,128)S(1)} %collective-permute-done.4.rb, ...), custom_call_target="tpu_custom_call", output_to_operand_aliasing={{0}: (4, {}), {1}: (5, {}), {2}: (6, {})} | custom-call | flops 10000000 | bytes 4000000 | tf_op jit(solution)/shard_map/relax1/pallas_call | solution.py:308
  52.4 1.6 %collective-permute-start.7 = (f32[8,1024]{1,0:T(8,128)S(1)}, f32[8,1024]{1,0:T(8,128)S(1)}, u32[]{:S(2)}, u32[]{:S(2)}) collective-permute-start(f32[8,1024]{1,0:T(8,128)S(1)} %get-tuple-element.43), channel_id=1, source_target_pairs={{0,1},{1,0},{2,3},{3,2},{4,5},{5,4},{6,7},{7,6},{8,9},{9,8},{10,11... | collective-permute-start | bytes 98312 | tf_op jit(solution)/shard_map/ppermute | solution.py:327
  54.9 2.5 %collective-permute-start.9 = (f32[8,512]{1,0:T(8,128)S(1)}, f32[8,512]{1,0:T(8,128)S(1)}, u32[]{:S(2)}, u32[]{:S(2)}) collective-permute-start(f32[8,512]{1,0:T(8,128)S(1)} %get-tuple-element.56), channel_id=1, source_target_pairs={{0,14},{1,15},{2,0},{3,1},{4,2},{5,3},{6,4},{7,5},{8,6},{9,7},{10,... | collective-permute-start | bytes 49160 | tf_op jit(solution)/shard_map/ppermute | solution.py:332
  58.2 2.9 %collective-permute-done.8.refs_1_ = f32[8,512]{1,0:T(8,128)S(1)} collective-permute-done((f32[8,512]{1,0:T(8,128)S(1)}, f32[8,512]{1,0:T(8,128)S(1)}, u32[]{:S(2)}, u32[]{:S(2)}) %collective-permute-start.8) | collective-permute-done | bytes 16416 | tf_op jit(solution)/shard_map/ppermute | solution.py:332
  61.2 3.7 %source2.1 = (f32[2,128]{1,0:T(2,128)}, f32[9,416,128]{2,1,0:T(8,128)S(1)}, f32[8,8,128]{2,1,0:T(8,128)S(1)}, f32[8,8,128]{2,1,0:T(8,128)S(1)}) custom-call(f32[8,1024]{1,0:T(8,128)S(1)} %add.7.refs_0_, f32[8,512]{1,0:T(8,128)S(1)} %collective-permute-done.8.refs_1_, f32[8,512]{1,0:T(8,128)S(1)} %collective-permute-done.9.refs_2_, ...), custom_call_target="tpu_custom_call" | custom-call | flops 10000000 | bytes 4000000 | tf_op jit(solution)/shard_map/source2/pallas_call | solution.py:308
  64.8 4.1 %collective-permute-start.11 = (f32[8,8,128]{2,1,0:T(8,128)S(1)}, f32[8,8,128]{2,1,0:T(8,128)S(1)}, u32[]{:S(2)}, u32[]{:S(2)}) collective-permute-start(f32[8,8,128]{2,1,0:T(8,128)S(1)} %get-tuple-element.47), channel_id=1, source_target_pairs={{0,240},{16,32},{32,16},{48,64},{64,48},{80,96},{96,80},{112,128},... | collective-permute-start | bytes 98312 | tf_op jit(solution)/shard_map/ppermute | solution.py:327
  69.2 1.7 %collective-permute-done.11.rb = f32[8,8,128]{2,1,0:T(8,128)S(1)} collective-permute-done((f32[8,8,128]{2,1,0:T(8,128)S(1)}, f32[8,8,128]{2,1,0:T(8,128)S(1)}, u32[]{:S(2)}, u32[]{:S(2)}) %collective-permute-start.11) | collective-permute-done | bytes 32800 | tf_op jit(solution)/shard_map/ppermute | solution.py:327
  71.0 2.8 %collective-permute-start.12 = (f32[8,512]{1,0:T(8,128)S(1)}, f32[8,512]{1,0:T(8,128)S(1)}, u32[]{:S(2)}, u32[]{:S(2)}) collective-permute-start(f32[8,512]{1,0:T(8,128)S(1)} %get-tuple-element.51), channel_id=1, source_target_pairs={{0,1},{1,0},{2,3},{3,2},{4,5},{5,4},{6,7},{7,6},{8,9},{9,8},{10,11... | collective-permute-start | bytes 49160 | tf_op jit(solution)/shard_map/ppermute | solution.py:327
  74.7 2.3 %collective-permute-done.13.cb = f32[8,512]{1,0:T(8,128)S(1)} collective-permute-done((f32[8,512]{1,0:T(8,128)S(1)}, f32[8,512]{1,0:T(8,128)S(1)}, u32[]{:S(2)}, u32[]{:S(2)}) %collective-permute-start.13) | collective-permute-done | bytes 16416 | tf_op jit(solution)/shard_map/ppermute | solution.py:327
  77.0 8.3 %relax2.1 = (f32[384,1024]{1,0:T(8,128)}, f32[9,416,128]{2,1,0:T(8,128)S(1)}, f32[9,416,128]{2,1,0:T(8,128)S(1)}) custom-call(f32[8,8,128]{2,1,0:T(8,128)S(1)} %collective-permute-done.10.ra, f32[8,8,128]{2,1,0:T(8,128)S(1)} %collective-permute-done.11.rb, f32[8,512]{1,0:T(8,128)S(1)} %collective-permute-done.12.ca, ...), custom_call_target="tpu_custom_call", output_to_operand_aliasing={{1}: (4, {}), {2}: (5, {})} | custom-call | flops 10000000 | bytes 4000000 | tf_op jit(solution)/shard_map/relax2/pallas_call | solution.py:308
  (42 shorter events, 9.2 us)
Async XLA Ops:
  0.6 19.6 %copy-start.6 = (s32[1024]{0:T(1024)S(1)}, s32[1024]{0:T(1024)}, u32[]{:S(2)}) copy-start(s32[1024]{0:T(1024)} %blk.3) | copy-start | bytes 12292
  0.6 1.4 %copy-start = (f32[384,1024]{1,0:T(8,128)S(1)}, f32[384,1024]{1,0:T(8,128)}, u32[]{:S(2)}) copy-start(f32[384,1024]{1,0:T(8,128)} %head.1) | copy-start | bytes 4718596
  2.1 1.0 %copy-start.3 = (s32[1024,128]{1,0:T(8,128)S(1)}, s32[1024,128]{1,0:T(8,128)}, u32[]{:S(2)}) copy-start(s32[1024,128]{1,0:T(8,128)} %mask.1) | copy-start | bytes 1572868
  3.1 1.0 %copy-start.4 = (f32[1024,128]{1,0:T(8,128)S(1)}, f32[1024,128]{1,0:T(8,128)}, u32[]{:S(2)}) copy-start(f32[1024,128]{1,0:T(8,128)} %condu.1) | copy-start | bytes 1572868
  4.1 0.7 copy-start.5
  4.8 0.7 copy-start.7
  5.5 0.7 copy-start.8
  6.2 0.7 copy-start.9
  8.2 12.0 %copy-start.1 = (f32[384,1024]{1,0:T(8,128)S(1)}, f32[384,1024]{1,0:T(8,128)}, u32[]{:S(2)}) copy-start(f32[384,1024]{1,0:T(8,128)} %recharge.1) | copy-start | bytes 4718596
  12.1 4.1 %collective-permute-start = (f32[8,1024]{1,0:T(8,128)S(1)}, f32[8,1024]{1,0:T(8,128)S(1)}, u32[]{:S(2)}, u32[]{:S(2)}) collective-permute-start(f32[8,1024]{1,0:T(8,128)S(1)} %get-tuple-element.29), channel_id=1, source_target_pairs={{0,1},{1,0},{2,3},{3,2},{4,5},{5,4},{6,7},{7,6},{8,9},{9,8},{10,11... | collective-permute-start | bytes 98312 | tf_op jit(solution)/shard_map/ppermute | solution.py:327
  16.3 8.1 %collective-permute-start.2 = (f32[8,512]{1,0:T(8,128)S(1)}, f32[8,512]{1,0:T(8,128)S(1)}, u32[]{:S(2)}, u32[]{:S(2)}) collective-permute-start(f32[8,512]{1,0:T(8,128)S(1)} %get-tuple-element.58), channel_id=1, source_target_pairs={{0,14},{1,15},{2,0},{3,1},{4,2},{5,3},{6,4},{7,5},{8,6},{9,7},{10,... | collective-permute-start | bytes 49160 | tf_op jit(solution)/shard_map/ppermute | solution.py:332
  20.2 4.2 %collective-permute-start.1 = (f32[8,512]{1,0:T(8,128)S(1)}, f32[8,512]{1,0:T(8,128)S(1)}, u32[]{:S(2)}, u32[]{:S(2)}) collective-permute-start(f32[8,512]{1,0:T(8,128)S(1)} %get-tuple-element.59), channel_id=1, source_target_pairs={{0,2},{1,3},{2,4},{3,5},{4,6},{5,7},{6,8},{7,9},{8,10},{9,11},{10,... | collective-permute-start | bytes 49160 | tf_op jit(solution)/shard_map/ppermute | solution.py:332
  20.2 1.4 %copy-start.2 = (f32[384,1024]{1,0:T(8,128)S(1)}, f32[384,1024]{1,0:T(8,128)}, u32[]{:S(2)}) copy-start(f32[384,1024]{1,0:T(8,128)} %storage.1) | copy-start | bytes 4718596
  28.1 5.7 %collective-permute-start.3 = (f32[8,16,128]{2,1,0:T(8,128)S(1)}, f32[8,16,128]{2,1,0:T(8,128)S(1)}, u32[]{:S(2)}, u32[]{:S(2)}) collective-permute-start(f32[8,16,128]{2,1,0:T(8,128)S(1)} %get-tuple-element.36), channel_id=1, source_target_pairs={{0,16},{16,0},{32,48},{48,32},{64,80},{80,64},{96,112},{112,96},{1... | collective-permute-start | bytes 196616 | tf_op jit(solution)/shard_map/ppermute | solution.py:327
  29.4 6.4 %collective-permute-start.4 = (f32[8,16,128]{2,1,0:T(8,128)S(1)}, f32[8,16,128]{2,1,0:T(8,128)S(1)}, u32[]{:S(2)}, u32[]{:S(2)}) collective-permute-start(f32[8,16,128]{2,1,0:T(8,128)S(1)} %get-tuple-element.37), channel_id=1, source_target_pairs={{0,240},{16,32},{32,16},{48,64},{64,48},{80,96},{96,80},{112,128},... | collective-permute-start | bytes 196616 | tf_op jit(solution)/shard_map/ppermute | solution.py:327
  36.0 3.8 %collective-permute-start.5 = (f32[16,512]{1,0:T(8,128)S(1)}, f32[16,512]{1,0:T(8,128)S(1)}, u32[]{:S(2)}, u32[]{:S(2)}) collective-permute-start(f32[16,512]{1,0:T(8,128)S(1)} %get-tuple-element.41), channel_id=1, source_target_pairs={{0,1},{1,0},{2,3},{3,2},{4,5},{5,4},{6,7},{7,6},{8,9},{9,8},{10,11... | collective-permute-start | bytes 98312 | tf_op jit(solution)/shard_map/ppermute | solution.py:327
  38.9 3.3 %collective-permute-start.6 = (f32[16,512]{1,0:T(8,128)S(1)}, f32[16,512]{1,0:T(8,128)S(1)}, u32[]{:S(2)}, u32[]{:S(2)}) collective-permute-start(f32[16,512]{1,0:T(8,128)S(1)} %get-tuple-element.42), channel_id=1, source_target_pairs={{0,15},{1,2},{2,1},{3,4},{4,3},{5,6},{6,5},{7,8},{8,7},{9,10},{10,... | collective-permute-start | bytes 98312 | tf_op jit(solution)/shard_map/ppermute | solution.py:327
  52.4 2.4 %collective-permute-start.7 = (f32[8,1024]{1,0:T(8,128)S(1)}, f32[8,1024]{1,0:T(8,128)S(1)}, u32[]{:S(2)}, u32[]{:S(2)}) collective-permute-start(f32[8,1024]{1,0:T(8,128)S(1)} %get-tuple-element.43), channel_id=1, source_target_pairs={{0,1},{1,0},{2,3},{3,2},{4,5},{5,4},{6,7},{7,6},{8,9},{9,8},{10,11... | collective-permute-start | bytes 98312 | tf_op jit(solution)/shard_map/ppermute | solution.py:327
  54.9 3.4 %collective-permute-start.9 = (f32[8,512]{1,0:T(8,128)S(1)}, f32[8,512]{1,0:T(8,128)S(1)}, u32[]{:S(2)}, u32[]{:S(2)}) collective-permute-start(f32[8,512]{1,0:T(8,128)S(1)} %get-tuple-element.56), channel_id=1, source_target_pairs={{0,14},{1,15},{2,0},{3,1},{4,2},{5,3},{6,4},{7,5},{8,6},{9,7},{10,... | collective-permute-start | bytes 49160 | tf_op jit(solution)/shard_map/ppermute | solution.py:332
  57.4 3.8 %collective-permute-start.8 = (f32[8,512]{1,0:T(8,128)S(1)}, f32[8,512]{1,0:T(8,128)S(1)}, u32[]{:S(2)}, u32[]{:S(2)}) collective-permute-start(f32[8,512]{1,0:T(8,128)S(1)} %get-tuple-element.57), channel_id=1, source_target_pairs={{0,2},{1,3},{2,4},{3,5},{4,6},{5,7},{6,8},{7,9},{8,10},{9,11},{10,... | collective-permute-start | bytes 49160 | tf_op jit(solution)/shard_map/ppermute | solution.py:332
  64.8 4.4 %collective-permute-start.10 = (f32[8,8,128]{2,1,0:T(8,128)S(1)}, f32[8,8,128]{2,1,0:T(8,128)S(1)}, u32[]{:S(2)}, u32[]{:S(2)}) collective-permute-start(f32[8,8,128]{2,1,0:T(8,128)S(1)} %get-tuple-element.46), channel_id=1, source_target_pairs={{0,16},{16,0},{32,48},{48,32},{64,80},{80,64},{96,112},{112,96},{1... | collective-permute-start | bytes 98312 | tf_op jit(solution)/shard_map/ppermute | solution.py:327
  64.8 6.1 %collective-permute-start.11 = (f32[8,8,128]{2,1,0:T(8,128)S(1)}, f32[8,8,128]{2,1,0:T(8,128)S(1)}, u32[]{:S(2)}, u32[]{:S(2)}) collective-permute-start(f32[8,8,128]{2,1,0:T(8,128)S(1)} %get-tuple-element.47), channel_id=1, source_target_pairs={{0,240},{16,32},{32,16},{48,64},{64,48},{80,96},{96,80},{112,128},... | collective-permute-start | bytes 98312 | tf_op jit(solution)/shard_map/ppermute | solution.py:327
  71.0 3.7 %collective-permute-start.12 = (f32[8,512]{1,0:T(8,128)S(1)}, f32[8,512]{1,0:T(8,128)S(1)}, u32[]{:S(2)}, u32[]{:S(2)}) collective-permute-start(f32[8,512]{1,0:T(8,128)S(1)} %get-tuple-element.51), channel_id=1, source_target_pairs={{0,1},{1,0},{2,3},{3,2},{4,5},{5,4},{6,7},{7,6},{8,9},{9,8},{10,11... | collective-permute-start | bytes 49160 | tf_op jit(solution)/shard_map/ppermute | solution.py:327
  73.9 3.2 %collective-permute-start.13 = (f32[8,512]{1,0:T(8,128)S(1)}, f32[8,512]{1,0:T(8,128)S(1)}, u32[]{:S(2)}, u32[]{:S(2)}) collective-permute-start(f32[8,512]{1,0:T(8,128)S(1)} %get-tuple-element.52), channel_id=1, source_target_pairs={{0,15},{1,2},{2,1},{3,4},{4,3},{5,6},{6,5},{7,8},{8,7},{9,10},{10,... | collective-permute-start | bytes 49160 | tf_op jit(solution)/shard_map/ppermute | solution.py:327
  (2 other events, 1.3 us)

commit v2 on v1

v2 whole, which is shorter than its diff:
```python
import functools

import jax
import jax.numpy as jnp
from jax import lax
from jax.experimental import pallas as pl
from jax.experimental.pallas import tpu as pltpu
from jax.sharding import PartitionSpec as P

NETS = 64
SWEEPS = 4
ROWS, COLS = 384, 1024
TILES = COLS // 128
WIDE = TILES + 1
SEG = 1024
REACH = 256
FRAME = 4 * REACH
OFF = 8
EXT = ROWS + 2 * OFF
H = 4
DEPTH = (4, 3, 3)
UNROLL = 12
F32 = jnp.float32
BF16 = jnp.bfloat16
I32 = jnp.int32


def split2(x):
    hi = x.astype(BF16)
    lo = (x - hi.astype(F32)).astype(BF16)
    return hi, lo


def both_halves(x):
    return jnp.concatenate(split2(x), axis=1)


def column_of(row):
    return jnp.broadcast_to(row, (128, 128)).T


def tile_rows(c, start, size):
    return slice(c * EXT + OFF + start, c * EXT + OFF + start + size)


def gather_rows(head, index, out):
    def group(k, carry):
        for u in range(128):
            out[pl.ds(k * 128 + u, 1), :] = head[pl.ds(index[k, u], 1), :]
        return carry

    lax.fori_loop(0, SEG // 128, group, 0)


def row_sums(get, lhs, first):
    for k in range(SEG // 128):
        at = slice(k * 128, (k + 1) * 128)
        row = jnp.sum(get(at).T, axis=0, keepdims=True)
        hi = row.astype(BF16).astype(F32)
        mid = (row - hi).astype(BF16).astype(F32)
        lhs[first : first + 1, at] = hi
        lhs[first + 1 : first + 2, at] = mid
        lhs[first + 2 : first + 3, at] = row - hi - mid


def prep(
    head, blk, reach, mask, condu, bed, sec0, net, infl,
    part, oh, weight, headx, index8,
    hs, lhs, blk_v, reach_v, mask_v, cond_v, bed_v, sec0_v, net_v, infl_s, index_s, sems,
):
    moves = [
        pltpu.make_async_copy(blk, blk_v, sems.at[0]),
        pltpu.make_async_copy(reach, reach_v, sems.at[1]),
        pltpu.make_async_copy(mask, mask_v, sems.at[2]),
        pltpu.make_async_copy(condu, cond_v, sems.at[3]),
        pltpu.make_async_copy(bed, bed_v, sems.at[4]),
        pltpu.make_async_copy(sec0, sec0_v, sems.at[5]),
        pltpu.make_async_copy(net, net_v, sems.at[6]),
        pltpu.make_async_copy(infl, infl_s, sems.at[7]),
    ]
    heads = [
        pltpu.make_async_copy(
            head.at[:, c * 128 : (c + 1) * 128], headx.at[tile_rows(c, 0, ROWS), :], sems.at[8 + c]
        )
        for c in range(TILES)
    ]
    for m in moves + heads:
        m.start()
    j = lax.axis_index("col")
    base = (j // 2) * 2 - 1
    for c in range(WIDE):
        headx[c * EXT : c * EXT + OFF, :] = jnp.zeros((OFF, 128), F32)
        headx[(c + 1) * EXT - OFF : (c + 1) * EXT, :] = jnp.zeros((OFF, 128), F32)
    headx[tile_rows(TILES, 0, ROWS), :] = jnp.zeros((ROWS, 128), F32)
    lhs[...] = jnp.zeros_like(lhs)
    part[...] = jnp.zeros_like(part)
    moves[0].wait()
    blocks = blk_v[...]
    index8[...] = (blocks & 7) * EXT + (blocks >> 3) + OFF
    listed = pltpu.make_async_copy(index8, index_s, sems.at[16])
    listed.start()
    moves[1].wait()
    reach8 = reach_v[...]
    slot8 = (((reach8 // REACH) % 16 - base + 16) % 16) * REACH + reach8 % REACH
    lane = lax.broadcasted_iota(I32, (128, 128), 1)
    for k in range(SEG // 128):
        slots = column_of(slot8[k : k + 1, :])
        for q in range(FRAME // 128):
            oh[k * 128 : (k + 1) * 128, q * 128 : (q + 1) * 128] = jnp.where(
                slots == lane + q * 128, 1.0, 0.0
            ).astype(BF16)
    for m in moves[2:]:
        m.wait()
    nets = net_v[...]
    inflow = jnp.zeros(nets.shape, F32)
    for n in range(NETS):
        inflow = jnp.where(nets == n, infl_s[n], inflow)
    values = (bed_v[...], inflow, sec0_v[...])
    odd = j % 2
    for w in range(2):
        keep = odd == w
        for t in range(2):
            at = (1 + w) * REACH + t * 128
            for q, v in enumerate(values):
                part[2 + q : 3 + q, at : at + 128] = jnp.where(keep, v[t : t + 1, :], 0.0)
    weight[...] = mask_v[...].astype(F32) * cond_v[...]
    row_sums(lambda at: weight[at, :], lhs, 3)
    listed.wait()
    for m in heads:
        m.wait()
    gather_rows(headx, index_s, hs)
    row_sums(lambda at: weight[at, :] * hs[at, :], lhs, 0)
    sums = jnp.dot(lhs[...].astype(BF16), oh[...], preferred_element_type=F32)
    part[0:1, :] = sums[0:1] + sums[1:2] + sums[2:3]
    part[1:2, :] = sums[3:4] + sums[4:5] + sums[5:6]


def fields(headx, recharge, storage, index8, weight, onehot, inv, supply, rech_v, store_v, sems):
    moves = [
        pltpu.make_async_copy(recharge, rech_v, sems.at[0]),
        pltpu.make_async_copy(storage, store_v, sems.at[1]),
    ]
    for m in moves:
        m.start()
    target = index8[...]
    iota = lax.broadcasted_iota(I32, (ROWS, 128), 0)
    for k in range(SEG // 128):
        row = jnp.broadcast_to(target[k : k + 1, :], (ROWS, 128))
        for c in range(TILES):
            onehot[c * ROWS : (c + 1) * ROWS, k * 128 : (k + 1) * 128] = jnp.where(
                row == iota + (c * EXT + OFF), 1.0, 0.0
            ).astype(BF16)
    both = both_halves(weight[...])
    inv[TILES] = jnp.zeros((ROWS, 128), F32)
    for m in moves:
        m.wait()
    for c in range(TILES):
        at = slice(c * 128, (c + 1) * 128)
        got = jnp.dot(onehot[c * ROWS : (c + 1) * ROWS, :], both, preferred_element_type=F32)
        cond = got[:, :128] + got[:, 128:]
        store = store_v[:, at]
        inv[c] = 1.0 / (4.0 + store + cond)
        supply[c] = store * headx[tile_rows(c, 0, ROWS), :] + rech_v[:, at]


def put_columns(left_tile, right_tile, q, ma, mb):
    odd = lax.axis_index("col") % 2 == 1
    for k in range(ROWS // 128):
        at = slice(k * 128, (k + 1) * 128)
        left = left_tile(at).T[0:H, :]
        right = right_tile(at).T[128 - H : 128, :]
        ma[q * H : (q + 1) * H, at] = jnp.where(odd, left, right)
        mb[q * H : (q + 1) * H, at] = jnp.where(odd, right, left)


def columns(first, *refs):
    head = refs[0]
    ma, mb = refs[-2:]
    ma[...] = jnp.zeros_like(ma)
    mb[...] = jnp.zeros_like(mb)
    put_columns(
        lambda at: head[tile_rows(0, at.start, 128), :],
        lambda at: head[tile_rows(TILES - 1, at.start, 128), :],
        0, ma, mb,
    )
    if first:
        inv = refs[1]
        put_columns(lambda at: inv[0, at, :], lambda at: inv[TILES - 1, at, :], 2, ma, mb)


def section_kernel(first, *refs):
    if first:
        own, up, down, oh, onehot, weight, supply, pa, pb, frame, section, mixed, rhs, ma, mb = refs
    else:
        own, up, down, old, oh, onehot, weight, supply, pa, pb, section, mixed, rhs, ma, mb = refs
    j = lax.axis_index("col")
    full = own[...] + jnp.concatenate([up[...], down[...]], axis=1)
    leak = full[0:1]
    if first:
        wsum, bed, inflow, sec = full[1:2], full[2:3], full[3:4], full[4:5]
    else:
        wsum, bed, inflow, sec = (old[q : q + 1, :] for q in (1, 2, 3, 4))
    x = inflow - (sec * wsum - leak)
    soft = jnp.maximum(x, 0.0) + jnp.log1p(jnp.exp(-jnp.abs(x)))
    sec = bed + jnp.sqrt(1.0 + soft) - 1.0
    if first:
        frame[...] = full
        frame[4:5, :] = sec
    odd = j % 2 == 1
    for t in range(2):
        a = REACH + t * 128
        b = 2 * REACH + t * 128
        section[t : t + 1, :] = jnp.where(odd, sec[:, b : b + 128], sec[:, a : a + 128])
    hi, lo = split2(sec)
    wide = jnp.concatenate(
        [jnp.broadcast_to(hi.astype(F32), (128, FRAME)), jnp.broadcast_to(lo.astype(F32), (128, FRAME))], axis=0
    ).astype(BF16)
    got = lax.dot_general(oh[...], wide, (((1,), (1,)), ((), ())), preferred_element_type=F32)
    both = both_halves(weight[...] * (got[:, :128] + got[:, 128:]))
    mixed[...] = both
    ma[...] = pa[...]
    mb[...] = pb[...]
    for c in (0, TILES - 1):
        scatter(c, onehot, both, supply, rhs)
    put_columns(lambda at: rhs[0, at, :], lambda at: rhs[TILES - 1, at, :], 1, ma, mb)


def scatter(c, onehot, both, supply, rhs):
    got = jnp.dot(onehot[c * ROWS : (c + 1) * ROWS, :], both, preferred_element_type=F32)
    rhs[c] = supply[c] + got[:, :128] + got[:, 128:]


def inner_source(onehot, mixed, supply, rhs_in, rhs):
    both = mixed[...]
    for c in range(1, TILES - 1):
        scatter(c, onehot, both, supply, rhs)


def place_columns(first, *refs):
    if first:
        ca, cb, _, _, _, head, rhs, inv, sa, sb, band, wide = refs
        grids = (rhs, inv)
    else:
        ca, cb, _, _, head, rhs, sa, sb, band, wide = refs
        grids = (rhs,)
    i = lax.axis_index("row")
    j = lax.axis_index("col")
    odd = j % 2 == 1
    right = jnp.where(j == 15, 0.0, jnp.where(odd, cb[...], ca[...]))
    left = jnp.where(j == 0, 0.0, jnp.where(odd, ca[...], cb[...]))
    wide[...] = jnp.zeros_like(wide)
    row_odd = i % 2 == 1
    sa[...] = jnp.zeros_like(sa)
    sb[...] = jnp.zeros_like(sb)
    for q in range(1 + len(grids)):
        own = slice(q * H, (q + 1) * H)
        wide[0:H, :] = right[own, :]
        wide[128 - H : 128, :] = left[own, :]
        for k in range(ROWS // 128):
            turned = wide[:, k * 128 : (k + 1) * 128].T
            if q == 0:
                head[tile_rows(TILES, k * 128, 128), :] = turned
            else:
                grids[q - 1][TILES, k * 128 : (k + 1) * 128, :] = turned
        depth = DEPTH[q]
        for c in range(WIDE):
            if q == 0:
                top = head[tile_rows(c, 0, depth), :]
                bottom = head[tile_rows(c, ROWS - depth, depth), :]
            else:
                ref = grids[q - 1]
                top = ref[c, 0:depth, :]
                bottom = ref[c, ROWS - depth : ROWS, :]
            at = strip_rows(c, q, 1 + len(grids))
            sa[at, :] = jnp.where(row_odd, top, bottom)
            sb[at, :] = jnp.where(row_odd, bottom, top)
    for c in range(WIDE):
        band[0, c] = head[tile_rows(c, 0, 8), :]
        band[1, c] = head[tile_rows(c, ROWS - 8, 8), :]


def strip_rows(c, q, count):
    first = c * sum(DEPTH[:count]) + sum(DEPTH[:q])
    return slice(first, first + DEPTH[q])


def halo_rows(ra, rb, q, count, top, bottom):
    i = lax.axis_index("row")
    odd = i % 2 == 1
    for c in range(WIDE):
        at = strip_rows(c, q, count)
        a, b = ra[at, :], rb[at, :]
        top(c, jnp.where(i == 0, 0.0, jnp.where(odd, a, b)))
        bottom(c, jnp.where(i == 15, 0.0, jnp.where(odd, b, a)))


def relax_chunk(src, dst, rhs, inv, spread):
    lane = lax.broadcasted_iota(I32, (8, 128), 1)
    mid = [src(c, 0) for c in range(WIDE)]
    fwd = [pltpu.roll(m, 1, 1) for m in mid]
    bwd = [pltpu.roll(m, 127, 1) for m in mid]
    for c in range(spread):
        left = jnp.where(lane == 0, fwd[c - 1], fwd[c])
        right = jnp.where(lane == 127, bwd[(c + 1) % WIDE], bwd[c])
        total = (src(c, -1) + src(c, 1)) + (left + right) + rhs(c)
        dst(c, total * inv(c))


def sweep(src, dst, rhs, inv):
    def put(c, r, value):
        dst[pl.ds(c * EXT + OFF + r, 8), :] = value

    def group(g, carry):
        for u in range(UNROLL):
            r = g * (8 * UNROLL) + u * 8
            relax_chunk(
                lambda c, d: src[pl.ds(c * EXT + OFF + r + d, 8), :],
                lambda c, value: put(c, r, value),
                lambda c: rhs[c, pl.ds(r, 8), :],
                lambda c: inv[c, pl.ds(r, 8), :],
                WIDE,
            )
        return carry

    lax.fori_loop(0, ROWS // (8 * UNROLL), group, 0)


def sweeps(head, other, rhs, inv):
    for c in range(WIDE):
        other[c * EXT : c * EXT + OFF, :] = jnp.zeros((OFF, 128), F32)
        other[(c + 1) * EXT - OFF : (c + 1) * EXT, :] = jnp.zeros((OFF, 128), F32)
    for _ in range(SWEEPS // 2):
        sweep(head, other, rhs, inv)
        sweep(other, head, rhs, inv)


def inner_relax(head_in, rhs, inv, head, other):
    sweeps(head, other, rhs, inv)


def band_relax(ra, rb, count, band, get_rhs, get_inv, one, two):
    one[...] = jnp.zeros_like(one)
    two[...] = jnp.zeros_like(two)
    for c in range(WIDE):
        one[0, c, 16:24, :] = band[0, c]
        one[1, c, 8:16, :] = band[1, c]

    def top(c, value):
        one[0, c, 16 - H : 16, :] = value

    def bottom(c, value):
        one[1, c, 16 : 16 + H, :] = value

    halo_rows(ra, rb, 0, count, top, bottom)
    src, dst = one, two
    for _ in range(SWEEPS):
        for side in range(2):
            for t in range(2):
                r = 8 + t * 8

                def put(c, value):
                    dst[side, c, r : r + 8, :] = value

                relax_chunk(
                    lambda c, d: src[side, c, r + d : r + d + 8, :],
                    put,
                    lambda c: get_rhs(side, c, t),
                    lambda c: get_inv(side, c, t),
                    WIDE,
                )
        src, dst = dst, src
    return one


def halo_or_own(ref, spare):
    def get(side, c, t):
        if side == 0:
            return ref[c, 0:8, :] if t == 1 else spare[0, c]
        return ref[c, ROWS - 8 : ROWS, :] if t == 0 else spare[1, c]

    return get


def fill_spare(ra, rb, q, count, spare):
    spare[...] = jnp.zeros_like(spare)

    def top(c, value):
        spare[0, c, 8 - DEPTH[q] : 8, :] = value

    def bottom(c, value):
        spare[1, c, 0 : DEPTH[q], :] = value

    halo_rows(ra, rb, q, count, top, bottom)


def finish_first(
    ra, rb, band, head_in, rhs, inv, index8, weight, oh, head, rim, part, one, two, hs, lhs, spare, index_s, sem
):
    listed = pltpu.make_async_copy(index8, index_s, sem)
    listed.start()
    fill_spare(ra, rb, 1, 3, spare)
    fill_spare(ra, rb, 2, 3, rim)
    done = band_relax(ra, rb, 3, band, halo_or_own(rhs, spare), halo_or_own(inv, rim), one, two)
    for c in range(TILES):
        head[tile_rows(c, 0, H), :] = done[0, c, 16 : 16 + H, :]
        head[tile_rows(c, ROWS - H, H), :] = done[1, c, 16 - H : 16, :]
    listed.wait()
    lhs[...] = jnp.zeros_like(lhs)
    gather_rows(head, index_s, hs)
    row_sums(lambda at: weight[at, :] * hs[at, :], lhs, 0)
    sums = jnp.dot(lhs[...].astype(BF16), oh[...], preferred_element_type=F32)
    part[...] = jnp.zeros_like(part)
    part[0:1, :] = sums[0:1] + sums[1:2] + sums[2:3]


def finish_last(ra, rb, band, head, rhs, inv, rim, out, one, two, spare, edge, sems):
    moves = [
        pltpu.make_async_copy(
            head.at[tile_rows(c, 8, ROWS - 16), :], out.at[8 : ROWS - 8, c * 128 : (c + 1) * 128], sems.at[2 + c]
        )
        for c in range(TILES)
    ]
    for m in moves:
        m.start()
    fill_spare(ra, rb, 1, 2, spare)
    done = band_relax(ra, rb, 2, band, halo_or_own(rhs, spare), halo_or_own(inv, rim), one, two)
    for c in range(TILES):
        at = slice(c * 128, (c + 1) * 128)
        edge[0, :, at] = head[tile_rows(c, 0, 8), :]
        edge[1, :, at] = head[tile_rows(c, ROWS - 8, 8), :]
        edge[0, 0:H, at] = done[0, c, 16 : 16 + H, :]
        edge[1, 8 - H : 8, at] = done[1, c, 16 - H : 16, :]
    edges = [
        pltpu.make_async_copy(edge.at[0], out.at[0:8, :], sems.at[0]),
        pltpu.make_async_copy(edge.at[1], out.at[ROWS - 8 : ROWS, :], sems.at[1]),
    ]
    for m in edges:
        m.start()
    for m in moves + edges:
        m.wait()


def shape(*dims, dtype=F32):
    return jax.ShapeDtypeStruct(dims, dtype)


def far(x):
    return pltpu.with_memory_space_constraint(x, pltpu.HBM)


def call(kernel, outs, ins, scratch=(), hbm=(), hbm_out=(), aliases=None, limit=16, flops=10_000_000):
    def at(k, far):
        return pl.BlockSpec(memory_space=pltpu.HBM if k in far else pltpu.VMEM)

    return pl.pallas_call(
        kernel,
        out_shape=outs,
        in_specs=[at(k, hbm) for k in range(len(ins))],
        out_specs=tuple(at(k, hbm_out) for k in range(len(outs))),
        scratch_shapes=list(scratch),
        input_output_aliases=aliases or {},
        compiler_params=pltpu.CompilerParams(vmem_limit_bytes=limit * 2**20),
        cost_estimate=pl.CostEstimate(flops=flops, bytes_accessed=4_000_000, transcendentals=0),
    )(*[far(x) if k in hbm else x for k, x in enumerate(ins)])


def swap(x, axis, which):
    n = lax.axis_size(axis)
    if which == 0:
        pairs = [(k, k ^ 1) for k in range(n)]
    else:
        pairs = [(k, (k + 1) % n if k % 2 else (k - 1) % n) for k in range(n)]
    return lax.ppermute(x, axis, pairs)


def swap_both(a, b, axis):
    b = swap(b, axis, 1)
    a = swap(a, axis, 0)
    return a, b


def shift(x, axis, by):
    n = lax.axis_size(axis)
    return lax.ppermute(x, axis, [(k, (k + by) % n) for k in range(n)])


def exchange_sums(part):
    both = part + swap(part, "col", 0)
    up = shift(both[:, 2 * REACH :], "col", 2)
    down = shift(both[:, : 2 * REACH], "col", -2)
    return both, up, down


EXT_SHAPE = shape(WIDE * EXT, 128)
GRID = shape(WIDE, ROWS, 128)
BAND = shape(2, WIDE, 8, 128)
SEG_ROWS = pltpu.VMEM((SEG, 128), F32)
SUMS = pltpu.VMEM((16, SEG), F32)
OTHER = pltpu.VMEM((WIDE * EXT, 128), F32)
WORK = pltpu.VMEM((2, WIDE, 32, 128), F32)
SPARE = pltpu.VMEM((2, WIDE, 8, 128), F32)
TURN = pltpu.VMEM((128, ROWS), F32)
SMALL = pltpu.SMEM((8, 128), I32)


def sems(n):
    return pltpu.SemaphoreType.DMA((n,))


def body(head0, recharge, storage, seg_block, seg_mask, seg_cond, seg_reach, bed, sec0, net, infl):
    part, oh, weight, head, index8 = call(
        prep,
        (shape(8, FRAME), shape(SEG, FRAME, dtype=BF16), shape(SEG, 128), EXT_SHAPE, shape(8, 128, dtype=I32)),
        (
            head0,
            seg_block.reshape(8, 128),
            seg_reach.reshape(8, 128),
            seg_mask,
            seg_cond,
            bed.reshape(2, 128),
            sec0.reshape(2, 128),
            net.reshape(2, 128),
            infl,
        ),
        scratch=[
            SEG_ROWS,
            SUMS,
            pltpu.VMEM((8, 128), I32),
            pltpu.VMEM((8, 128), I32),
            pltpu.VMEM((SEG, 128), I32),
            SEG_ROWS,
            pltpu.VMEM((2, 128), F32),
            pltpu.VMEM((2, 128), F32),
            pltpu.VMEM((2, 128), I32),
            pltpu.SMEM((NETS,), F32),
            SMALL,
            sems(17),
        ],
        hbm=range(9),
    )
    own, up, down = exchange_sums(part)
    onehot, inv, supply = call(
        fields,
        (shape(TILES * ROWS, SEG, dtype=BF16), GRID, shape(TILES, ROWS, 128)),
        (head, recharge, storage, index8, weight),
        scratch=[pltpu.VMEM((ROWS, COLS), F32), pltpu.VMEM((ROWS, COLS), F32), sems(2)],
        hbm=(1, 2),
    )
    strip = shape(16, ROWS)
    pa, pb = call(functools.partial(columns, True), (strip, strip), (head, inv))
    mixed_shape = shape(SEG, 256, dtype=BF16)
    frame, section, mixed, rhs, ma, mb = call(
        functools.partial(section_kernel, True),
        (shape(8, FRAME), shape(2, 128), mixed_shape, GRID, strip, strip),
        (own, up, down, oh, onehot, weight, supply, pa, pb),
    )
    ca, cb = swap_both(ma, mb, "col")
    (rhs,) = call(inner_source, (GRID,), (onehot, mixed, supply, rhs), aliases={3: 0})
    rows = shape(96, 128)
    head, rhs, inv, sa, sb, band = call(
        functools.partial(place_columns, True),
        (EXT_SHAPE, GRID, GRID, rows, rows, BAND),
        (ca, cb, head, rhs, inv),
        scratch=[TURN],
        aliases={2: 0, 3: 1, 4: 2},
    )
    ra, rb = swap_both(sa, sb, "row")
    (head,) = call(inner_relax, (EXT_SHAPE,), (head, rhs, inv), scratch=[OTHER], aliases={0: 0})
    head, rim, part = call(
        finish_first,
        (EXT_SHAPE, BAND, shape(8, FRAME)),
        (ra, rb, band, head, rhs, inv, index8, weight, oh),
        scratch=[WORK, WORK, SEG_ROWS, SUMS, SPARE, SMALL, pltpu.SemaphoreType.DMA],
        aliases={3: 0},
    )
    own, up, down = exchange_sums(part)
    strip = shape(8, ROWS)
    pa, pb = call(functools.partial(columns, False), (strip, strip), (head,))
    section, mixed, rhs, ma, mb = call(
        functools.partial(section_kernel, False),
        (shape(2, 128), mixed_shape, GRID, strip, strip),
        (own, up, down, frame, oh, onehot, weight, supply, pa, pb),
    )
    ca, cb = swap_both(ma, mb, "col")
    (rhs,) = call(inner_source, (GRID,), (onehot, mixed, supply, rhs), aliases={3: 0})
    rows = shape(64, 128)
    head, rhs, sa, sb, band = call(
        functools.partial(place_columns, False),
        (EXT_SHAPE, GRID, rows, rows, BAND),
        (ca, cb, head, rhs),
        scratch=[TURN],
        aliases={2: 0, 3: 1},
    )
    ra, rb = swap_both(sa, sb, "row")
    (head,) = call(inner_relax, (EXT_SHAPE,), (head, rhs, inv), scratch=[OTHER], aliases={0: 0})
    (out,) = call(
        finish_last,
        (shape(ROWS, COLS),),
        (ra, rb, band, head, rhs, inv, rim),
        scratch=[WORK, WORK, SPARE, pltpu.VMEM((2, 8, COLS), F32), sems(2 + TILES)],
        hbm_out=(0,),
    )
    return out, section.reshape(REACH)


def solution(mesh):
    placed = (
        P("row", "col"),
        P("row", "col"),
        P("row", "col"),
        P(("row", "col")),
        P(("row", "col"), None),
        P(("row", "col"), None),
        P(("row", "col")),
        P(("row", "col")),
        P(("row", "col")),
        P(("row", "col")),
        P(),
    )
    return jax.shard_map(
        body,
        mesh=mesh,
        in_specs=placed,
        out_specs=(P("row", "col"), P(("row", "col"))),
        check_vma=False,
    )
```

time: 85.7 us -> 61.2 us (0.71)
  local copies, waits for them, and re-layouts: 8.97 us -> 0.01 us
  waiting for transfers between devices: 15.7 us -> 9.51 us
  starting transfers between devices: 26.5 us -> 20.7 us
  Pallas kernels: 33.4 us -> 29.9 us
    unnamed x24 -> x0, local copies, waits for them, and re-layouts: 8.96 us -> none
    ppermute x10, waiting for transfers between devices: 11.9 us -> 5.85 us  [swap(): return lax.ppermute(x, axis, pairs)]
    ppermute x10, starting transfers between devices: 20.1 us -> 14.6 us  [swap(): return lax.ppermute(x, axis, pairs)]
    pallas_call x10 -> x14, Pallas kernels: 33.4 us -> 29.9 us  [call(): pl.pallas_call(kernel, out_shape=outs, in_specs=[at(k, hbm) for k in rang...]
  transfers between devices with their start and end apart: 14 -> 14, of which waited for: 10 -> 6; matrix products, arithmetic and copies ran while one was open for 0% -> 0% of each run, Pallas kernels for 4% -> 29%
where the time goes in v2:
time: 61.2 us; the launch traced here: 61 us
  Pallas kernels  29.9 us (49%)
  starting transfers between devices  20.7 us (34%)
  waiting for transfers between devices  9.51 us (16%)
  between operations  0.95 us (2%)
    pallas_call x14, Pallas kernels, call(): pl.pallas_call(kernel, out_shape=outs, in_specs=[at(k, hbm) for k in rang...  29.9 us
    ppermute x10, starting transfers between devices, swap(): return lax.ppermute(x, axis, pairs)  14.6 us
    ppermute x4, starting transfers between devices, shift(): return lax.ppermute(x, axis, [(k, (k + by) % n) for k in range(n)])  6.07 us
    ppermute x10, waiting for transfers between devices, swap(): return lax.ppermute(x, axis, pairs)  5.85 us
    ppermute x4, waiting for transfers between devices, shift(): return lax.ppermute(x, axis, [(k, (k + by) % n) for k in range(n)])  3.65 us
  transfers between devices with their start and end apart: 14, of which 6 were waited for; matrix products, arithmetic and copies ran while one was open for 0% of the time, Pallas kernels for 29%

profile of v2, /device:TPU:1, one launch (start us, length us, event | category | flops | bytes accessed | tf_op | source)
XLA Modules:
  0.0 61.0 jit_solution(3850604040827620967)
XLA Ops:
  0.6 3.2 %shard_map.122 = (f32[8,1024]{1,0:T(8,128)S(1)}, bf16[1024,1024]{1,0:T(8,128)(2,1)S(1)}, f32[1024,128]{1,0:T(8,128)S(1)}, f32[3600,128]{1,0:T(8,128)S(1)}, s32[8,128]{1,0:T(8,128)S(1)}) custom-call(f32[384,1024]{1,0:T(8,128)} %head.1, s32[8,128]{1,0:T(8,128)} %bitcast.6, s32[8,128]{1,0:T(8,128)} %bitcast.7, s32[1024,128]{1,0:T(8,128)} %mask.1, ...), custom_call_target="tpu_custom_call" | custom-call | flops 10000000 | bytes 4000000 | tf_op jit(solution)/shard_map/pallas_call | solution.py:455
  3.9 3.3 %collective-permute-start = (f32[8,1024]{1,0:T(8,128)S(1)}, f32[8,1024]{1,0:T(8,128)S(1)}, u32[]{:S(2)}, u32[]{:S(2)}) collective-permute-start(f32[8,1024]{1,0:T(8,128)S(1)} %get-tuple-element.38), channel_id=1, source_target_pairs={{0,1},{1,0},{2,3},{3,2},{4,5},{5,4},{6,7},{7,6},{8,9},{9,8},{10,11... | collective-permute-start | bytes 98312 | tf_op jit(solution)/shard_map/ppermute | solution.py:473
  7.2 0.9 %collective-permute-done = f32[8,1024]{1,0:T(8,128)S(1)} collective-permute-done((f32[8,1024]{1,0:T(8,128)S(1)}, f32[8,1024]{1,0:T(8,128)S(1)}, u32[]{:S(2)}, u32[]{:S(2)}) %collective-permute-start) | collective-permute-done | bytes 32800 | tf_op jit(solution)/shard_map/ppermute | solution.py:473
  8.0 3.9 %collective-permute-start.2 = (f32[8,512]{1,0:T(8,128)S(1)}, f32[8,512]{1,0:T(8,128)S(1)}, u32[]{:S(2)}, u32[]{:S(2)}) collective-permute-start(f32[8,512]{1,0:T(8,128)S(1)} %get-tuple-element.76), channel_id=1, source_target_pairs={{0,14},{1,15},{2,0},{3,1},{4,2},{5,3},{6,4},{7,5},{8,6},{9,7},{10,... | collective-permute-start | bytes 49160 | tf_op jit(solution)/shard_map/ppermute | solution.py:484
  12.0 4.0 %shard_map.123 = (bf16[3072,1024]{1,0:T(8,128)(2,1)S(1)}, f32[9,384,128]{2,1,0:T(8,128)S(1)}, f32[8,384,128]{2,1,0:T(8,128)S(1)}) custom-call(f32[3600,128]{1,0:T(8,128)S(1)} %get-tuple-element.40.headx.refs_0_.refs_2_, f32[384,1024]{1,0:T(8,128)} %recharge.1, f32[384,1024]{1,0:T(8,128)} %storage.1, s32[8,128]{1,0:T(8,128)S(1)} %get-tuple-element.41.index8, ...), custom_call_target="tpu_custom_call" | custom-call | flops 10000000 | bytes 4000000 | tf_op jit(solution)/shard_map/pallas_call | solution.py:455
  16.2 2.5 %shard_map.125 = (f32[8,1024]{1,0:T(8,128)S(1)}, f32[2,128]{1,0:T(2,128)}, bf16[1024,256]{1,0:T(8,128)(2,1)S(1)}, f32[9,384,128]{2,1,0:T(8,128)S(1)}, f32[16,384]{1,0:T(8,128)S(1)}, /*index=5*/f32[16,384]{1,0:T(8,128)S(1)}) custom-call(f32[8,1024]{1,0:T(8,128)S(1)} %add.6.refs_0_, f32[8,512]{1,0:T(8,128)S(1)} %collective-permute-done.1.refs_1_, ...), custom_call_target="tpu_custom_call" | custom-call | flops 10000000 | bytes 4000000 | tf_op jit(solution)/shard_map/pallas_call | solution.py:455
  18.7 1.3 %collective-permute-start.3 = (f32[16,384]{1,0:T(8,128)S(1)}, f32[16,384]{1,0:T(8,128)S(1)}, u32[]{:S(2)}, u32[]{:S(2)}) collective-permute-start(f32[16,384]{1,0:T(8,128)S(1)} %get-tuple-element.48), channel_id=1, source_target_pairs={{0,1},{1,0},{2,3},{3,2},{4,5},{5,4},{6,7},{7,6},{8,9},{9,8},{10,11... | collective-permute-start | bytes 73736 | tf_op jit(solution)/shard_map/ppermute | solution.py:473
  20.0 1.4 %shard_map.126.refs_3_ = f32[9,384,128]{2,1,0:T(8,128)S(1)} custom-call(bf16[3072,1024]{1,0:T(8,128)(2,1)S(1)} %get-tuple-element.43.refs_4_.onehot.refs_5_, bf16[1024,256]{1,0:T(8,128)(2,1)S(1)} %get-tuple-element.50.mixed, f32[8,384,128]{2,1,0:T(8,128)S(1)} %get-tuple-element.44.refs_6_.supply.refs_7_, ...), custom_call_target="tpu_custom_call", output_to_operand_aliasing={{}: (3, {})} | custom-call | flops 10000000 | bytes 4000000 | tf_op jit(solution)/shard_map/pallas_call | solution.py:455
  21.5 2.1 %collective-permute-done.4.refs_1_ = f32[16,384]{1,0:T(8,128)S(1)} collective-permute-done((f32[16,384]{1,0:T(8,128)S(1)}, f32[16,384]{1,0:T(8,128)S(1)}, u32[]{:S(2)}, u32[]{:S(2)}) %collective-permute-start.4) | collective-permute-done | bytes 24608 | tf_op jit(solution)/shard_map/ppermute | solution.py:473
  23.9 1.4 %collective-permute-start.5 = (f32[96,128]{1,0:T(8,128)S(1)}, f32[96,128]{1,0:T(8,128)S(1)}, u32[]{:S(2)}, u32[]{:S(2)}) collective-permute-start(f32[96,128]{1,0:T(8,128)S(1)} %get-tuple-element.52), channel_id=1, source_target_pairs={{0,16},{16,0},{32,48},{48,32},{64,80},{80,64},{96,112},{112,96},{1... | collective-permute-start | bytes 147464 | tf_op jit(solution)/shard_map/ppermute | solution.py:473
  25.2 4.1 %collective-permute-start.6 = (f32[96,128]{1,0:T(8,128)S(1)}, f32[96,128]{1,0:T(8,128)S(1)}, u32[]{:S(2)}, u32[]{:S(2)}) collective-permute-start(f32[96,128]{1,0:T(8,128)S(1)} %get-tuple-element.53), channel_id=1, source_target_pairs={{0,240},{16,32},{32,16},{48,64},{64,48},{80,96},{96,80},{112,128},... | collective-permute-start | bytes 147464 | tf_op jit(solution)/shard_map/ppermute | solution.py:473
  29.3 5.1 %shard_map.128.head_in = f32[3600,128]{1,0:T(8,128)S(1)} custom-call(f32[3600,128]{1,0:T(8,128)S(1)} %get-tuple-element.55.head_in, f32[9,384,128]{2,1,0:T(8,128)S(1)} %get-tuple-element.56.rhs, f32[9,384,128]{2,1,0:T(8,128)S(1)} %get-tuple-element.57.inv), custom_call_target="tpu_custom_call", output_to_operand_aliasing={{}: (0, {})} | custom-call | flops 10000000 | bytes 4000000 | tf_op jit(solution)/shard_map/pallas_call | solution.py:455
  34.5 2.0 %shard_map.129 = (f32[3600,128]{1,0:T(8,128)S(1)}, f32[2,9,8,128]{3,2,1,0:T(8,128)S(1)}, f32[8,1024]{1,0:T(8,128)S(1)}) custom-call(f32[96,128]{1,0:T(8,128)S(1)} %collective-permute-done.5.ra, f32[96,128]{1,0:T(8,128)S(1)} %collective-permute-done.6.rb, f32[2,9,8,128]{3,2,1,0:T(8,128)S(1)} %get-tuple-element.54.band, ...), custom_call_target="tpu_custom_call", output_to_operand_aliasing={{0}: (3, {})} | custom-call | flops 10000000 | bytes 4000000 | tf_op jit(solution)/shard_map/pallas_call | solution.py:455
  36.5 1.6 %collective-permute-start.7 = (f32[8,1024]{1,0:T(8,128)S(1)}, f32[8,1024]{1,0:T(8,128)S(1)}, u32[]{:S(2)}, u32[]{:S(2)}) collective-permute-start(f32[8,1024]{1,0:T(8,128)S(1)} %get-tuple-element.58), channel_id=1, source_target_pairs={{0,1},{1,0},{2,3},{3,2},{4,5},{5,4},{6,7},{7,6},{8,9},{9,8},{10,11... | collective-permute-start | bytes 98312 | tf_op jit(solution)/shard_map/ppermute | solution.py:473
  38.1 0.9 %collective-permute-done.7 = f32[8,1024]{1,0:T(8,128)S(1)} collective-permute-done((f32[8,1024]{1,0:T(8,128)S(1)}, f32[8,1024]{1,0:T(8,128)S(1)}, u32[]{:S(2)}, u32[]{:S(2)}) %collective-permute-start.7) | collective-permute-done | bytes 32800 | tf_op jit(solution)/shard_map/ppermute | solution.py:473
  38.9 2.1 %collective-permute-start.9 = (f32[8,512]{1,0:T(8,128)S(1)}, f32[8,512]{1,0:T(8,128)S(1)}, u32[]{:S(2)}, u32[]{:S(2)}) collective-permute-start(f32[8,512]{1,0:T(8,128)S(1)} %get-tuple-element.74), channel_id=1, source_target_pairs={{0,14},{1,15},{2,0},{3,1},{4,2},{5,3},{6,4},{7,5},{8,6},{9,7},{10,... | collective-permute-start | bytes 49160 | tf_op jit(solution)/shard_map/ppermute | solution.py:484
  41.9 2.9 %collective-permute-done.8.refs_1_ = f32[8,512]{1,0:T(8,128)S(1)} collective-permute-done((f32[8,512]{1,0:T(8,128)S(1)}, f32[8,512]{1,0:T(8,128)S(1)}, u32[]{:S(2)}, u32[]{:S(2)}) %collective-permute-start.8) | collective-permute-done | bytes 16416 | tf_op jit(solution)/shard_map/ppermute | solution.py:484
  44.8 2.5 %shard_map.131 = (f32[2,128]{1,0:T(2,128)}, bf16[1024,256]{1,0:T(8,128)(2,1)S(1)}, f32[9,384,128]{2,1,0:T(8,128)S(1)}, f32[8,384]{1,0:T(8,128)S(1)}, f32[8,384]{1,0:T(8,128)S(1)}) custom-call(f32[8,1024]{1,0:T(8,128)S(1)} %add.7.refs_0_, f32[8,512]{1,0:T(8,128)S(1)} %collective-permute-done.8.refs_1_, f32[8,512]{1,0:T(8,128)S(1)} %collective-permute-done.9.refs_2_, ...), custom_call_target="tpu_custom_call" | custom-call | flops 10000000 | bytes 4000000 | tf_op jit(solution)/shard_map/pallas_call | solution.py:455
  47.3 1.6 %collective-permute-start.10 = (f32[8,384]{1,0:T(8,128)S(1)}, f32[8,384]{1,0:T(8,128)S(1)}, u32[]{:S(2)}, u32[]{:S(2)}) collective-permute-start(f32[8,384]{1,0:T(8,128)S(1)} %get-tuple-element.63), channel_id=1, source_target_pairs={{0,1},{1,0},{2,3},{3,2},{4,5},{5,4},{6,7},{7,6},{8,9},{9,8},{10,11... | collective-permute-start | bytes 36872 | tf_op jit(solution)/shard_map/ppermute | solution.py:473
  48.9 1.4 %shard_map.132.refs_3_ = f32[9,384,128]{2,1,0:T(8,128)S(1)} custom-call(bf16[3072,1024]{1,0:T(8,128)(2,1)S(1)} %get-tuple-element.43.refs_4_.onehot.refs_5_, bf16[1024,256]{1,0:T(8,128)(2,1)S(1)} %get-tuple-element.65.mixed, f32[8,384,128]{2,1,0:T(8,128)S(1)} %get-tuple-element.44.refs_6_.supply.refs_7_, ...), custom_call_target="tpu_custom_call", output_to_operand_aliasing={{}: (3, {})} | custom-call | flops 10000000 | bytes 4000000 | tf_op jit(solution)/shard_map/pallas_call | solution.py:455
  50.3 2.0 %collective-permute-done.11.refs_1_ = f32[8,384]{1,0:T(8,128)S(1)} collective-permute-done((f32[8,384]{1,0:T(8,128)S(1)}, f32[8,384]{1,0:T(8,128)S(1)}, u32[]{:S(2)}, u32[]{:S(2)}) %collective-permute-start.11) | collective-permute-done | bytes 12320 | tf_op jit(solution)/shard_map/ppermute | solution.py:473
  52.6 1.3 %collective-permute-start.13 = (f32[64,128]{1,0:T(8,128)S(1)}, f32[64,128]{1,0:T(8,128)S(1)}, u32[]{:S(2)}, u32[]{:S(2)}) collective-permute-start(f32[64,128]{1,0:T(8,128)S(1)} %get-tuple-element.68), channel_id=1, source_target_pairs={{0,240},{16,32},{32,16},{48,64},{64,48},{80,96},{96,80},{112,128},... | collective-permute-start | bytes 98312 | tf_op jit(solution)/shard_map/ppermute | solution.py:473
  53.9 5.3 %shard_map.134.head = f32[3600,128]{1,0:T(8,128)S(1)} custom-call(f32[3600,128]{1,0:T(8,128)S(1)} %get-tuple-element.70.head_in, f32[9,384,128]{2,1,0:T(8,128)S(1)} %get-tuple-element.71.rhs, f32[9,384,128]{2,1,0:T(8,128)S(1)} %get-tuple-element.57.inv), custom_call_target="tpu_custom_call", output_to_operand_aliasing={{}: (0, {})} | custom-call | flops 10000000 | bytes 4000000 | tf_op jit(solution)/shard_map/pallas_call | solution.py:455
  59.2 1.7 %shard_map.135 = f32[384,1024]{1,0:T(8,128)} custom-call(f32[64,128]{1,0:T(8,128)S(1)} %collective-permute-done.12.ra, f32[64,128]{1,0:T(8,128)S(1)} %collective-permute-done.13.rb, f32[2,9,8,128]{3,2,1,0:T(8,128)S(1)} %get-tuple-element.69.band, f32[3600,128]{1,0:T(8,128)S(1)} %shard_map.134.head, f32[9,384,128]{2,1,0:T(8,128)S(1)} %get-tuple-element.71.rhs, ...), custom_call_target="tpu_custom_call" | custom-call | flops 10000000 | bytes 4000000 | tf_op jit(solution)/shard_map/pallas_call | solution.py:455
  (22 shorter events, 1.7 us)
Async XLA Ops:
  3.9 4.1 %collective-permute-start = (f32[8,1024]{1,0:T(8,128)S(1)}, f32[8,1024]{1,0:T(8,128)S(1)}, u32[]{:S(2)}, u32[]{:S(2)}) collective-permute-start(f32[8,1024]{1,0:T(8,128)S(1)} %get-tuple-element.38), channel_id=1, source_target_pairs={{0,1},{1,0},{2,3},{3,2},{4,5},{5,4},{6,7},{7,6},{8,9},{9,8},{10,11... | collective-permute-start | bytes 98312 | tf_op jit(solution)/shard_map/ppermute | solution.py:473
  8.0 8.2 %collective-permute-start.2 = (f32[8,512]{1,0:T(8,128)S(1)}, f32[8,512]{1,0:T(8,128)S(1)}, u32[]{:S(2)}, u32[]{:S(2)}) collective-permute-start(f32[8,512]{1,0:T(8,128)S(1)} %get-tuple-element.76), channel_id=1, source_target_pairs={{0,14},{1,15},{2,0},{3,1},{4,2},{5,3},{6,4},{7,5},{8,6},{9,7},{10,... | collective-permute-start | bytes 49160 | tf_op jit(solution)/shard_map/ppermute | solution.py:484
  12.0 4.2 %collective-permute-start.1 = (f32[8,512]{1,0:T(8,128)S(1)}, f32[8,512]{1,0:T(8,128)S(1)}, u32[]{:S(2)}, u32[]{:S(2)}) collective-permute-start(f32[8,512]{1,0:T(8,128)S(1)} %get-tuple-element.77), channel_id=1, source_target_pairs={{0,2},{1,3},{2,4},{3,5},{4,6},{5,7},{6,8},{7,9},{8,10},{9,11},{10,... | collective-permute-start | bytes 49160 | tf_op jit(solution)/shard_map/ppermute | solution.py:484
  18.7 2.7 %collective-permute-start.3 = (f32[16,384]{1,0:T(8,128)S(1)}, f32[16,384]{1,0:T(8,128)S(1)}, u32[]{:S(2)}, u32[]{:S(2)}) collective-permute-start(f32[16,384]{1,0:T(8,128)S(1)} %get-tuple-element.48), channel_id=1, source_target_pairs={{0,1},{1,0},{2,3},{3,2},{4,5},{5,4},{6,7},{7,6},{8,9},{9,8},{10,11... | collective-permute-start | bytes 73736 | tf_op jit(solution)/shard_map/ppermute | solution.py:473
  20.0 3.5 %collective-permute-start.4 = (f32[16,384]{1,0:T(8,128)S(1)}, f32[16,384]{1,0:T(8,128)S(1)}, u32[]{:S(2)}, u32[]{:S(2)}) collective-permute-start(f32[16,384]{1,0:T(8,128)S(1)} %get-tuple-element.49), channel_id=1, source_target_pairs={{0,15},{1,2},{2,1},{3,4},{4,3},{5,6},{6,5},{7,8},{8,7},{9,10},{10,... | collective-permute-start | bytes 73736 | tf_op jit(solution)/shard_map/ppermute | solution.py:473
  23.9 10.6 %collective-permute-start.5 = (f32[96,128]{1,0:T(8,128)S(1)}, f32[96,128]{1,0:T(8,128)S(1)}, u32[]{:S(2)}, u32[]{:S(2)}) collective-permute-start(f32[96,128]{1,0:T(8,128)S(1)} %get-tuple-element.52), channel_id=1, source_target_pairs={{0,16},{16,0},{32,48},{48,32},{64,80},{80,64},{96,112},{112,96},{1... | collective-permute-start | bytes 147464 | tf_op jit(solution)/shard_map/ppermute | solution.py:473
  25.2 9.3 %collective-permute-start.6 = (f32[96,128]{1,0:T(8,128)S(1)}, f32[96,128]{1,0:T(8,128)S(1)}, u32[]{:S(2)}, u32[]{:S(2)}) collective-permute-start(f32[96,128]{1,0:T(8,128)S(1)} %get-tuple-element.53), channel_id=1, source_target_pairs={{0,240},{16,32},{32,16},{48,64},{64,48},{80,96},{96,80},{112,128},... | collective-permute-start | bytes 147464 | tf_op jit(solution)/shard_map/ppermute | solution.py:473
  36.5 2.4 %collective-permute-start.7 = (f32[8,1024]{1,0:T(8,128)S(1)}, f32[8,1024]{1,0:T(8,128)S(1)}, u32[]{:S(2)}, u32[]{:S(2)}) collective-permute-start(f32[8,1024]{1,0:T(8,128)S(1)} %get-tuple-element.58), channel_id=1, source_target_pairs={{0,1},{1,0},{2,3},{3,2},{4,5},{5,4},{6,7},{7,6},{8,9},{9,8},{10,11... | collective-permute-start | bytes 98312 | tf_op jit(solution)/shard_map/ppermute | solution.py:473
  38.9 3.0 %collective-permute-start.9 = (f32[8,512]{1,0:T(8,128)S(1)}, f32[8,512]{1,0:T(8,128)S(1)}, u32[]{:S(2)}, u32[]{:S(2)}) collective-permute-start(f32[8,512]{1,0:T(8,128)S(1)} %get-tuple-element.74), channel_id=1, source_target_pairs={{0,14},{1,15},{2,0},{3,1},{4,2},{5,3},{6,4},{7,5},{8,6},{9,7},{10,... | collective-permute-start | bytes 49160 | tf_op jit(solution)/shard_map/ppermute | solution.py:484
  41.0 3.8 %collective-permute-start.8 = (f32[8,512]{1,0:T(8,128)S(1)}, f32[8,512]{1,0:T(8,128)S(1)}, u32[]{:S(2)}, u32[]{:S(2)}) collective-permute-start(f32[8,512]{1,0:T(8,128)S(1)} %get-tuple-element.75), channel_id=1, source_target_pairs={{0,2},{1,3},{2,4},{3,5},{4,6},{5,7},{6,8},{7,9},{8,10},{9,11},{10,... | collective-permute-start | bytes 49160 | tf_op jit(solution)/shard_map/ppermute | solution.py:484
  47.3 3.0 %collective-permute-start.10 = (f32[8,384]{1,0:T(8,128)S(1)}, f32[8,384]{1,0:T(8,128)S(1)}, u32[]{:S(2)}, u32[]{:S(2)}) collective-permute-start(f32[8,384]{1,0:T(8,128)S(1)} %get-tuple-element.63), channel_id=1, source_target_pairs={{0,1},{1,0},{2,3},{3,2},{4,5},{5,4},{6,7},{7,6},{8,9},{9,8},{10,11... | collective-permute-start | bytes 36872 | tf_op jit(solution)/shard_map/ppermute | solution.py:473
  48.9 3.4 %collective-permute-start.11 = (f32[8,384]{1,0:T(8,128)S(1)}, f32[8,384]{1,0:T(8,128)S(1)}, u32[]{:S(2)}, u32[]{:S(2)}) collective-permute-start(f32[8,384]{1,0:T(8,128)S(1)} %get-tuple-element.64), channel_id=1, source_target_pairs={{0,15},{1,2},{2,1},{3,4},{4,3},{5,6},{6,5},{7,8},{8,7},{9,10},{10,... | collective-permute-start | bytes 36872 | tf_op jit(solution)/shard_map/ppermute | solution.py:473
  52.5 6.7 %collective-permute-start.12 = (f32[64,128]{1,0:T(8,128)S(1)}, f32[64,128]{1,0:T(8,128)S(1)}, u32[]{:S(2)}, u32[]{:S(2)}) collective-permute-start(f32[64,128]{1,0:T(8,128)S(1)} %get-tuple-element.67), channel_id=1, source_target_pairs={{0,16},{16,0},{32,48},{48,32},{64,80},{80,64},{96,112},{112,96},{1... | collective-permute-start | bytes 98312 | tf_op jit(solution)/shard_map/ppermute | solution.py:473
  52.6 6.6 %collective-permute-start.13 = (f32[64,128]{1,0:T(8,128)S(1)}, f32[64,128]{1,0:T(8,128)S(1)}, u32[]{:S(2)}, u32[]{:S(2)}) collective-permute-start(f32[64,128]{1,0:T(8,128)S(1)} %get-tuple-element.68), channel_id=1, source_target_pairs={{0,240},{16,32},{32,16},{48,64},{64,48},{80,96},{96,80},{112,128},... | collective-permute-start | bytes 98312 | tf_op jit(solution)/shard_map/ppermute | solution.py:473

commit v3 on v2

--- a/solution.py
+++ b/solution.py
@@ -15,6 +15,7 @@
 SEG = 1024
 REACH = 256
 FRAME = 4 * REACH
+LOCAL = 3 * REACH
 OFF = 8
 EXT = ROWS + 2 * OFF
 H = 4
@@ -61,6 +62,20 @@
         lhs[first : first + 1, at] = hi
         lhs[first + 1 : first + 2, at] = mid
         lhs[first + 2 : first + 3, at] = row - hi - mid
+
+
+def to_frame(row):
+    odd = lax.axis_index("col") % 2 == 1
+    parts = [row[:, m * REACH : (m + 1) * REACH] for m in range(3)]
+    none = jnp.zeros_like(parts[0])
+    pairs = zip([none] + parts, parts + [none])
+    return jnp.concatenate([jnp.where(odd, a, b) for a, b in pairs], axis=1)
+
+
+def to_local(row):
+    odd = lax.axis_index("col") % 2 == 1
+    parts = [row[:, m * REACH : (m + 1) * REACH] for m in range(4)]
+    return jnp.concatenate([jnp.where(odd, b, a) for a, b in zip(parts[:3], parts[1:])], axis=1)
 
 
 def prep(
@@ -87,7 +102,7 @@
     for m in moves + heads:
         m.start()
     j = lax.axis_index("col")
-    base = (j // 2) * 2 - 1
+    base = j - 1
     for c in range(WIDE):
         headx[c * EXT : c * EXT + OFF, :] = jnp.zeros((OFF, 128), F32)
         headx[(c + 1) * EXT - OFF : (c + 1) * EXT, :] = jnp.zeros((OFF, 128), F32)
@@ -105,7 +120,7 @@
     lane = lax.broadcasted_iota(I32, (128, 128), 1)
     for k in range(SEG // 128):
         slots = column_of(slot8[k : k + 1, :])
-        for q in range(FRAME // 128):
+        for q in range(LOCAL // 128):
             oh[k * 128 : (k + 1) * 128, q * 128 : (q + 1) * 128] = jnp.where(
                 slots == lane + q * 128, 1.0, 0.0
             ).astype(BF16)
@@ -131,8 +146,8 @@
     gather_rows(headx, index_s, hs)
     row_sums(lambda at: weight[at, :] * hs[at, :], lhs, 0)
     sums = jnp.dot(lhs[...].astype(BF16), oh[...], preferred_element_type=F32)
-    part[0:1, :] = sums[0:1] + sums[1:2] + sums[2:3]
-    part[1:2, :] = sums[3:4] + sums[4:5] + sums[5:6]
+    part[0:1, :] = to_frame(sums[0:1] + sums[1:2] + sums[2:3])
+    part[1:2, :] = to_frame(sums[3:4] + sums[4:5] + sums[5:6])
 
 
 def fields(headx, recharge, storage, index8, weight, onehot, inv, supply, rech_v, store_v, sems):
@@ -190,10 +205,9 @@
 
 def section_kernel(first, *refs):
     if first:
-        own, up, down, oh, onehot, weight, supply, pa, pb, frame, section, mixed, rhs, ma, mb = refs
+        own, up, down, oh, onehot, weight, supply, pa, pb, frame, mixed, rhs, ma, mb = refs
     else:
-        own, up, down, old, oh, onehot, weight, supply, pa, pb, section, mixed, rhs, ma, mb = refs
-    j = lax.axis_index("col")
+        own, up, down, old, oh, onehot, weight, supply, pa, pb, reaches, mixed, rhs, ma, mb = refs
     full = own[...] + jnp.concatenate([up[...], down[...]], axis=1)
     leak = full[0:1]
     if first:
@@ -206,14 +220,11 @@
     if first:
         frame[...] = full
         frame[4:5, :] = sec
-    odd = j % 2 == 1
-    for t in range(2):
-        a = REACH + t * 128
-        b = 2 * REACH + t * 128
-        section[t : t + 1, :] = jnp.where(odd, sec[:, b : b + 128], sec[:, a : a + 128])
-    hi, lo = split2(sec)
+    else:
+        reaches[...] = sec
+    hi, lo = split2(to_local(sec))
     wide = jnp.concatenate(
-        [jnp.broadcast_to(hi.astype(F32), (128, FRAME)), jnp.broadcast_to(lo.astype(F32), (128, FRAME))], axis=0
+        [jnp.broadcast_to(hi.astype(F32), (128, LOCAL)), jnp.broadcast_to(lo.astype(F32), (128, LOCAL))], axis=0
     ).astype(BF16)
     got = lax.dot_general(oh[...], wide, (((1,), (1,)), ((), ())), preferred_element_type=F32)
     both = both_halves(weight[...] * (got[:, :128] + got[:, 128:]))
@@ -410,16 +421,20 @@
     row_sums(lambda at: weight[at, :] * hs[at, :], lhs, 0)
     sums = jnp.dot(lhs[...].astype(BF16), oh[...], preferred_element_type=F32)
     part[...] = jnp.zeros_like(part)
-    part[0:1, :] = sums[0:1] + sums[1:2] + sums[2:3]
-
-
-def finish_last(ra, rb, band, head, rhs, inv, rim, out, one, two, spare, edge, sems):
+    part[0:1, :] = to_frame(sums[0:1] + sums[1:2] + sums[2:3])
+
+
+def finish_last(ra, rb, band, head, rhs, inv, rim, reaches, out, section, one, two, spare, edge, mine, sems):
+    sec = to_local(reaches[...])
+    for t in range(2):
+        mine[t : t + 1, :] = sec[:, REACH + t * 128 : REACH + (t + 1) * 128]
     moves = [
         pltpu.make_async_copy(
             head.at[tile_rows(c, 8, ROWS - 16), :], out.at[8 : ROWS - 8, c * 128 : (c + 1) * 128], sems.at[2 + c]
         )
         for c in range(TILES)
     ]
+    moves.append(pltpu.make_async_copy(mine, section, sems.at[2 + TILES]))
     for m in moves:
         m.start()
     fill_spare(ra, rb, 1, 2, spare)
@@ -464,18 +479,31 @@
     )(*[far(x) if k in hbm else x for k, x in enumerate(ins)])
 
 
-def swap(x, axis, which):
-    n = lax.axis_size(axis)
-    if which == 0:
-        pairs = [(k, k ^ 1) for k in range(n)]
-    else:
-        pairs = [(k, (k + 1) % n if k % 2 else (k - 1) % n) for k in range(n)]
-    return lax.ppermute(x, axis, pairs)
+def swap(x, axis):
+    return lax.ppermute(x, axis, [(k, k ^ 1) for k in range(lax.axis_size(axis))])
+
+
+def far_swap(x, axis):
+    n, m = lax.axis_size("row"), lax.axis_size("col")
+
+    def partner(r, c):
+        if axis == "col":
+            return r, (c + 1) % m if c % 2 else (c - 1) % m
+        if r in (0, n - 1):
+            return r, c ^ 1
+        return (r + 1 if r % 2 else r - 1), c
+
+    pairs = []
+    for r in range(n):
+        for c in range(m):
+            to = partner(r, c)
+            pairs.append((r * m + c, to[0] * m + to[1]))
+    return lax.ppermute(x, ("row", "col"), pairs)
 
 
 def swap_both(a, b, axis):
-    b = swap(b, axis, 1)
-    a = swap(a, axis, 0)
+    b = far_swap(b, axis)
+    a = swap(a, axis)
     return a, b
 
 
@@ -485,7 +513,7 @@
 
 
 def exchange_sums(part):
-    both = part + swap(part, "col", 0)
+    both = part + swap(part, "col")
     up = shift(both[:, 2 * REACH :], "col", 2)
     down = shift(both[:, : 2 * REACH], "col", -2)
     return both, up, down
@@ -510,7 +538,7 @@
 def body(head0, recharge, storage, seg_block, seg_mask, seg_cond, seg_reach, bed, sec0, net, infl):
     part, oh, weight, head, index8 = call(
         prep,
-        (shape(8, FRAME), shape(SEG, FRAME, dtype=BF16), shape(SEG, 128), EXT_SHAPE, shape(8, 128, dtype=I32)),
+        (shape(8, FRAME), shape(SEG, LOCAL, dtype=BF16), shape(SEG, 128), EXT_SHAPE, shape(8, 128, dtype=I32)),
         (
             head0,
             seg_block.reshape(8, 128),
@@ -549,9 +577,9 @@
     strip = shape(16, ROWS)
     pa, pb = call(functools.partial(columns, True), (strip, strip), (head, inv))
     mixed_shape = shape(SEG, 256, dtype=BF16)
-    frame, section, mixed, rhs, ma, mb = call(
+    frame, mixed, rhs, ma, mb = call(
         functools.partial(section_kernel, True),
-        (shape(8, FRAME), shape(2, 128), mixed_shape, GRID, strip, strip),
+        (shape(8, FRAME), mixed_shape, GRID, strip, strip),
         (own, up, down, oh, onehot, weight, supply, pa, pb),
     )
     ca, cb = swap_both(ma, mb, "col")
@@ -576,9 +604,9 @@
     own, up, down = exchange_sums(part)
     strip = shape(8, ROWS)
     pa, pb = call(functools.partial(columns, False), (strip, strip), (head,))
-    section, mixed, rhs, ma, mb = call(
+    reaches, mixed, rhs, ma, mb = call(
         functools.partial(section_kernel, False),
-        (shape(2, 128), mixed_shape, GRID, strip, strip),
+        (shape(1, FRAME), mixed_shape, GRID, strip, strip),
         (own, up, down, frame, oh, onehot, weight, supply, pa, pb),
     )
     ca, cb = swap_both(ma, mb, "col")
@@ -593,12 +621,12 @@
     )
     ra, rb = swap_both(sa, sb, "row")
     (head,) = call(inner_relax, (EXT_SHAPE,), (head, rhs, inv), scratch=[OTHER], aliases={0: 0})
-    (out,) = call(
+    out, section = call(
         finish_last,
-        (shape(ROWS, COLS),),
-        (ra, rb, band, head, rhs, inv, rim),
-        scratch=[WORK, WORK, SPARE, pltpu.VMEM((2, 8, COLS), F32), sems(2 + TILES)],
-        hbm_out=(0,),
+        (shape(ROWS, COLS), shape(2, 128)),
+        (ra, rb, band, head, rhs, inv, rim, reaches),
+        scratch=[WORK, WORK, SPARE, pltpu.VMEM((2, 8, COLS), F32), pltpu.VMEM((2, 128), F32), sems(3 + TILES)],
+        hbm_out=(0, 1),
     )
     return out, section.reshape(REACH)
 

time: 61.2 us -> 57.9 us (0.946)
  Pallas kernels: 29.9 us -> 28.3 us
  starting transfers between devices: 20.7 us -> 19.3 us
    pallas_call x14, Pallas kernels: 29.9 us -> 28.3 us  [call(): pl.pallas_call(kernel, out_shape=outs, in_specs=[at(k, hbm) for k in rang...]
    ppermute x10, starting transfers between devices: 14.6 us -> 13.3 us  [the longest x6 10.1 us: swap(): lax.ppermute(x, axis, [(k, k ^ 1) for k in range(lax.axis_size(axis))])]
  transfers between devices with their start and end apart: 14 -> 14, of which waited for: 6 -> 6; matrix products, arithmetic and copies ran while one was open for 0% -> 0% of each run, Pallas kernels for 29% -> 30%
where the time goes in v3:
time: 57.9 us; the launch traced here: 57.8 us
  Pallas kernels  28.3 us (49%)
  starting transfers between devices  19.3 us (33%)
  waiting for transfers between devices  9.26 us (16%)
  between operations  0.96 us (2%)
    pallas_call x14, Pallas kernels, call(): pl.pallas_call(kernel, out_shape=outs, in_specs=[at(k, hbm) for k in rang...  28.3 us
    ppermute x6, starting transfers between devices, swap(): lax.ppermute(x, axis, [(k, k ^ 1) for k in range(lax.axis_size(axis))])  10.1 us
    ppermute x4, starting transfers between devices, shift(): return lax.ppermute(x, axis, [(k, (k + by) % n) for k in range(n)])  6.02 us
    ppermute x4, waiting for transfers between devices, shift(): return lax.ppermute(x, axis, [(k, (k + by) % n) for k in range(n)])  3.65 us
    ppermute x4, waiting for transfers between devices, far_swap(): return lax.ppermute(x, ('row', 'col'), pairs)  3.54 us
    ppermute x4, starting transfers between devices, far_swap(): return lax.ppermute(x, ('row', 'col'), pairs)  3.19 us
    ppermute x6, waiting for transfers between devices, swap(): lax.ppermute(x, axis, [(k, k ^ 1) for k in range(lax.axis_size(axis))])  2.06 us
  transfers between devices with their start and end apart: 14, of which 6 were waited for; matrix products, arithmetic and copies ran while one was open for 0% of the time, Pallas kernels for 30%

profile of v3, /device:TPU:1, one launch (start us, length us, event | category | flops | bytes accessed | tf_op | source)
XLA Modules:
  0.0 57.8 jit_solution(14299097791154026583)
XLA Ops:
  0.6 3.2 %shard_map.122 = (f32[8,1024]{1,0:T(8,128)S(1)}, bf16[1024,768]{1,0:T(8,128)(2,1)S(1)}, f32[1024,128]{1,0:T(8,128)S(1)}, f32[3600,128]{1,0:T(8,128)S(1)}, s32[8,128]{1,0:T(8,128)S(1)}) custom-call(f32[384,1024]{1,0:T(8,128)} %head.1, s32[8,128]{1,0:T(8,128)} %bitcast.6, s32[8,128]{1,0:T(8,128)} %bitcast.7, s32[1024,128]{1,0:T(8,128)} %mask.1, ...), custom_call_target="tpu_custom_call" | custom-call | flops 10000000 | bytes 4000000 | tf_op jit(solution)/shard_map/pallas_call | solution.py:470
  3.9 3.3 %collective-permute-start = (f32[8,1024]{1,0:T(8,128)S(1)}, f32[8,1024]{1,0:T(8,128)S(1)}, u32[]{:S(2)}, u32[]{:S(2)}) collective-permute-start(f32[8,1024]{1,0:T(8,128)S(1)} %get-tuple-element.40), channel_id=1, source_target_pairs={{0,1},{1,0},{2,3},{3,2},{4,5},{5,4},{6,7},{7,6},{8,9},{9,8},{10,11... | collective-permute-start | bytes 98312 | tf_op jit(solution)/shard_map/ppermute | solution.py:483
  7.2 0.9 %collective-permute-done = f32[8,1024]{1,0:T(8,128)S(1)} collective-permute-done((f32[8,1024]{1,0:T(8,128)S(1)}, f32[8,1024]{1,0:T(8,128)S(1)}, u32[]{:S(2)}, u32[]{:S(2)}) %collective-permute-start) | collective-permute-done | bytes 32800 | tf_op jit(solution)/shard_map/ppermute | solution.py:483
  8.0 3.9 %collective-permute-start.2 = (f32[8,512]{1,0:T(8,128)S(1)}, f32[8,512]{1,0:T(8,128)S(1)}, u32[]{:S(2)}, u32[]{:S(2)}) collective-permute-start(f32[8,512]{1,0:T(8,128)S(1)} %get-tuple-element.80), channel_id=1, source_target_pairs={{0,14},{1,15},{2,0},{3,1},{4,2},{5,3},{6,4},{7,5},{8,6},{9,7},{10,... | collective-permute-start | bytes 49160 | tf_op jit(solution)/shard_map/ppermute | solution.py:512
  12.0 3.9 %shard_map.123 = (bf16[3072,1024]{1,0:T(8,128)(2,1)S(1)}, f32[9,384,128]{2,1,0:T(8,128)S(1)}, f32[8,384,128]{2,1,0:T(8,128)S(1)}) custom-call(f32[3600,128]{1,0:T(8,128)S(1)} %get-tuple-element.42.headx.refs_0_.refs_2_, f32[384,1024]{1,0:T(8,128)} %recharge.1, f32[384,1024]{1,0:T(8,128)} %storage.1, s32[8,128]{1,0:T(8,128)S(1)} %get-tuple-element.43.index8, ...), custom_call_target="tpu_custom_call" | custom-call | flops 10000000 | bytes 4000000 | tf_op jit(solution)/shard_map/pallas_call | solution.py:470
  16.2 1.8 %shard_map.125 = (f32[8,1024]{1,0:T(8,128)S(1)}, bf16[1024,256]{1,0:T(8,128)(2,1)S(1)}, f32[9,384,128]{2,1,0:T(8,128)S(1)}, f32[16,384]{1,0:T(8,128)S(1)}, f32[16,384]{1,0:T(8,128)S(1)}) custom-call(f32[8,1024]{1,0:T(8,128)S(1)} %add.6.refs_0_, f32[8,512]{1,0:T(8,128)S(1)} %collective-permute-done.1.refs_1_, f32[8,512]{1,0:T(8,128)S(1)} %collective-permute-done.2.refs_2_, ...), custom_call_target="tpu_custom_call" | custom-call | flops 10000000 | bytes 4000000 | tf_op jit(solution)/shard_map/pallas_call | solution.py:470
  18.0 1.5 %collective-permute-start.3 = (f32[16,384]{1,0:T(8,128)S(1)}, f32[16,384]{1,0:T(8,128)S(1)}, u32[]{:S(2)}, u32[]{:S(2)}) collective-permute-start(f32[16,384]{1,0:T(8,128)S(1)} %get-tuple-element.50), channel_id=1, source_target_pairs={{0,1},{1,0},{2,3},{3,2},{4,5},{5,4},{6,7},{7,6},{8,9},{9,8},{10,11... | collective-permute-start | bytes 73736 | tf_op jit(solution)/shard_map/ppermute | solution.py:483
  19.5 1.4 %shard_map.126.refs_3_ = f32[9,384,128]{2,1,0:T(8,128)S(1)} custom-call(bf16[3072,1024]{1,0:T(8,128)(2,1)S(1)} %get-tuple-element.45.refs_4_.onehot.refs_5_, bf16[1024,256]{1,0:T(8,128)(2,1)S(1)} %get-tuple-element.52.mixed, f32[8,384,128]{2,1,0:T(8,128)S(1)} %get-tuple-element.46.refs_6_.supply.refs_7_, ...), custom_call_target="tpu_custom_call", output_to_operand_aliasing={{}: (3, {})} | custom-call | flops 10000000 | bytes 4000000 | tf_op jit(solution)/shard_map/pallas_call | solution.py:470
  20.9 1.8 %collective-permute-done.4.refs_1_ = f32[16,384]{1,0:T(8,128)S(1)} collective-permute-done((f32[16,384]{1,0:T(8,128)S(1)}, f32[16,384]{1,0:T(8,128)S(1)}, u32[]{:S(2)}, u32[]{:S(2)}) %collective-permute-start.4) | collective-permute-done | bytes 24608 | tf_op jit(solution)/shard_map/ppermute | solution.py:501
  23.0 1.4 %collective-permute-start.5 = (f32[96,128]{1,0:T(8,128)S(1)}, f32[96,128]{1,0:T(8,128)S(1)}, u32[]{:S(2)}, u32[]{:S(2)}) collective-permute-start(f32[96,128]{1,0:T(8,128)S(1)} %get-tuple-element.54), channel_id=1, source_target_pairs={{0,16},{16,0},{32,48},{48,32},{64,80},{80,64},{96,112},{112,96},{1... | collective-permute-start | bytes 147464 | tf_op jit(solution)/shard_map/ppermute | solution.py:483
  24.4 1.6 %collective-permute-start.6 = (f32[96,128]{1,0:T(8,128)S(1)}, f32[96,128]{1,0:T(8,128)S(1)}, u32[]{:S(2)}, u32[]{:S(2)}) collective-permute-start(f32[96,128]{1,0:T(8,128)S(1)} %get-tuple-element.55), channel_id=1, source_target_pairs={{0,1},{1,0},{2,3},{3,2},{4,5},{5,4},{6,7},{7,6},{8,9},{9,8},{10,11... | collective-permute-start | bytes 147464 | tf_op jit(solution)/shard_map/ppermute | solution.py:501
  26.0 5.0 %shard_map.128.head_in = f32[3600,128]{1,0:T(8,128)S(1)} custom-call(f32[3600,128]{1,0:T(8,128)S(1)} %get-tuple-element.57.head_in, f32[9,384,128]{2,1,0:T(8,128)S(1)} %get-tuple-element.58.rhs, f32[9,384,128]{2,1,0:T(8,128)S(1)} %get-tuple-element.59.inv), custom_call_target="tpu_custom_call", output_to_operand_aliasing={{}: (0, {})} | custom-call | flops 10000000 | bytes 4000000 | tf_op jit(solution)/shard_map/pallas_call | solution.py:470
  31.0 2.0 %shard_map.129 = (f32[3600,128]{1,0:T(8,128)S(1)}, f32[2,9,8,128]{3,2,1,0:T(8,128)S(1)}, f32[8,1024]{1,0:T(8,128)S(1)}) custom-call(f32[96,128]{1,0:T(8,128)S(1)} %collective-permute-done.5.ra, f32[96,128]{1,0:T(8,128)S(1)} %collective-permute-done.6.rb, f32[2,9,8,128]{3,2,1,0:T(8,128)S(1)} %get-tuple-element.56.band, ...), custom_call_target="tpu_custom_call", output_to_operand_aliasing={{0}: (3, {})} | custom-call | flops 10000000 | bytes 4000000 | tf_op jit(solution)/shard_map/pallas_call | solution.py:470
  33.1 1.2 %collective-permute-done.7 = f32[8,1024]{1,0:T(8,128)S(1)} collective-permute-done((f32[8,1024]{1,0:T(8,128)S(1)}, f32[8,1024]{1,0:T(8,128)S(1)}, u32[]{:S(2)}, u32[]{:S(2)}) %collective-permute-start.7) | collective-permute-done | bytes 32800 | tf_op jit(solution)/shard_map/ppermute | solution.py:483
  34.3 2.1 %collective-permute-start.9 = (f32[8,512]{1,0:T(8,128)S(1)}, f32[8,512]{1,0:T(8,128)S(1)}, u32[]{:S(2)}, u32[]{:S(2)}) collective-permute-start(f32[8,512]{1,0:T(8,128)S(1)} %get-tuple-element.78), channel_id=1, source_target_pairs={{0,14},{1,15},{2,0},{3,1},{4,2},{5,3},{6,4},{7,5},{8,6},{9,7},{10,... | collective-permute-start | bytes 49160 | tf_op jit(solution)/shard_map/ppermute | solution.py:512
  37.3 2.9 %collective-permute-done.8.refs_1_ = f32[8,512]{1,0:T(8,128)S(1)} collective-permute-done((f32[8,512]{1,0:T(8,128)S(1)}, f32[8,512]{1,0:T(8,128)S(1)}, u32[]{:S(2)}, u32[]{:S(2)}) %collective-permute-start.8) | collective-permute-done | bytes 16416 | tf_op jit(solution)/shard_map/ppermute | solution.py:512
  40.2 1.8 %shard_map.131 = (f32[1,1024]{1,0:T(1,128)S(1)}, bf16[1024,256]{1,0:T(8,128)(2,1)S(1)}, f32[9,384,128]{2,1,0:T(8,128)S(1)}, f32[8,384]{1,0:T(8,128)S(1)}, f32[8,384]{1,0:T(8,128)S(1)}) custom-call(f32[8,1024]{1,0:T(8,128)S(1)} %add.7.refs_0_, f32[8,512]{1,0:T(8,128)S(1)} %collective-permute-done.8.refs_1_, f32[8,512]{1,0:T(8,128)S(1)} %collective-permute-done.9.refs_2_, ...), custom_call_target="tpu_custom_call" | custom-call | flops 10000000 | bytes 4000000 | tf_op jit(solution)/shard_map/pallas_call | solution.py:470
  42.0 1.9 %collective-permute-start.10 = (f32[8,384]{1,0:T(8,128)S(1)}, f32[8,384]{1,0:T(8,128)S(1)}, u32[]{:S(2)}, u32[]{:S(2)}) collective-permute-start(f32[8,384]{1,0:T(8,128)S(1)} %get-tuple-element.65), channel_id=1, source_target_pairs={{0,1},{1,0},{2,3},{3,2},{4,5},{5,4},{6,7},{7,6},{8,9},{9,8},{10,11... | collective-permute-start | bytes 36872 | tf_op jit(solution)/shard_map/ppermute | solution.py:483
  43.9 1.4 %shard_map.132.refs_3_ = f32[9,384,128]{2,1,0:T(8,128)S(1)} custom-call(bf16[3072,1024]{1,0:T(8,128)(2,1)S(1)} %get-tuple-element.45.refs_4_.onehot.refs_5_, bf16[1024,256]{1,0:T(8,128)(2,1)S(1)} %get-tuple-element.67.mixed, f32[8,384,128]{2,1,0:T(8,128)S(1)} %get-tuple-element.46.refs_6_.supply.refs_7_, ...), custom_call_target="tpu_custom_call", output_to_operand_aliasing={{}: (3, {})} | custom-call | flops 10000000 | bytes 4000000 | tf_op jit(solution)/shard_map/pallas_call | solution.py:470
  45.3 1.7 %collective-permute-done.11.refs_1_ = f32[8,384]{1,0:T(8,128)S(1)} collective-permute-done((f32[8,384]{1,0:T(8,128)S(1)}, f32[8,384]{1,0:T(8,128)S(1)}, u32[]{:S(2)}, u32[]{:S(2)}) %collective-permute-start.11) | collective-permute-done | bytes 12320 | tf_op jit(solution)/shard_map/ppermute | solution.py:501
  47.2 2.0 %collective-permute-start.12 = (f32[64,128]{1,0:T(8,128)S(1)}, f32[64,128]{1,0:T(8,128)S(1)}, u32[]{:S(2)}, u32[]{:S(2)}) collective-permute-start(f32[64,128]{1,0:T(8,128)S(1)} %get-tuple-element.69), channel_id=1, source_target_pairs={{0,16},{16,0},{32,48},{48,32},{64,80},{80,64},{96,112},{112,96},{1... | collective-permute-start | bytes 98312 | tf_op jit(solution)/shard_map/ppermute | solution.py:483
  49.2 1.6 %collective-permute-start.13 = (f32[64,128]{1,0:T(8,128)S(1)}, f32[64,128]{1,0:T(8,128)S(1)}, u32[]{:S(2)}, u32[]{:S(2)}) collective-permute-start(f32[64,128]{1,0:T(8,128)S(1)} %get-tuple-element.70), channel_id=1, source_target_pairs={{0,1},{1,0},{2,3},{3,2},{4,5},{5,4},{6,7},{7,6},{8,9},{9,8},{10,11... | collective-permute-start | bytes 98312 | tf_op jit(solution)/shard_map/ppermute | solution.py:501
  50.8 5.2 %shard_map.134.head = f32[3600,128]{1,0:T(8,128)S(1)} custom-call(f32[3600,128]{1,0:T(8,128)S(1)} %get-tuple-element.72.head_in, f32[9,384,128]{2,1,0:T(8,128)S(1)} %get-tuple-element.73.rhs, f32[9,384,128]{2,1,0:T(8,128)S(1)} %get-tuple-element.59.inv), custom_call_target="tpu_custom_call", output_to_operand_aliasing={{}: (0, {})} | custom-call | flops 10000000 | bytes 4000000 | tf_op jit(solution)/shard_map/pallas_call | solution.py:470
  56.1 1.6 %shard_map.135 = (f32[384,1024]{1,0:T(8,128)}, f32[2,128]{1,0:T(2,128)}) custom-call(f32[64,128]{1,0:T(8,128)S(1)} %collective-permute-done.12.ra, f32[64,128]{1,0:T(8,128)S(1)} %collective-permute-done.13.rb, f32[2,9,8,128]{3,2,1,0:T(8,128)S(1)} %get-tuple-element.71.band, f32[3600,128]{1,0:T(8,128)S(1)} %shard_map.134.head, ...), custom_call_target="tpu_custom_call" | custom-call | flops 10000000 | bytes 4000000 | tf_op jit(solution)/shard_map/pallas_call | solution.py:470
  (22 shorter events, 1.7 us)
Async XLA Ops:
  3.9 4.1 %collective-permute-start = (f32[8,1024]{1,0:T(8,128)S(1)}, f32[8,1024]{1,0:T(8,128)S(1)}, u32[]{:S(2)}, u32[]{:S(2)}) collective-permute-start(f32[8,1024]{1,0:T(8,128)S(1)} %get-tuple-element.40), channel_id=1, source_target_pairs={{0,1},{1,0},{2,3},{3,2},{4,5},{5,4},{6,7},{7,6},{8,9},{9,8},{10,11... | collective-permute-start | bytes 98312 | tf_op jit(solution)/shard_map/ppermute | solution.py:483
  8.0 8.1 %collective-permute-start.2 = (f32[8,512]{1,0:T(8,128)S(1)}, f32[8,512]{1,0:T(8,128)S(1)}, u32[]{:S(2)}, u32[]{:S(2)}) collective-permute-start(f32[8,512]{1,0:T(8,128)S(1)} %get-tuple-element.80), channel_id=1, source_target_pairs={{0,14},{1,15},{2,0},{3,1},{4,2},{5,3},{6,4},{7,5},{8,6},{9,7},{10,... | collective-permute-start | bytes 49160 | tf_op jit(solution)/shard_map/ppermute | solution.py:512
  12.0 4.2 %collective-permute-start.1 = (f32[8,512]{1,0:T(8,128)S(1)}, f32[8,512]{1,0:T(8,128)S(1)}, u32[]{:S(2)}, u32[]{:S(2)}) collective-permute-start(f32[8,512]{1,0:T(8,128)S(1)} %get-tuple-element.81), channel_id=1, source_target_pairs={{0,2},{1,3},{2,4},{3,5},{4,6},{5,7},{6,8},{7,9},{8,10},{9,11},{10,... | collective-permute-start | bytes 49160 | tf_op jit(solution)/shard_map/ppermute | solution.py:512
  18.0 2.9 %collective-permute-start.3 = (f32[16,384]{1,0:T(8,128)S(1)}, f32[16,384]{1,0:T(8,128)S(1)}, u32[]{:S(2)}, u32[]{:S(2)}) collective-permute-start(f32[16,384]{1,0:T(8,128)S(1)} %get-tuple-element.50), channel_id=1, source_target_pairs={{0,1},{1,0},{2,3},{3,2},{4,5},{5,4},{6,7},{7,6},{8,9},{9,8},{10,11... | collective-permute-start | bytes 73736 | tf_op jit(solution)/shard_map/ppermute | solution.py:483
  19.5 3.3 %collective-permute-start.4 = (f32[16,384]{1,0:T(8,128)S(1)}, f32[16,384]{1,0:T(8,128)S(1)}, u32[]{:S(2)}, u32[]{:S(2)}) collective-permute-start(f32[16,384]{1,0:T(8,128)S(1)} %get-tuple-element.51), channel_id=1, source_target_pairs={{0,15},{1,2},{2,1},{3,4},{4,3},{5,6},{6,5},{7,8},{8,7},{9,10},{10,... | collective-permute-start | bytes 73736 | tf_op jit(solution)/shard_map/ppermute | solution.py:501
  23.0 8.0 %collective-permute-start.5 = (f32[96,128]{1,0:T(8,128)S(1)}, f32[96,128]{1,0:T(8,128)S(1)}, u32[]{:S(2)}, u32[]{:S(2)}) collective-permute-start(f32[96,128]{1,0:T(8,128)S(1)} %get-tuple-element.54), channel_id=1, source_target_pairs={{0,16},{16,0},{32,48},{48,32},{64,80},{80,64},{96,112},{112,96},{1... | collective-permute-start | bytes 147464 | tf_op jit(solution)/shard_map/ppermute | solution.py:483
  24.4 6.6 %collective-permute-start.6 = (f32[96,128]{1,0:T(8,128)S(1)}, f32[96,128]{1,0:T(8,128)S(1)}, u32[]{:S(2)}, u32[]{:S(2)}) collective-permute-start(f32[96,128]{1,0:T(8,128)S(1)} %get-tuple-element.55), channel_id=1, source_target_pairs={{0,1},{1,0},{2,3},{3,2},{4,5},{5,4},{6,7},{7,6},{8,9},{9,8},{10,11... | collective-permute-start | bytes 147464 | tf_op jit(solution)/shard_map/ppermute | solution.py:501
  33.0 1.3 %collective-permute-start.7 = (f32[8,1024]{1,0:T(8,128)S(1)}, f32[8,1024]{1,0:T(8,128)S(1)}, u32[]{:S(2)}, u32[]{:S(2)}) collective-permute-start(f32[8,1024]{1,0:T(8,128)S(1)} %get-tuple-element.60), channel_id=1, source_target_pairs={{0,1},{1,0},{2,3},{3,2},{4,5},{5,4},{6,7},{7,6},{8,9},{9,8},{10,11... | collective-permute-start | bytes 98312 | tf_op jit(solution)/shard_map/ppermute | solution.py:483
  34.3 2.9 %collective-permute-start.9 = (f32[8,512]{1,0:T(8,128)S(1)}, f32[8,512]{1,0:T(8,128)S(1)}, u32[]{:S(2)}, u32[]{:S(2)}) collective-permute-start(f32[8,512]{1,0:T(8,128)S(1)} %get-tuple-element.78), channel_id=1, source_target_pairs={{0,14},{1,15},{2,0},{3,1},{4,2},{5,3},{6,4},{7,5},{8,6},{9,7},{10,... | collective-permute-start | bytes 49160 | tf_op jit(solution)/shard_map/ppermute | solution.py:512
  36.4 3.8 %collective-permute-start.8 = (f32[8,512]{1,0:T(8,128)S(1)}, f32[8,512]{1,0:T(8,128)S(1)}, u32[]{:S(2)}, u32[]{:S(2)}) collective-permute-start(f32[8,512]{1,0:T(8,128)S(1)} %get-tuple-element.79), channel_id=1, source_target_pairs={{0,2},{1,3},{2,4},{3,5},{4,6},{5,7},{6,8},{7,9},{8,10},{9,11},{10,... | collective-permute-start | bytes 49160 | tf_op jit(solution)/shard_map/ppermute | solution.py:512
  42.0 3.3 %collective-permute-start.10 = (f32[8,384]{1,0:T(8,128)S(1)}, f32[8,384]{1,0:T(8,128)S(1)}, u32[]{:S(2)}, u32[]{:S(2)}) collective-permute-start(f32[8,384]{1,0:T(8,128)S(1)} %get-tuple-element.65), channel_id=1, source_target_pairs={{0,1},{1,0},{2,3},{3,2},{4,5},{5,4},{6,7},{7,6},{8,9},{9,8},{10,11... | collective-permute-start | bytes 36872 | tf_op jit(solution)/shard_map/ppermute | solution.py:483
  43.9 3.1 %collective-permute-start.11 = (f32[8,384]{1,0:T(8,128)S(1)}, f32[8,384]{1,0:T(8,128)S(1)}, u32[]{:S(2)}, u32[]{:S(2)}) collective-permute-start(f32[8,384]{1,0:T(8,128)S(1)} %get-tuple-element.66), channel_id=1, source_target_pairs={{0,15},{1,2},{2,1},{3,4},{4,3},{5,6},{6,5},{7,8},{8,7},{9,10},{10,... | collective-permute-start | bytes 36872 | tf_op jit(solution)/shard_map/ppermute | solution.py:501
  47.2 8.8 %collective-permute-start.12 = (f32[64,128]{1,0:T(8,128)S(1)}, f32[64,128]{1,0:T(8,128)S(1)}, u32[]{:S(2)}, u32[]{:S(2)}) collective-permute-start(f32[64,128]{1,0:T(8,128)S(1)} %get-tuple-element.69), channel_id=1, source_target_pairs={{0,16},{16,0},{32,48},{48,32},{64,80},{80,64},{96,112},{112,96},{1... | collective-permute-start | bytes 98312 | tf_op jit(solution)/shard_map/ppermute | solution.py:483
  49.2 6.8 %collective-permute-start.13 = (f32[64,128]{1,0:T(8,128)S(1)}, f32[64,128]{1,0:T(8,128)S(1)}, u32[]{:S(2)}, u32[]{:S(2)}) collective-permute-start(f32[64,128]{1,0:T(8,128)S(1)} %get-tuple-element.70), channel_id=1, source_target_pairs={{0,1},{1,0},{2,3},{3,2},{4,5},{5,4},{6,7},{7,6},{8,9},{9,8},{10,11... | collective-permute-start | bytes 98312 | tf_op jit(solution)/shard_map/ppermute | solution.py:501

commit v4 on v3

--- a/solution.py
+++ b/solution.py
@@ -20,7 +20,7 @@
 EXT = ROWS + 2 * OFF
 H = 4
 DEPTH = (4, 3, 3)
-UNROLL = 12
+UNROLL = 24
 F32 = jnp.float32
 BF16 = jnp.bfloat16
 I32 = jnp.int32
@@ -79,8 +79,8 @@
 
 
 def prep(
-    head, blk, reach, mask, condu, bed, sec0, net, infl,
-    part, oh, weight, headx, index8,
+    head, blk, reach, mask, condu, bed, sec0, net, infl, recharge,
+    part, oh, weight, headx, index8, rech_v,
     hs, lhs, blk_v, reach_v, mask_v, cond_v, bed_v, sec0_v, net_v, infl_s, index_s, sems,
 ):
     moves = [
@@ -143,20 +143,19 @@
     listed.wait()
     for m in heads:
         m.wait()
+    later = pltpu.make_async_copy(recharge, rech_v, sems.at[17])
+    later.start()
     gather_rows(headx, index_s, hs)
     row_sums(lambda at: weight[at, :] * hs[at, :], lhs, 0)
     sums = jnp.dot(lhs[...].astype(BF16), oh[...], preferred_element_type=F32)
     part[0:1, :] = to_frame(sums[0:1] + sums[1:2] + sums[2:3])
     part[1:2, :] = to_frame(sums[3:4] + sums[4:5] + sums[5:6])
-
-
-def fields(headx, recharge, storage, index8, weight, onehot, inv, supply, rech_v, store_v, sems):
-    moves = [
-        pltpu.make_async_copy(recharge, rech_v, sems.at[0]),
-        pltpu.make_async_copy(storage, store_v, sems.at[1]),
-    ]
-    for m in moves:
-        m.start()
+    later.wait()
+
+
+def one_hot(index8, storage, onehot, store_v, sem):
+    move = pltpu.make_async_copy(storage, store_v, sem)
+    move.start()
     target = index8[...]
     iota = lax.broadcasted_iota(I32, (ROWS, 128), 0)
     for k in range(SEG // 128):
@@ -165,10 +164,12 @@
             onehot[c * ROWS : (c + 1) * ROWS, k * 128 : (k + 1) * 128] = jnp.where(
                 row == iota + (c * EXT + OFF), 1.0, 0.0
             ).astype(BF16)
+    move.wait()
+
+
+def fields(headx, rech_v, store_v, weight, onehot, inv, supply):
     both = both_halves(weight[...])
     inv[TILES] = jnp.zeros((ROWS, 128), F32)
-    for m in moves:
-        m.wait()
     for c in range(TILES):
         at = slice(c * 128, (c + 1) * 128)
         got = jnp.dot(onehot[c * ROWS : (c + 1) * ROWS, :], both, preferred_element_type=F32)
@@ -536,9 +537,9 @@
 
 
 def body(head0, recharge, storage, seg_block, seg_mask, seg_cond, seg_reach, bed, sec0, net, infl):
-    part, oh, weight, head, index8 = call(
+    part, oh, weight, head, index8, rech = call(
         prep,
-        (shape(8, FRAME), shape(SEG, LOCAL, dtype=BF16), shape(SEG, 128), EXT_SHAPE, shape(8, 128, dtype=I32)),
+        (shape(8, FRAME), shape(SEG, LOCAL, dtype=BF16), shape(SEG, 128), EXT_SHAPE, shape(8, 128, dtype=I32), shape(ROWS, COLS)),
         (
             head0,
             seg_block.reshape(8, 128),
@@ -549,6 +550,7 @@
             sec0.reshape(2, 128),
             net.reshape(2, 128),
             infl,
+            recharge,
         ),
         scratch=[
             SEG_ROWS,
@@ -562,18 +564,19 @@
             pltpu.VMEM((2, 128), I32),
             pltpu.SMEM((NETS,), F32),
             SMALL,
-            sems(17),
+            sems(18),
         ],
-        hbm=range(9),
+        hbm=range(10),
     )
     own, up, down = exchange_sums(part)
-    onehot, inv, supply = call(
-        fields,
-        (shape(TILES * ROWS, SEG, dtype=BF16), GRID, shape(TILES, ROWS, 128)),
-        (head, recharge, storage, index8, weight),
-        scratch=[pltpu.VMEM((ROWS, COLS), F32), pltpu.VMEM((ROWS, COLS), F32), sems(2)],
-        hbm=(1, 2),
-    )
+    onehot, store = call(
+        one_hot,
+        (shape(TILES * ROWS, SEG, dtype=BF16), shape(ROWS, COLS)),
+        (index8, storage),
+        scratch=[pltpu.SemaphoreType.DMA],
+        hbm=(1,),
+    )
+    inv, supply = call(fields, (GRID, shape(TILES, ROWS, 128)), (head, rech, store, weight, onehot))
     strip = shape(16, ROWS)
     pa, pb = call(functools.partial(columns, True), (strip, strip), (head, inv))
     mixed_shape = shape(SEG, 256, dtype=BF16)

time: 57.9 us -> 56.8 us (0.981)
  Pallas kernels: 28.3 us -> 27.1 us
    pallas_call x14 -> x15, Pallas kernels: 28.3 us -> 27.1 us  [call(): pl.pallas_call(kernel, out_shape=outs, in_specs=[at(k, hbm) for k in rang...]
  transfers between devices with their start and end apart: 14 -> 14, of which waited for: 6 -> 6; matrix products, arithmetic and copies ran while one was open for 0% -> 0% of each run, Pallas kernels for 30% -> 28%
where the time goes in v4:
time: 56.8 us; the launch traced here: 56.7 us
  Pallas kernels  27.1 us (48%)
  starting transfers between devices  19.3 us (34%)
  waiting for transfers between devices  9.22 us (16%)
  between operations  0.97 us (2%)
    pallas_call x15, Pallas kernels, call(): pl.pallas_call(kernel, out_shape=outs, in_specs=[at(k, hbm) for k in rang...  27.1 us
    ppermute x6, starting transfers between devices, swap(): lax.ppermute(x, axis, [(k, k ^ 1) for k in range(lax.axis_size(axis))])  10.1 us
    ppermute x4, starting transfers between devices, shift(): return lax.ppermute(x, axis, [(k, (k + by) % n) for k in range(n)])  5.99 us
    ppermute x4, waiting for transfers between devices, shift(): return lax.ppermute(x, axis, [(k, (k + by) % n) for k in range(n)])  3.65 us
    ppermute x4, waiting for transfers between devices, far_swap(): return lax.ppermute(x, ('row', 'col'), pairs)  3.51 us
    ppermute x4, starting transfers between devices, far_swap(): return lax.ppermute(x, ('row', 'col'), pairs)  3.19 us
    ppermute x6, waiting for transfers between devices, swap(): lax.ppermute(x, axis, [(k, k ^ 1) for k in range(lax.axis_size(axis))])  2.06 us
  transfers between devices with their start and end apart: 14, of which 6 were waited for; matrix products, arithmetic and copies ran while one was open for 0% of the time, Pallas kernels for 28%

profile of v4, /device:TPU:1, one launch (start us, length us, event | category | flops | bytes accessed | tf_op | source)
XLA Modules:
  0.0 56.7 jit_solution(17210036362759120526)
XLA Ops:
  0.6 3.3 %shard_map.122 = (f32[8,1024]{1,0:T(8,128)S(1)}, bf16[1024,768]{1,0:T(8,128)(2,1)S(1)}, f32[1024,128]{1,0:T(8,128)S(1)}, f32[3600,128]{1,0:T(8,128)S(1)}, s32[8,128]{1,0:T(8,128)S(1)}, /*index=5*/f32[384,1024]{1,0:T(8,128)S(1)}) custom-call(f32[384,1024]{1,0:T(8,128)} %head.1, s32[8,128]{1,0:T(8,128)} %bitcast.6, s32[8,128]{1,0:T(8,128)} %bitcast.7, ...), custom_call_target="tpu_custom_call" | custom-call | flops 10000000 | bytes 4000000 | tf_op jit(solution)/shard_map/pallas_call | solution.py:471
  4.0 3.3 %collective-permute-start = (f32[8,1024]{1,0:T(8,128)S(1)}, f32[8,1024]{1,0:T(8,128)S(1)}, u32[]{:S(2)}, u32[]{:S(2)}) collective-permute-start(f32[8,1024]{1,0:T(8,128)S(1)} %get-tuple-element.42), channel_id=1, source_target_pairs={{0,1},{1,0},{2,3},{3,2},{4,5},{5,4},{6,7},{7,6},{8,9},{9,8},{10,11... | collective-permute-start | bytes 98312 | tf_op jit(solution)/shard_map/ppermute | solution.py:484
  8.1 3.9 %collective-permute-start.2 = (f32[8,512]{1,0:T(8,128)S(1)}, f32[8,512]{1,0:T(8,128)S(1)}, u32[]{:S(2)}, u32[]{:S(2)}) collective-permute-start(f32[8,512]{1,0:T(8,128)S(1)} %get-tuple-element.84), channel_id=1, source_target_pairs={{0,14},{1,15},{2,0},{3,1},{4,2},{5,3},{6,4},{7,5},{8,6},{9,7},{10,... | collective-permute-start | bytes 49160 | tf_op jit(solution)/shard_map/ppermute | solution.py:513
  12.1 1.9 %shard_map.123 = (bf16[3072,1024]{1,0:T(8,128)(2,1)S(1)}, f32[384,1024]{1,0:T(8,128)S(1)}) custom-call(s32[8,128]{1,0:T(8,128)S(1)} %get-tuple-element.44.index8, f32[384,1024]{1,0:T(8,128)} %storage.1), custom_call_target="tpu_custom_call" | custom-call | flops 10000000 | bytes 4000000 | tf_op jit(solution)/shard_map/pallas_call | solution.py:471
  14.0 2.0 %shard_map.124 = (f32[9,384,128]{2,1,0:T(8,128)S(1)}, f32[8,384,128]{2,1,0:T(8,128)S(1)}) custom-call(f32[3600,128]{1,0:T(8,128)S(1)} %get-tuple-element.47.headx.refs_0_.refs_2_, f32[384,1024]{1,0:T(8,128)S(1)} %get-tuple-element.48.rech_v, f32[384,1024]{1,0:T(8,128)S(1)} %get-tuple-element.49.store_v, ...), custom_call_target="tpu_custom_call" | custom-call | flops 10000000 | bytes 4000000 | tf_op jit(solution)/shard_map/pallas_call | solution.py:471
  16.2 1.8 %shard_map.126 = (f32[8,1024]{1,0:T(8,128)S(1)}, bf16[1024,256]{1,0:T(8,128)(2,1)S(1)}, f32[9,384,128]{2,1,0:T(8,128)S(1)}, f32[16,384]{1,0:T(8,128)S(1)}, f32[16,384]{1,0:T(8,128)S(1)}) custom-call(f32[8,1024]{1,0:T(8,128)S(1)} %add.6.refs_0_, f32[8,512]{1,0:T(8,128)S(1)} %collective-permute-done.1.refs_1_, f32[8,512]{1,0:T(8,128)S(1)} %collective-permute-done.2.refs_2_, ...), custom_call_target="tpu_custom_call" | custom-call | flops 10000000 | bytes 4000000 | tf_op jit(solution)/shard_map/pallas_call | solution.py:471
  18.1 1.5 %collective-permute-start.3 = (f32[16,384]{1,0:T(8,128)S(1)}, f32[16,384]{1,0:T(8,128)S(1)}, u32[]{:S(2)}, u32[]{:S(2)}) collective-permute-start(f32[16,384]{1,0:T(8,128)S(1)} %get-tuple-element.54), channel_id=1, source_target_pairs={{0,1},{1,0},{2,3},{3,2},{4,5},{5,4},{6,7},{7,6},{8,9},{9,8},{10,11... | collective-permute-start | bytes 73736 | tf_op jit(solution)/shard_map/ppermute | solution.py:484
  19.6 1.4 %shard_map.127.refs_3_ = f32[9,384,128]{2,1,0:T(8,128)S(1)} custom-call(bf16[3072,1024]{1,0:T(8,128)(2,1)S(1)} %get-tuple-element.45.onehot.refs_4_.refs_5_, bf16[1024,256]{1,0:T(8,128)(2,1)S(1)} %get-tuple-element.56.mixed, f32[8,384,128]{2,1,0:T(8,128)S(1)} %get-tuple-element.50.refs_6_.supply.refs_7_, ...), custom_call_target="tpu_custom_call", output_to_operand_aliasing={{}: (3, {})} | custom-call | flops 10000000 | bytes 4000000 | tf_op jit(solution)/shard_map/pallas_call | solution.py:471
  21.0 1.8 %collective-permute-done.4.refs_1_ = f32[16,384]{1,0:T(8,128)S(1)} collective-permute-done((f32[16,384]{1,0:T(8,128)S(1)}, f32[16,384]{1,0:T(8,128)S(1)}, u32[]{:S(2)}, u32[]{:S(2)}) %collective-permute-start.4) | collective-permute-done | bytes 24608 | tf_op jit(solution)/shard_map/ppermute | solution.py:502
  23.1 1.4 %collective-permute-start.5 = (f32[96,128]{1,0:T(8,128)S(1)}, f32[96,128]{1,0:T(8,128)S(1)}, u32[]{:S(2)}, u32[]{:S(2)}) collective-permute-start(f32[96,128]{1,0:T(8,128)S(1)} %get-tuple-element.58), channel_id=1, source_target_pairs={{0,16},{16,0},{32,48},{48,32},{64,80},{80,64},{96,112},{112,96},{1... | collective-permute-start | bytes 147464 | tf_op jit(solution)/shard_map/ppermute | solution.py:484
  24.5 1.6 %collective-permute-start.6 = (f32[96,128]{1,0:T(8,128)S(1)}, f32[96,128]{1,0:T(8,128)S(1)}, u32[]{:S(2)}, u32[]{:S(2)}) collective-permute-start(f32[96,128]{1,0:T(8,128)S(1)} %get-tuple-element.59), channel_id=1, source_target_pairs={{0,1},{1,0},{2,3},{3,2},{4,5},{5,4},{6,7},{7,6},{8,9},{9,8},{10,11... | collective-permute-start | bytes 147464 | tf_op jit(solution)/shard_map/ppermute | solution.py:502
  26.1 4.5 %shard_map.129.head_in = f32[3600,128]{1,0:T(8,128)S(1)} custom-call(f32[3600,128]{1,0:T(8,128)S(1)} %get-tuple-element.61.head_in, f32[9,384,128]{2,1,0:T(8,128)S(1)} %get-tuple-element.62.rhs, f32[9,384,128]{2,1,0:T(8,128)S(1)} %get-tuple-element.63.inv), custom_call_target="tpu_custom_call", output_to_operand_aliasing={{}: (0, {})} | custom-call | flops 10000000 | bytes 4000000 | tf_op jit(solution)/shard_map/pallas_call | solution.py:471
  30.5 2.0 %shard_map.130 = (f32[3600,128]{1,0:T(8,128)S(1)}, f32[2,9,8,128]{3,2,1,0:T(8,128)S(1)}, f32[8,1024]{1,0:T(8,128)S(1)}) custom-call(f32[96,128]{1,0:T(8,128)S(1)} %collective-permute-done.5.ra, f32[96,128]{1,0:T(8,128)S(1)} %collective-permute-done.6.rb, f32[2,9,8,128]{3,2,1,0:T(8,128)S(1)} %get-tuple-element.60.band, ...), custom_call_target="tpu_custom_call", output_to_operand_aliasing={{0}: (3, {})} | custom-call | flops 10000000 | bytes 4000000 | tf_op jit(solution)/shard_map/pallas_call | solution.py:471
  32.6 1.2 %collective-permute-done.7 = f32[8,1024]{1,0:T(8,128)S(1)} collective-permute-done((f32[8,1024]{1,0:T(8,128)S(1)}, f32[8,1024]{1,0:T(8,128)S(1)}, u32[]{:S(2)}, u32[]{:S(2)}) %collective-permute-start.7) | collective-permute-done | bytes 32800 | tf_op jit(solution)/shard_map/ppermute | solution.py:484
  33.8 2.0 %collective-permute-start.9 = (f32[8,512]{1,0:T(8,128)S(1)}, f32[8,512]{1,0:T(8,128)S(1)}, u32[]{:S(2)}, u32[]{:S(2)}) collective-permute-start(f32[8,512]{1,0:T(8,128)S(1)} %get-tuple-element.82), channel_id=1, source_target_pairs={{0,14},{1,15},{2,0},{3,1},{4,2},{5,3},{6,4},{7,5},{8,6},{9,7},{10,... | collective-permute-start | bytes 49160 | tf_op jit(solution)/shard_map/ppermute | solution.py:513
  36.7 2.9 %collective-permute-done.8.refs_1_ = f32[8,512]{1,0:T(8,128)S(1)} collective-permute-done((f32[8,512]{1,0:T(8,128)S(1)}, f32[8,512]{1,0:T(8,128)S(1)}, u32[]{:S(2)}, u32[]{:S(2)}) %collective-permute-start.8) | collective-permute-done | bytes 16416 | tf_op jit(solution)/shard_map/ppermute | solution.py:513
  39.7 1.8 %shard_map.132 = (f32[1,1024]{1,0:T(1,128)S(1)}, bf16[1024,256]{1,0:T(8,128)(2,1)S(1)}, f32[9,384,128]{2,1,0:T(8,128)S(1)}, f32[8,384]{1,0:T(8,128)S(1)}, f32[8,384]{1,0:T(8,128)S(1)}) custom-call(f32[8,1024]{1,0:T(8,128)S(1)} %add.7.refs_0_, f32[8,512]{1,0:T(8,128)S(1)} %collective-permute-done.8.refs_1_, f32[8,512]{1,0:T(8,128)S(1)} %collective-permute-done.9.refs_2_, ...), custom_call_target="tpu_custom_call" | custom-call | flops 10000000 | bytes 4000000 | tf_op jit(solution)/shard_map/pallas_call | solution.py:471
  41.5 1.9 %collective-permute-start.10 = (f32[8,384]{1,0:T(8,128)S(1)}, f32[8,384]{1,0:T(8,128)S(1)}, u32[]{:S(2)}, u32[]{:S(2)}) collective-permute-start(f32[8,384]{1,0:T(8,128)S(1)} %get-tuple-element.69), channel_id=1, source_target_pairs={{0,1},{1,0},{2,3},{3,2},{4,5},{5,4},{6,7},{7,6},{8,9},{9,8},{10,11... | collective-permute-start | bytes 36872 | tf_op jit(solution)/shard_map/ppermute | solution.py:484
  43.4 1.4 %shard_map.133.refs_3_ = f32[9,384,128]{2,1,0:T(8,128)S(1)} custom-call(bf16[3072,1024]{1,0:T(8,128)(2,1)S(1)} %get-tuple-element.45.onehot.refs_4_.refs_5_, bf16[1024,256]{1,0:T(8,128)(2,1)S(1)} %get-tuple-element.71.mixed, f32[8,384,128]{2,1,0:T(8,128)S(1)} %get-tuple-element.50.refs_6_.supply.refs_7_, ...), custom_call_target="tpu_custom_call", output_to_operand_aliasing={{}: (3, {})} | custom-call | flops 10000000 | bytes 4000000 | tf_op jit(solution)/shard_map/pallas_call | solution.py:471
  44.8 1.7 %collective-permute-done.11.refs_1_ = f32[8,384]{1,0:T(8,128)S(1)} collective-permute-done((f32[8,384]{1,0:T(8,128)S(1)}, f32[8,384]{1,0:T(8,128)S(1)}, u32[]{:S(2)}, u32[]{:S(2)}) %collective-permute-start.11) | collective-permute-done | bytes 12320 | tf_op jit(solution)/shard_map/ppermute | solution.py:502
  46.7 2.0 %collective-permute-start.12 = (f32[64,128]{1,0:T(8,128)S(1)}, f32[64,128]{1,0:T(8,128)S(1)}, u32[]{:S(2)}, u32[]{:S(2)}) collective-permute-start(f32[64,128]{1,0:T(8,128)S(1)} %get-tuple-element.73), channel_id=1, source_target_pairs={{0,16},{16,0},{32,48},{48,32},{64,80},{80,64},{96,112},{112,96},{1... | collective-permute-start | bytes 98312 | tf_op jit(solution)/shard_map/ppermute | solution.py:484
  48.7 1.6 %collective-permute-start.13 = (f32[64,128]{1,0:T(8,128)S(1)}, f32[64,128]{1,0:T(8,128)S(1)}, u32[]{:S(2)}, u32[]{:S(2)}) collective-permute-start(f32[64,128]{1,0:T(8,128)S(1)} %get-tuple-element.74), channel_id=1, source_target_pairs={{0,1},{1,0},{2,3},{3,2},{4,5},{5,4},{6,7},{7,6},{8,9},{9,8},{10,11... | collective-permute-start | bytes 98312 | tf_op jit(solution)/shard_map/ppermute | solution.py:502
  50.3 4.6 %shard_map.135.head = f32[3600,128]{1,0:T(8,128)S(1)} custom-call(f32[3600,128]{1,0:T(8,128)S(1)} %get-tuple-element.76.head_in, f32[9,384,128]{2,1,0:T(8,128)S(1)} %get-tuple-element.77.rhs, f32[9,384,128]{2,1,0:T(8,128)S(1)} %get-tuple-element.63.inv), custom_call_target="tpu_custom_call", output_to_operand_aliasing={{}: (0, {})} | custom-call | flops 10000000 | bytes 4000000 | tf_op jit(solution)/shard_map/pallas_call | solution.py:471
  54.9 1.6 %shard_map.136 = (f32[384,1024]{1,0:T(8,128)}, f32[2,128]{1,0:T(2,128)}) custom-call(f32[64,128]{1,0:T(8,128)S(1)} %collective-permute-done.12.ra, f32[64,128]{1,0:T(8,128)S(1)} %collective-permute-done.13.rb, f32[2,9,8,128]{3,2,1,0:T(8,128)S(1)} %get-tuple-element.75.band, f32[3600,128]{1,0:T(8,128)S(1)} %shard_map.135.head, ...), custom_call_target="tpu_custom_call" | custom-call | flops 10000000 | bytes 4000000 | tf_op jit(solution)/shard_map/pallas_call | solution.py:471
  (23 shorter events, 2.6 us)
Async XLA Ops:
  4.0 4.1 %collective-permute-start = (f32[8,1024]{1,0:T(8,128)S(1)}, f32[8,1024]{1,0:T(8,128)S(1)}, u32[]{:S(2)}, u32[]{:S(2)}) collective-permute-start(f32[8,1024]{1,0:T(8,128)S(1)} %get-tuple-element.42), channel_id=1, source_target_pairs={{0,1},{1,0},{2,3},{3,2},{4,5},{5,4},{6,7},{7,6},{8,9},{9,8},{10,11... | collective-permute-start | bytes 98312 | tf_op jit(solution)/shard_map/ppermute | solution.py:484
  8.1 8.1 %collective-permute-start.2 = (f32[8,512]{1,0:T(8,128)S(1)}, f32[8,512]{1,0:T(8,128)S(1)}, u32[]{:S(2)}, u32[]{:S(2)}) collective-permute-start(f32[8,512]{1,0:T(8,128)S(1)} %get-tuple-element.84), channel_id=1, source_target_pairs={{0,14},{1,15},{2,0},{3,1},{4,2},{5,3},{6,4},{7,5},{8,6},{9,7},{10,... | collective-permute-start | bytes 49160 | tf_op jit(solution)/shard_map/ppermute | solution.py:513
  12.1 4.2 %collective-permute-start.1 = (f32[8,512]{1,0:T(8,128)S(1)}, f32[8,512]{1,0:T(8,128)S(1)}, u32[]{:S(2)}, u32[]{:S(2)}) collective-permute-start(f32[8,512]{1,0:T(8,128)S(1)} %get-tuple-element.85), channel_id=1, source_target_pairs={{0,2},{1,3},{2,4},{3,5},{4,6},{5,7},{6,8},{7,9},{8,10},{9,11},{10,... | collective-permute-start | bytes 49160 | tf_op jit(solution)/shard_map/ppermute | solution.py:513
  18.1 2.9 %collective-permute-start.3 = (f32[16,384]{1,0:T(8,128)S(1)}, f32[16,384]{1,0:T(8,128)S(1)}, u32[]{:S(2)}, u32[]{:S(2)}) collective-permute-start(f32[16,384]{1,0:T(8,128)S(1)} %get-tuple-element.54), channel_id=1, source_target_pairs={{0,1},{1,0},{2,3},{3,2},{4,5},{5,4},{6,7},{7,6},{8,9},{9,8},{10,11... | collective-permute-start | bytes 73736 | tf_op jit(solution)/shard_map/ppermute | solution.py:484
  19.6 3.3 %collective-permute-start.4 = (f32[16,384]{1,0:T(8,128)S(1)}, f32[16,384]{1,0:T(8,128)S(1)}, u32[]{:S(2)}, u32[]{:S(2)}) collective-permute-start(f32[16,384]{1,0:T(8,128)S(1)} %get-tuple-element.55), channel_id=1, source_target_pairs={{0,15},{1,2},{2,1},{3,4},{4,3},{5,6},{6,5},{7,8},{8,7},{9,10},{10,... | collective-permute-start | bytes 73736 | tf_op jit(solution)/shard_map/ppermute | solution.py:502
  23.1 7.4 %collective-permute-start.5 = (f32[96,128]{1,0:T(8,128)S(1)}, f32[96,128]{1,0:T(8,128)S(1)}, u32[]{:S(2)}, u32[]{:S(2)}) collective-permute-start(f32[96,128]{1,0:T(8,128)S(1)} %get-tuple-element.58), channel_id=1, source_target_pairs={{0,16},{16,0},{32,48},{48,32},{64,80},{80,64},{96,112},{112,96},{1... | collective-permute-start | bytes 147464 | tf_op jit(solution)/shard_map/ppermute | solution.py:484
  24.5 6.1 %collective-permute-start.6 = (f32[96,128]{1,0:T(8,128)S(1)}, f32[96,128]{1,0:T(8,128)S(1)}, u32[]{:S(2)}, u32[]{:S(2)}) collective-permute-start(f32[96,128]{1,0:T(8,128)S(1)} %get-tuple-element.59), channel_id=1, source_target_pairs={{0,1},{1,0},{2,3},{3,2},{4,5},{5,4},{6,7},{7,6},{8,9},{9,8},{10,11... | collective-permute-start | bytes 147464 | tf_op jit(solution)/shard_map/ppermute | solution.py:502
  32.5 1.3 %collective-permute-start.7 = (f32[8,1024]{1,0:T(8,128)S(1)}, f32[8,1024]{1,0:T(8,128)S(1)}, u32[]{:S(2)}, u32[]{:S(2)}) collective-permute-start(f32[8,1024]{1,0:T(8,128)S(1)} %get-tuple-element.64), channel_id=1, source_target_pairs={{0,1},{1,0},{2,3},{3,2},{4,5},{5,4},{6,7},{7,6},{8,9},{9,8},{10,11... | collective-permute-start | bytes 98312 | tf_op jit(solution)/shard_map/ppermute | solution.py:484
  33.8 2.9 %collective-permute-start.9 = (f32[8,512]{1,0:T(8,128)S(1)}, f32[8,512]{1,0:T(8,128)S(1)}, u32[]{:S(2)}, u32[]{:S(2)}) collective-permute-start(f32[8,512]{1,0:T(8,128)S(1)} %get-tuple-element.82), channel_id=1, source_target_pairs={{0,14},{1,15},{2,0},{3,1},{4,2},{5,3},{6,4},{7,5},{8,6},{9,7},{10,... | collective-permute-start | bytes 49160 | tf_op jit(solution)/shard_map/ppermute | solution.py:513
  35.9 3.8 %collective-permute-start.8 = (f32[8,512]{1,0:T(8,128)S(1)}, f32[8,512]{1,0:T(8,128)S(1)}, u32[]{:S(2)}, u32[]{:S(2)}) collective-permute-start(f32[8,512]{1,0:T(8,128)S(1)} %get-tuple-element.83), channel_id=1, source_target_pairs={{0,2},{1,3},{2,4},{3,5},{4,6},{5,7},{6,8},{7,9},{8,10},{9,11},{10,... | collective-permute-start | bytes 49160 | tf_op jit(solution)/shard_map/ppermute | solution.py:513
  41.5 3.3 %collective-permute-start.10 = (f32[8,384]{1,0:T(8,128)S(1)}, f32[8,384]{1,0:T(8,128)S(1)}, u32[]{:S(2)}, u32[]{:S(2)}) collective-permute-start(f32[8,384]{1,0:T(8,128)S(1)} %get-tuple-element.69), channel_id=1, source_target_pairs={{0,1},{1,0},{2,3},{3,2},{4,5},{5,4},{6,7},{7,6},{8,9},{9,8},{10,11... | collective-permute-start | bytes 36872 | tf_op jit(solution)/shard_map/ppermute | solution.py:484
  43.4 3.1 %collective-permute-start.11 = (f32[8,384]{1,0:T(8,128)S(1)}, f32[8,384]{1,0:T(8,128)S(1)}, u32[]{:S(2)}, u32[]{:S(2)}) collective-permute-start(f32[8,384]{1,0:T(8,128)S(1)} %get-tuple-element.70), channel_id=1, source_target_pairs={{0,15},{1,2},{2,1},{3,4},{4,3},{5,6},{6,5},{7,8},{8,7},{9,10},{10,... | collective-permute-start | bytes 36872 | tf_op jit(solution)/shard_map/ppermute | solution.py:502
  46.7 8.2 %collective-permute-start.12 = (f32[64,128]{1,0:T(8,128)S(1)}, f32[64,128]{1,0:T(8,128)S(1)}, u32[]{:S(2)}, u32[]{:S(2)}) collective-permute-start(f32[64,128]{1,0:T(8,128)S(1)} %get-tuple-element.73), channel_id=1, source_target_pairs={{0,16},{16,0},{32,48},{48,32},{64,80},{80,64},{96,112},{112,96},{1... | collective-permute-start | bytes 98312 | tf_op jit(solution)/shard_map/ppermute | solution.py:484
  48.7 6.2 %collective-permute-start.13 = (f32[64,128]{1,0:T(8,128)S(1)}, f32[64,128]{1,0:T(8,128)S(1)}, u32[]{:S(2)}, u32[]{:S(2)}) collective-permute-start(f32[64,128]{1,0:T(8,128)S(1)} %get-tuple-element.74), channel_id=1, source_target_pairs={{0,1},{1,0},{2,3},{3,2},{4,5},{5,4},{6,7},{7,6},{8,9},{9,8},{10,11... | collective-permute-start | bytes 98312 | tf_op jit(solution)/shard_map/ppermute | solution.py:502

commit v5 on v4

--- a/solution.py
+++ b/solution.py
@@ -20,7 +20,7 @@
 EXT = ROWS + 2 * OFF
 H = 4
 DEPTH = (4, 3, 3)
-UNROLL = 24
+UNROLL = 48
 F32 = jnp.float32
 BF16 = jnp.bfloat16
 I32 = jnp.int32
@@ -153,9 +153,7 @@
     later.wait()
 
 
-def one_hot(index8, storage, onehot, store_v, sem):
-    move = pltpu.make_async_copy(storage, store_v, sem)
-    move.start()
+def one_hot(index8, onehot):
     target = index8[...]
     iota = lax.broadcasted_iota(I32, (ROWS, 128), 0)
     for k in range(SEG // 128):
@@ -164,7 +162,6 @@
             onehot[c * ROWS : (c + 1) * ROWS, k * 128 : (k + 1) * 128] = jnp.where(
                 row == iota + (c * EXT + OFF), 1.0, 0.0
             ).astype(BF16)
-    move.wait()
 
 
 def fields(headx, rech_v, store_v, weight, onehot, inv, supply):
@@ -569,14 +566,10 @@
         hbm=range(10),
     )
     own, up, down = exchange_sums(part)
-    onehot, store = call(
-        one_hot,
-        (shape(TILES * ROWS, SEG, dtype=BF16), shape(ROWS, COLS)),
-        (index8, storage),
-        scratch=[pltpu.SemaphoreType.DMA],
-        hbm=(1,),
-    )
-    inv, supply = call(fields, (GRID, shape(TILES, ROWS, 128)), (head, rech, store, weight, onehot))
+    (onehot,) = call(one_hot, (shape(TILES * ROWS, SEG, dtype=BF16),), (index8,))
+    inv, supply = call(
+        fields, (GRID, shape(TILES, ROWS, 128)), (head, rech, storage, weight, onehot)
+    )
     strip = shape(16, ROWS)
     pa, pb = call(functools.partial(columns, True), (strip, strip), (head, inv))
     mixed_shape = shape(SEG, 256, dtype=BF16)
@@ -599,7 +592,7 @@
     (head,) = call(inner_relax, (EXT_SHAPE,), (head, rhs, inv), scratch=[OTHER], aliases={0: 0})
     head, rim, part = call(
         finish_first,
-        (EXT_SHAPE, BAND, shape(8, FRAME)),
+        (EXT_SHAPE, BAND, shape(1, FRAME)),
         (ra, rb, band, head, rhs, inv, index8, weight, oh),
         scratch=[WORK, WORK, SEG_ROWS, SUMS, SPARE, SMALL, pltpu.SemaphoreType.DMA],
         aliases={3: 0},

time: 56.8 us -> 56.2 us (0.989)
  the two profiles are of different devices: /device:TPU:1 before, /device:TPU:6 now
where the time goes in v5:
time: 56.2 us; the launch traced here: 56 us
  Pallas kernels  26.1 us (46%)
  starting transfers between devices  17.3 us (31%)
  waiting for transfers between devices  11.6 us (21%)
  between operations  1.01 us (2%)
    pallas_call x15, Pallas kernels, call(): pl.pallas_call(kernel, out_shape=outs, in_specs=[at(k, hbm) for k in rang...  26.1 us
    ppermute x4, starting transfers between devices, shift(): return lax.ppermute(x, axis, [(k, (k + by) % n) for k in range(n)])  8.04 us
    ppermute x4, starting transfers between devices, far_swap(): return lax.ppermute(x, ('row', 'col'), pairs)  6.7 us
    ppermute x4, waiting for transfers between devices, shift(): return lax.ppermute(x, axis, [(k, (k + by) % n) for k in range(n)])  5.37 us
    ppermute x4, waiting for transfers between devices, far_swap(): return lax.ppermute(x, ('row', 'col'), pairs)  3.83 us
    ppermute x6, starting transfers between devices, swap(): lax.ppermute(x, axis, [(k, k ^ 1) for k in range(lax.axis_size(axis))])  2.54 us
    ppermute x6, waiting for transfers between devices, swap(): lax.ppermute(x, axis, [(k, k ^ 1) for k in range(lax.axis_size(axis))])  2.36 us
  transfers between devices with their start and end apart: 14, of which 8 were waited for; matrix products, arithmetic and copies ran while one was open for 0% of the time, Pallas kernels for 27%

profile of v5, /device:TPU:6, one launch (start us, length us, event | category | flops | bytes accessed | tf_op | source)
XLA Modules:
  0.0 56.0 jit_solution(14987997552218469837)
XLA Ops:
  0.6 3.3 %shard_map.122 = (f32[8,1024]{1,0:T(8,128)S(1)}, bf16[1024,768]{1,0:T(8,128)(2,1)S(1)}, f32[1024,128]{1,0:T(8,128)S(1)}, f32[3600,128]{1,0:T(8,128)S(1)}, s32[8,128]{1,0:T(8,128)S(1)}, /*index=5*/f32[384,1024]{1,0:T(8,128)S(1)}) custom-call(f32[384,1024]{1,0:T(8,128)} %head.1, s32[8,128]{1,0:T(8,128)} %bitcast.6, s32[8,128]{1,0:T(8,128)} %bitcast.7, ...), custom_call_target="tpu_custom_call" | custom-call | flops 10000000 | bytes 4000000 | tf_op jit(solution)/shard_map/pallas_call | solution.py:468
  4.1 1.2 %collective-permute-done = f32[8,1024]{1,0:T(8,128)S(1)} collective-permute-done((f32[8,1024]{1,0:T(8,128)S(1)}, f32[8,1024]{1,0:T(8,128)S(1)}, u32[]{:S(2)}, u32[]{:S(2)}) %collective-permute-start) | collective-permute-done | bytes 32800 | tf_op jit(solution)/shard_map/ppermute | solution.py:481
  5.3 5.9 %collective-permute-start.2 = (f32[8,512]{1,0:T(8,128)S(1)}, f32[8,512]{1,0:T(8,128)S(1)}, u32[]{:S(2)}, u32[]{:S(2)}) collective-permute-start(f32[8,512]{1,0:T(8,128)S(1)} %get-tuple-element.78), channel_id=1, source_target_pairs={{0,14},{1,15},{2,0},{3,1},{4,2},{5,3},{6,4},{7,5},{8,6},{9,7},{10,... | collective-permute-start | bytes 49160 | tf_op jit(solution)/shard_map/ppermute | solution.py:510
  11.2 1.9 %shard_map.123.onehot.refs_4_.refs_5_ = bf16[3072,1024]{1,0:T(8,128)(2,1)S(1)} custom-call(s32[8,128]{1,0:T(8,128)S(1)} %get-tuple-element.42.index8), custom_call_target="tpu_custom_call" | custom-call | flops 10000000 | bytes 4000000 | tf_op jit(solution)/shard_map/pallas_call | solution.py:468
  13.1 2.0 %shard_map.124 = (f32[9,384,128]{2,1,0:T(8,128)S(1)}, f32[8,384,128]{2,1,0:T(8,128)S(1)}) custom-call(f32[3600,128]{1,0:T(8,128)S(1)} %get-tuple-element.44.headx.refs_0_.refs_2_, f32[384,1024]{1,0:T(8,128)S(1)} %get-tuple-element.45.rech_v, f32[384,1024]{1,0:T(8,128)S(1)} %copy-done, f32[1024,128]{1,0:T(8,128)S(1)} %get-tuple-element.43.weight.refs_5_.refs_6_, ...), custom_call_target="tpu_custom_call" | custom-call | flops 10000000 | bytes 4000000 | tf_op jit(solution)/shard_map/pallas_call | solution.py:468
  15.4 0.8 %collective-permute-done.1.refs_1_ = f32[8,512]{1,0:T(8,128)S(1)} collective-permute-done((f32[8,512]{1,0:T(8,128)S(1)}, f32[8,512]{1,0:T(8,128)S(1)}, u32[]{:S(2)}, u32[]{:S(2)}) %collective-permute-start.1) | collective-permute-done | bytes 16416 | tf_op jit(solution)/shard_map/ppermute | solution.py:510
  16.2 1.8 %shard_map.126 = (f32[8,1024]{1,0:T(8,128)S(1)}, bf16[1024,256]{1,0:T(8,128)(2,1)S(1)}, f32[9,384,128]{2,1,0:T(8,128)S(1)}, f32[16,384]{1,0:T(8,128)S(1)}, f32[16,384]{1,0:T(8,128)S(1)}) custom-call(f32[8,1024]{1,0:T(8,128)S(1)} %add.6.refs_0_, f32[8,512]{1,0:T(8,128)S(1)} %collective-permute-done.1.refs_1_, f32[8,512]{1,0:T(8,128)S(1)} %collective-permute-done.2.refs_2_, ...), custom_call_target="tpu_custom_call" | custom-call | flops 10000000 | bytes 4000000 | tf_op jit(solution)/shard_map/pallas_call | solution.py:468
  18.1 2.6 %collective-permute-start.4 = (f32[16,384]{1,0:T(8,128)S(1)}, f32[16,384]{1,0:T(8,128)S(1)}, u32[]{:S(2)}, u32[]{:S(2)}) collective-permute-start(f32[16,384]{1,0:T(8,128)S(1)} %get-tuple-element.51), channel_id=1, source_target_pairs={{0,15},{1,2},{2,1},{3,4},{4,3},{5,6},{6,5},{7,8},{8,7},{9,10},{10,... | collective-permute-start | bytes 73736 | tf_op jit(solution)/shard_map/ppermute | solution.py:499
  20.6 1.4 %shard_map.127.refs_3_ = f32[9,384,128]{2,1,0:T(8,128)S(1)} custom-call(bf16[3072,1024]{1,0:T(8,128)(2,1)S(1)} %shard_map.123.onehot.refs_4_.refs_5_, bf16[1024,256]{1,0:T(8,128)(2,1)S(1)} %get-tuple-element.52.mixed, f32[8,384,128]{2,1,0:T(8,128)S(1)} %get-tuple-element.46.refs_6_.supply.refs_7_, ...), custom_call_target="tpu_custom_call", output_to_operand_aliasing={{}: (3, {})} | custom-call | flops 10000000 | bytes 4000000 | tf_op jit(solution)/shard_map/pallas_call | solution.py:468
  22.1 0.6 %collective-permute-done.4.refs_1_ = f32[16,384]{1,0:T(8,128)S(1)} collective-permute-done((f32[16,384]{1,0:T(8,128)S(1)}, f32[16,384]{1,0:T(8,128)S(1)}, u32[]{:S(2)}, u32[]{:S(2)}) %collective-permute-start.4) | collective-permute-done | bytes 24608 | tf_op jit(solution)/shard_map/ppermute | solution.py:499
  22.9 1.7 %collective-permute-start.5 = (f32[96,128]{1,0:T(8,128)S(1)}, f32[96,128]{1,0:T(8,128)S(1)}, u32[]{:S(2)}, u32[]{:S(2)}) collective-permute-start(f32[96,128]{1,0:T(8,128)S(1)} %get-tuple-element.54), channel_id=1, source_target_pairs={{0,16},{16,0},{32,48},{48,32},{64,80},{80,64},{96,112},{112,96},{1... | collective-permute-start | bytes 147464 | tf_op jit(solution)/shard_map/ppermute | solution.py:481
  24.6 2.4 %collective-permute-start.6 = (f32[96,128]{1,0:T(8,128)S(1)}, f32[96,128]{1,0:T(8,128)S(1)}, u32[]{:S(2)}, u32[]{:S(2)}) collective-permute-start(f32[96,128]{1,0:T(8,128)S(1)} %get-tuple-element.55), channel_id=1, source_target_pairs={{0,1},{1,0},{2,3},{3,2},{4,5},{5,4},{6,7},{7,6},{8,9},{9,8},{10,11... | collective-permute-start | bytes 147464 | tf_op jit(solution)/shard_map/ppermute | solution.py:499
  27.0 4.0 %shard_map.129.head_in = f32[3600,128]{1,0:T(8,128)S(1)} custom-call(f32[3600,128]{1,0:T(8,128)S(1)} %get-tuple-element.57.head_in, f32[9,384,128]{2,1,0:T(8,128)S(1)} %get-tuple-element.58.rhs, f32[9,384,128]{2,1,0:T(8,128)S(1)} %get-tuple-element.59.inv), custom_call_target="tpu_custom_call", output_to_operand_aliasing={{}: (0, {})} | custom-call | flops 10000000 | bytes 4000000 | tf_op jit(solution)/shard_map/pallas_call | solution.py:468
  31.1 2.0 %shard_map.130 = (f32[3600,128]{1,0:T(8,128)S(1)}, f32[2,9,8,128]{3,2,1,0:T(8,128)S(1)}, f32[1,1024]{1,0:T(1,128)S(1)}) custom-call(f32[96,128]{1,0:T(8,128)S(1)} %collective-permute-done.5.ra, f32[96,128]{1,0:T(8,128)S(1)} %collective-permute-done.6.rb, f32[2,9,8,128]{3,2,1,0:T(8,128)S(1)} %get-tuple-element.56.band, ...), custom_call_target="tpu_custom_call", output_to_operand_aliasing={{0}: (3, {})} | custom-call | flops 10000000 | bytes 4000000 | tf_op jit(solution)/shard_map/pallas_call | solution.py:468
  33.2 1.2 %collective-permute-done.7 = f32[1,1024]{1,0:T(1,128)S(1)} collective-permute-done((f32[1,1024]{1,0:T(1,128)S(1)}, f32[1,1024]{1,0:T(1,128)S(1)}, u32[]{:S(2)}, u32[]{:S(2)}) %collective-permute-start.7) | collective-permute-done | bytes 4128 | tf_op jit(solution)/shard_map/ppermute | solution.py:481
  34.3 2.0 %collective-permute-start.9 = (f32[1,512]{1,0:T(1,128)S(1)}, f32[1,512]{1,0:T(1,128)S(1)}, u32[]{:S(2)}, u32[]{:S(2)}) collective-permute-start(f32[1,512]{1,0:T(1,128)S(1)} %get-tuple-element.80), channel_id=1, source_target_pairs={{0,14},{1,15},{2,0},{3,1},{4,2},{5,3},{6,4},{7,5},{8,6},{9,7},{10,... | collective-permute-start | bytes 6152 | tf_op jit(solution)/shard_map/ppermute | solution.py:510
  36.6 1.4 %collective-permute-done.9.refs_2_ = f32[1,512]{1,0:T(1,128)S(1)} collective-permute-done((f32[1,512]{1,0:T(1,128)S(1)}, f32[1,512]{1,0:T(1,128)S(1)}, u32[]{:S(2)}, u32[]{:S(2)}) %collective-permute-start.9) | collective-permute-done | bytes 2080 | tf_op jit(solution)/shard_map/ppermute | solution.py:510
  38.0 3.2 %collective-permute-done.8.refs_1_ = f32[1,512]{1,0:T(1,128)S(1)} collective-permute-done((f32[1,512]{1,0:T(1,128)S(1)}, f32[1,512]{1,0:T(1,128)S(1)}, u32[]{:S(2)}, u32[]{:S(2)}) %collective-permute-start.8) | collective-permute-done | bytes 2080 | tf_op jit(solution)/shard_map/ppermute | solution.py:510
  41.1 1.8 %shard_map.132 = (f32[1,1024]{1,0:T(1,128)S(1)}, bf16[1024,256]{1,0:T(8,128)(2,1)S(1)}, f32[9,384,128]{2,1,0:T(8,128)S(1)}, f32[8,384]{1,0:T(8,128)S(1)}, f32[8,384]{1,0:T(8,128)S(1)}) custom-call(f32[1,1024]{1,0:T(1,128)S(1)} %add.7.refs_0_, f32[1,512]{1,0:T(1,128)S(1)} %collective-permute-done.8.refs_1_, f32[1,512]{1,0:T(1,128)S(1)} %collective-permute-done.9.refs_2_, ...), custom_call_target="tpu_custom_call" | custom-call | flops 10000000 | bytes 4000000 | tf_op jit(solution)/shard_map/pallas_call | solution.py:468
  43.2 1.4 %shard_map.133.refs_3_ = f32[9,384,128]{2,1,0:T(8,128)S(1)} custom-call(bf16[3072,1024]{1,0:T(8,128)(2,1)S(1)} %shard_map.123.onehot.refs_4_.refs_5_, bf16[1024,256]{1,0:T(8,128)(2,1)S(1)} %get-tuple-element.67.mixed, f32[8,384,128]{2,1,0:T(8,128)S(1)} %get-tuple-element.46.refs_6_.supply.refs_7_, ...), custom_call_target="tpu_custom_call", output_to_operand_aliasing={{}: (3, {})} | custom-call | flops 10000000 | bytes 4000000 | tf_op jit(solution)/shard_map/pallas_call | solution.py:468
  44.6 2.9 %collective-permute-done.11.refs_1_ = f32[8,384]{1,0:T(8,128)S(1)} collective-permute-done((f32[8,384]{1,0:T(8,128)S(1)}, f32[8,384]{1,0:T(8,128)S(1)}, u32[]{:S(2)}, u32[]{:S(2)}) %collective-permute-start.11) | collective-permute-done | bytes 12320 | tf_op jit(solution)/shard_map/ppermute | solution.py:499
  48.2 1.6 %collective-permute-start.13 = (f32[64,128]{1,0:T(8,128)S(1)}, f32[64,128]{1,0:T(8,128)S(1)}, u32[]{:S(2)}, u32[]{:S(2)}) collective-permute-start(f32[64,128]{1,0:T(8,128)S(1)} %get-tuple-element.70), channel_id=1, source_target_pairs={{0,1},{1,0},{2,3},{3,2},{4,5},{5,4},{6,7},{7,6},{8,9},{9,8},{10,11... | collective-permute-start | bytes 98312 | tf_op jit(solution)/shard_map/ppermute | solution.py:499
  49.8 4.0 %shard_map.135.head = f32[3600,128]{1,0:T(8,128)S(1)} custom-call(f32[3600,128]{1,0:T(8,128)S(1)} %get-tuple-element.72.head_in, f32[9,384,128]{2,1,0:T(8,128)S(1)} %get-tuple-element.73.rhs, f32[9,384,128]{2,1,0:T(8,128)S(1)} %get-tuple-element.59.inv), custom_call_target="tpu_custom_call", output_to_operand_aliasing={{}: (0, {})} | custom-call | flops 10000000 | bytes 4000000 | tf_op jit(solution)/shard_map/pallas_call | solution.py:468
  54.2 1.6 %shard_map.136 = (f32[384,1024]{1,0:T(8,128)}, f32[2,128]{1,0:T(2,128)}) custom-call(f32[64,128]{1,0:T(8,128)S(1)} %collective-permute-done.12.ra, f32[64,128]{1,0:T(8,128)S(1)} %collective-permute-done.13.rb, f32[2,9,8,128]{3,2,1,0:T(8,128)S(1)} %get-tuple-element.71.band, f32[3600,128]{1,0:T(8,128)S(1)} %shard_map.135.head, ...), custom_call_target="tpu_custom_call" | custom-call | flops 10000000 | bytes 4000000 | tf_op jit(solution)/shard_map/pallas_call | solution.py:468
  (25 shorter events, 2.3 us)
Async XLA Ops:
  4.0 1.3 %collective-permute-start = (f32[8,1024]{1,0:T(8,128)S(1)}, f32[8,1024]{1,0:T(8,128)S(1)}, u32[]{:S(2)}, u32[]{:S(2)}) collective-permute-start(f32[8,1024]{1,0:T(8,128)S(1)} %get-tuple-element.40), channel_id=1, source_target_pairs={{0,1},{1,0},{2,3},{3,2},{4,5},{5,4},{6,7},{7,6},{8,9},{9,8},{10,11... | collective-permute-start | bytes 98312 | tf_op jit(solution)/shard_map/ppermute | solution.py:481
  5.3 10.1 %collective-permute-start.2 = (f32[8,512]{1,0:T(8,128)S(1)}, f32[8,512]{1,0:T(8,128)S(1)}, u32[]{:S(2)}, u32[]{:S(2)}) collective-permute-start(f32[8,512]{1,0:T(8,128)S(1)} %get-tuple-element.78), channel_id=1, source_target_pairs={{0,14},{1,15},{2,0},{3,1},{4,2},{5,3},{6,4},{7,5},{8,6},{9,7},{10,... | collective-permute-start | bytes 49160 | tf_op jit(solution)/shard_map/ppermute | solution.py:510
  11.2 4.9 %collective-permute-start.1 = (f32[8,512]{1,0:T(8,128)S(1)}, f32[8,512]{1,0:T(8,128)S(1)}, u32[]{:S(2)}, u32[]{:S(2)}) collective-permute-start(f32[8,512]{1,0:T(8,128)S(1)} %get-tuple-element.79), channel_id=1, source_target_pairs={{0,2},{1,3},{2,4},{3,5},{4,6},{5,7},{6,8},{7,9},{8,10},{9,11},{10,... | collective-permute-start | bytes 49160 | tf_op jit(solution)/shard_map/ppermute | solution.py:510
  11.2 1.9 %copy-start = (f32[384,1024]{1,0:T(8,128)S(1)}, f32[384,1024]{1,0:T(8,128)}, u32[]{:S(2)}) copy-start(f32[384,1024]{1,0:T(8,128)} %store_v.1) | copy-start | bytes 4718596
  18.0 4.1 %collective-permute-start.3 = (f32[16,384]{1,0:T(8,128)S(1)}, f32[16,384]{1,0:T(8,128)S(1)}, u32[]{:S(2)}, u32[]{:S(2)}) collective-permute-start(f32[16,384]{1,0:T(8,128)S(1)} %get-tuple-element.50), channel_id=1, source_target_pairs={{0,1},{1,0},{2,3},{3,2},{4,5},{5,4},{6,7},{7,6},{8,9},{9,8},{10,11... | collective-permute-start | bytes 73736 | tf_op jit(solution)/shard_map/ppermute | solution.py:481
  18.1 4.5 %collective-permute-start.4 = (f32[16,384]{1,0:T(8,128)S(1)}, f32[16,384]{1,0:T(8,128)S(1)}, u32[]{:S(2)}, u32[]{:S(2)}) collective-permute-start(f32[16,384]{1,0:T(8,128)S(1)} %get-tuple-element.51), channel_id=1, source_target_pairs={{0,15},{1,2},{2,1},{3,4},{4,3},{5,6},{6,5},{7,8},{8,7},{9,10},{10,... | collective-permute-start | bytes 73736 | tf_op jit(solution)/shard_map/ppermute | solution.py:499
  22.9 8.2 %collective-permute-start.5 = (f32[96,128]{1,0:T(8,128)S(1)}, f32[96,128]{1,0:T(8,128)S(1)}, u32[]{:S(2)}, u32[]{:S(2)}) collective-permute-start(f32[96,128]{1,0:T(8,128)S(1)} %get-tuple-element.54), channel_id=1, source_target_pairs={{0,16},{16,0},{32,48},{48,32},{64,80},{80,64},{96,112},{112,96},{1... | collective-permute-start | bytes 147464 | tf_op jit(solution)/shard_map/ppermute | solution.py:481
  24.6 6.5 %collective-permute-start.6 = (f32[96,128]{1,0:T(8,128)S(1)}, f32[96,128]{1,0:T(8,128)S(1)}, u32[]{:S(2)}, u32[]{:S(2)}) collective-permute-start(f32[96,128]{1,0:T(8,128)S(1)} %get-tuple-element.55), channel_id=1, source_target_pairs={{0,1},{1,0},{2,3},{3,2},{4,5},{5,4},{6,7},{7,6},{8,9},{9,8},{10,11... | collective-permute-start | bytes 147464 | tf_op jit(solution)/shard_map/ppermute | solution.py:499
  33.1 1.3 %collective-permute-start.7 = (f32[1,1024]{1,0:T(1,128)S(1)}, f32[1,1024]{1,0:T(1,128)S(1)}, u32[]{:S(2)}, u32[]{:S(2)}) collective-permute-start(f32[1,1024]{1,0:T(1,128)S(1)} %get-tuple-element.60), channel_id=1, source_target_pairs={{0,1},{1,0},{2,3},{3,2},{4,5},{5,4},{6,7},{7,6},{8,9},{9,8},{10,11... | collective-permute-start | bytes 12296 | tf_op jit(solution)/shard_map/ppermute | solution.py:481
  34.3 3.7 %collective-permute-start.9 = (f32[1,512]{1,0:T(1,128)S(1)}, f32[1,512]{1,0:T(1,128)S(1)}, u32[]{:S(2)}, u32[]{:S(2)}) collective-permute-start(f32[1,512]{1,0:T(1,128)S(1)} %get-tuple-element.80), channel_id=1, source_target_pairs={{0,14},{1,15},{2,0},{3,1},{4,2},{5,3},{6,4},{7,5},{8,6},{9,7},{10,... | collective-permute-start | bytes 6152 | tf_op jit(solution)/shard_map/ppermute | solution.py:510
  36.4 4.8 %collective-permute-start.8 = (f32[1,512]{1,0:T(1,128)S(1)}, f32[1,512]{1,0:T(1,128)S(1)}, u32[]{:S(2)}, u32[]{:S(2)}) collective-permute-start(f32[1,512]{1,0:T(1,128)S(1)} %get-tuple-element.81), channel_id=1, source_target_pairs={{0,2},{1,3},{2,4},{3,5},{4,6},{5,7},{6,8},{7,9},{8,10},{9,11},{10,... | collective-permute-start | bytes 6152 | tf_op jit(solution)/shard_map/ppermute | solution.py:510
  43.0 1.6 %collective-permute-start.10 = (f32[8,384]{1,0:T(8,128)S(1)}, f32[8,384]{1,0:T(8,128)S(1)}, u32[]{:S(2)}, u32[]{:S(2)}) collective-permute-start(f32[8,384]{1,0:T(8,128)S(1)} %get-tuple-element.65), channel_id=1, source_target_pairs={{0,1},{1,0},{2,3},{3,2},{4,5},{5,4},{6,7},{7,6},{8,9},{9,8},{10,11... | collective-permute-start | bytes 36872 | tf_op jit(solution)/shard_map/ppermute | solution.py:481
  43.1 4.4 %collective-permute-start.11 = (f32[8,384]{1,0:T(8,128)S(1)}, f32[8,384]{1,0:T(8,128)S(1)}, u32[]{:S(2)}, u32[]{:S(2)}) collective-permute-start(f32[8,384]{1,0:T(8,128)S(1)} %get-tuple-element.66), channel_id=1, source_target_pairs={{0,15},{1,2},{2,1},{3,4},{4,3},{5,6},{6,5},{7,8},{8,7},{9,10},{10,... | collective-permute-start | bytes 36872 | tf_op jit(solution)/shard_map/ppermute | solution.py:499
  47.7 6.1 %collective-permute-start.12 = (f32[64,128]{1,0:T(8,128)S(1)}, f32[64,128]{1,0:T(8,128)S(1)}, u32[]{:S(2)}, u32[]{:S(2)}) collective-permute-start(f32[64,128]{1,0:T(8,128)S(1)} %get-tuple-element.69), channel_id=1, source_target_pairs={{0,16},{16,0},{32,48},{48,32},{64,80},{80,64},{96,112},{112,96},{1... | collective-permute-start | bytes 98312 | tf_op jit(solution)/shard_map/ppermute | solution.py:481
  48.2 6.0 %collective-permute-start.13 = (f32[64,128]{1,0:T(8,128)S(1)}, f32[64,128]{1,0:T(8,128)S(1)}, u32[]{:S(2)}, u32[]{:S(2)}) collective-permute-start(f32[64,128]{1,0:T(8,128)S(1)} %get-tuple-element.70), channel_id=1, source_target_pairs={{0,1},{1,0},{2,3},{3,2},{4,5},{5,4},{6,7},{7,6},{8,9},{9,8},{10,11... | collective-permute-start | bytes 98312 | tf_op jit(solution)/shard_map/ppermute | solution.py:499
